TPU v7x, 32 devices: a whole 2x2x4 slice. The times are simulated.
32 devices in a mesh: cfg: 2 (over x), seq: 16 (over z, y, core).
Axes of the slice: x: 2, y: 2, z: 4, core: 2. Of those that a mesh axis runs over, the one named last changes fastest.
Arguments:
- coarse_hidden: bfloat16 [2, 32, 64, 2048], P('cfg', 'seq'), may hold values from -6 to 6
- coarse_modulation: float32 [2, 2, 2048], P('cfg'), may hold values from -3 to 3
- final_weight: bfloat16 [2048, 32], replicated, may hold values from -0.125 to 0.125
- coarse_latent: float32 [32, 2048], P('seq'), may hold values from -6 to 6
- step_index: int32 [1], replicated, may hold values from 0 to 49
- guide_index: int32 [1], replicated, may hold values from 0 to 4095
- guide_scales: float32 [4096], replicated, may hold values from 1.5 to 6
- upsample_weight: float32 [288, 32], replicated, may hold values from -0.375 to 0.375
- upsample_bias: float32 [32], replicated, may hold values from -3 to 3
- embed_weight: bfloat16 [32, 2048], replicated, may hold values from -1 to 1
- embed_bias: float32 [2048], replicated, may hold values from -3 to 3
- fine_modulation: float32 [3, 2048], replicated, may hold values from -3 to 3
- project_weight: bfloat16 [2048, 3072], P(('cfg', 'seq')), may hold values from -0.125 to 0.125
- query_gain: float32 [128], replicated, may hold values from 0.25 to 1.75
- key_gain: float32 [128], replicated, may hold values from 0.25 to 1.75
- text_keys: bfloat16 [256, 1024], replicated, may hold values from -6 to 6
- text_values: bfloat16 [256, 1024], replicated, may hold values from -6 to 6
- text_length: int32 [1], replicated, may hold values from 192 to 256
- output_weight: bfloat16 [1024, 2048], P(None, ('cfg', 'seq')), may hold values from -0.1875 to 0.1875
Outputs:
- guided_velocity: float32 [32, 2048], P('seq')
- fine_latent: float32 [32, 2, 4096], P('seq', 'cfg')
- fine_hidden: bfloat16 [32, 2, 128, 2048], P('seq', 'cfg')
All inputs are finite; a program needn't handle non-finite values.
Results may differ from a plain program's by a relative error of at most 0.0053.
Values may be sent and summed in bfloat16 or wider, within the bound.
No kernel may reach another device: no remote copies, remote signals or barrier semaphores. Data moves between devices by JAX's collectives and lax.ppermute only.
A program may use at most 128 MiB of HBM per device.

v0:
```python
import jax
import jax.numpy as jnp
from jax import lax
from jax.sharding import PartitionSpec as P

HEADS = 8
STEPS = 50


epsilon = 1e-06
flow_shift = 5.0
highest = lax.Precision.HIGHEST


def from_partner(shard, axis, bit):
    return lax.ppermute(shard, axis, [(i, i ^ 1 << bit) for i in range(lax.axis_size(axis))])


def with_halo(block, sides, width):
    for axis, dim in sides:
        count = lax.axis_size(axis)
        forward = [(i, i + 1) for i in range(count - 1)]
        backward = [(target, source) for source, target in forward]
        low = lax.ppermute(
            lax.slice_in_dim(block, block.shape[dim] - width, None, axis=dim), axis, forward
        )
        high = lax.ppermute(lax.slice_in_dim(block, 0, width, axis=dim), axis, backward)
        block = jnp.concatenate([low, block, high], axis=dim)
    return block


def layer_norm(values):
    centred = values - jnp.mean(values, -1, keepdims=True)
    return centred * lax.rsqrt(jnp.mean(centred * centred, -1, keepdims=True) + epsilon)


def rms_heads(values, gain_vector, head_width):
    shaped = values.reshape(values.shape[0], -1, head_width)
    scaled = (
        shaped * lax.rsqrt(jnp.mean(shaped * shaped, -1, keepdims=True) + epsilon) * gain_vector
    )
    return scaled.reshape(values.shape[0], -1)


def sigma_at(step_value):
    fraction = 1.0 - step_value.astype(jnp.float32) / STEPS
    return flow_shift * fraction / (1.0 + (flow_shift - 1.0) * fraction)


def pick_scale(scale_table, slot_index):
    slots = jnp.arange(scale_table.shape[0], dtype=jnp.int32)
    return jnp.sum(jnp.where(slots == slot_index, scale_table, 0.0))


def attend(queries, image_keys, image_values, text_keys, text_values, image_mask, text_mask, heads):
    head_width = queries.shape[1] // heads
    score_scale = head_width ** (-0.5)
    dims = (((1,), (1,)), ((), ()))

    def one_head(head_index):
        column_start = head_index * head_width
        query_part = lax.dynamic_slice_in_dim(queries, column_start, head_width, 1)
        key_part = lax.dynamic_slice_in_dim(image_keys, column_start, head_width, 1)
        value_part = lax.dynamic_slice_in_dim(image_values, column_start, head_width, 1)
        text_key_part = lax.dynamic_slice_in_dim(text_keys, column_start, head_width, 1)
        text_value_part = lax.dynamic_slice_in_dim(text_values, column_start, head_width, 1)
        image_scores = (
            lax.dot_general(query_part, key_part, dims, preferred_element_type=jnp.float32)
            * score_scale
        )
        text_scores = (
            lax.dot_general(query_part, text_key_part, dims, preferred_element_type=jnp.float32)
            * score_scale
        )
        image_weights = jnp.where(image_mask, jnp.exp(image_scores), 0.0)
        text_weights = jnp.where(text_mask, jnp.exp(text_scores), 0.0)
        denominator = jnp.sum(image_weights, 1, keepdims=True) + jnp.sum(
            text_weights, 1, keepdims=True
        )
        image_weights = (image_weights / denominator).astype(jnp.bfloat16)
        text_weights = (text_weights / denominator).astype(jnp.bfloat16)
        return jnp.dot(image_weights, value_part, preferred_element_type=jnp.float32) + jnp.dot(
            text_weights, text_value_part, preferred_element_type=jnp.float32
        )

    stacked = lax.map(one_head, jnp.arange(heads, dtype=jnp.int32))
    return stacked.transpose(1, 0, 2).reshape(queries.shape[0], -1).astype(jnp.bfloat16)


def conv_rows(above, centre, below, upsample_weight, upsample_bias):
    tap_list = []
    for row_set in (above, centre, below):
        breadth = row_set.shape[1]
        padded = jnp.pad(row_set, ((0, 0), (1, 1), (0, 0)))
        for col_shift in range(3):
            tap_list.append(padded[:, col_shift : col_shift + breadth])
    patches = jnp.concatenate(tap_list, -1)
    flat_patches = patches.reshape(-1, patches.shape[-1])
    product = jnp.dot(flat_patches, upsample_weight, precision=highest).reshape(centre.shape)
    return product + upsample_bias + centre


def per_device(
    coarse_hidden,
    coarse_modulation,
    final_weight,
    coarse_latent,
    step_index,
    guide_index,
    guide_scales,
    upsample_weight,
    upsample_bias,
    embed_weight,
    embed_bias,
    fine_modulation,
    project_weight,
    query_gain,
    key_gain,
    text_keys,
    text_values,
    text_length,
    output_weight,
):
    row_count = coarse_hidden.shape[1]
    row_cells = coarse_hidden.shape[2]
    model_width = coarse_hidden.shape[3]
    channels = final_weight.shape[1]
    head_width = query_gain.shape[0]
    inner = project_weight.shape[1] // 3
    reach = max(row_count // 2, 1)
    branch = lax.axis_index("cfg")
    seq_index = lax.axis_index("seq")
    normed = layer_norm(coarse_hidden[0].astype(jnp.float32))
    modulated = (normed * (1.0 + coarse_modulation[0, 1]) + coarse_modulation[0, 0]).astype(
        jnp.bfloat16
    )
    velocity = jnp.dot(
        modulated.reshape(row_count * row_cells, model_width),
        final_weight,
        preferred_element_type=jnp.float32,
    ).reshape(row_count, row_cells * channels)
    partner = from_partner(velocity, "cfg", 0)
    conditional = jnp.where(branch == 0, velocity, partner)
    unconditional = jnp.where(branch == 0, partner, velocity)
    guidance = pick_scale(guide_scales, guide_index[0])
    guided = unconditional + guidance * (conditional - unconditional)
    stepped = coarse_latent + (sigma_at(step_index[0] + 1) - sigma_at(step_index[0])) * guided

    def embed_rows(grid_rows):
        grid_tokens = grid_rows.reshape(-1, channels).astype(jnp.bfloat16)
        state = jnp.dot(grid_tokens, embed_weight, preferred_element_type=jnp.float32) + embed_bias
        normed_state = (layer_norm(state) * (1.0 + fine_modulation[1]) + fine_modulation[0]).astype(
            jnp.bfloat16
        )
        return (state, normed_state)

    latent_grid = stepped.reshape(row_count, row_cells, channels)
    rim_width = reach + 1
    rimmed = with_halo(latent_grid, (("seq", 0),), rim_width)
    upsampled = jnp.repeat(jnp.repeat(rimmed, 2, 0), 2, 1)
    span = row_count + 2 * reach
    wide_grid = conv_rows(
        upsampled[1 : 1 + 2 * span],
        upsampled[2 : 2 + 2 * span],
        upsampled[3 : 3 + 2 * span],
        upsample_weight,
        upsample_bias,
    )
    grouped = wide_grid.reshape(span, 2, 2 * row_cells, channels)
    fine_grid = lax.dynamic_index_in_dim(
        grouped[reach : reach + row_count], branch, 1, keepdims=False
    )
    fine_state, fine_normed = embed_rows(fine_grid)

    def normed_rows(grid_rows):
        return embed_rows(grid_rows)[1]

    key_normed = lax.map(normed_rows, wide_grid.reshape(span, 4 * row_cells, channels)).reshape(
        -1, model_width
    )
    token_count = fine_normed.shape[0]
    weight_piece = lax.all_gather(project_weight, ("cfg", "seq"), axis=0, tiled=True)
    query_sum = jnp.dot(fine_normed, weight_piece[:, :inner], preferred_element_type=jnp.float32)
    key_sum = jnp.dot(
        key_normed, weight_piece[:, inner : 2 * inner], preferred_element_type=jnp.float32
    )
    value_sum = jnp.dot(
        key_normed, weight_piece[:, 2 * inner :], preferred_element_type=jnp.float32
    )
    queries = rms_heads(query_sum, query_gain, head_width).astype(jnp.bfloat16)
    keys = rms_heads(key_sum, key_gain, head_width).astype(jnp.bfloat16)
    values = value_sum.astype(jnp.bfloat16)
    image_keys, image_values = (keys, values)
    normed_text_keys = rms_heads(text_keys.astype(jnp.float32), key_gain, head_width).astype(
        jnp.bfloat16
    )
    key_count = image_keys.shape[0]
    query_rows = jnp.arange(token_count, dtype=jnp.int32) // (2 * row_cells)
    key_rows = jnp.arange(key_count, dtype=jnp.int32) // (4 * row_cells)
    distance = key_rows[None, :] - query_rows[:, None]
    global_rows = seq_index * row_count + key_rows - reach
    row_valid = (global_rows >= 0) & (global_rows < row_count * lax.axis_size("seq"))
    image_mask = (distance >= 0) & (distance <= 2 * reach) & row_valid[None, :]
    text_mask = (jnp.arange(text_keys.shape[0], dtype=jnp.int32) < text_length[0])[None, :]
    attended = attend(
        queries,
        image_keys,
        image_values,
        normed_text_keys,
        text_values,
        image_mask,
        text_mask,
        HEADS,
    )
    output_part = jnp.dot(
        attended,
        lax.all_gather(output_weight, ("cfg", "seq"), axis=1, tiled=True),
        preferred_element_type=jnp.float32,
    )
    fine_hidden = (fine_state + fine_modulation[2] * output_part).astype(jnp.bfloat16)
    fine_hidden = fine_hidden.reshape(row_count, 1, 2 * row_cells, model_width)
    fine_latent = fine_grid.reshape(row_count, 1, 2 * row_cells * channels)
    return (guided, fine_latent, fine_hidden)


def solution(mesh):
    placed = (
        P("cfg", "seq", None, None),
        P("cfg", None, None),
        P(),
        P("seq", None),
        P(),
        P(),
        P(),
        P(),
        P(),
        P(),
        P(),
        P(),
        P(("cfg", "seq"), None),
        P(),
        P(),
        P(),
        P(),
        P(),
        P(None, ("cfg", "seq")),
    )
    return jax.shard_map(
        per_device,
        mesh=mesh,
        in_specs=placed,
        out_specs=(P("seq", None), P("seq", "cfg", None), P("seq", "cfg", None, None)),
        check_vma=False,
    )
```

profile of v0, /device:TPU:0, one launch (start us, length us, event | category | flops | bytes accessed | tf_op | source)
XLA Modules:
  0.0 220.7 jit_solution(1284092491841628550)
XLA Ops:
  9.3 1.3 fusion.43
  11.5 1.4 fusion.47
  13.4 3.0 %collective-permute-start = (f32[2,2048]{1,0:T(2,128)S(1)}, f32[2,2048]{1,0:T(2,128)S(1)}, u32[]{:S(2)}, u32[]{:S(2)}) collective-permute-start(f32[2,2048]{1,0:T(2,128)S(1)} %reshape.235), channel_id=1, source_target_pairs={{0,16},{16,0},{1,17},{17,1},{2,18},{18,2},{3,19},{19,3},{4,20},{20... | collective-permute-start | bytes 49160 | tf_op jit(solution)/shard_map/ppermute | solution.py:16
  22.3 1.5 collective-permute-start.1
  25.2 3.4 %collective-permute-done.2 = f32[2,64,32]{2,1,0:T(8,128)S(1)} collective-permute-done((f32[2,64,32]{2,1,0:T(8,128)S(1)}, f32[2,64,32]{2,1,0:T(8,128)S(1)}, u32[]{:S(2)}, u32[]{:S(2)}) %collective-permute-start.2) | collective-permute-done | bytes 16416 | tf_op jit(solution)/shard_map/ppermute | solution.py:27
  31.8 9.6 %while.21 = (s32[]{:T(128)}, bf16[4,256,2048]{2,1,0:T(8,128)(2,1)}, bf16[4,256,32]{2,1,0:T(8,128)(2,1)S(1)}, bf16[32,2048]{1,0:T(8,128)(2,1)S(1)}, f32[2048]{0:T(1024)S(1)}, /*index=5*/f32[3,2048]{1,0:T(4,128)S(1)}, s32[]{:T(128)}) while((s32[]{:T(128)}, bf16[4,256,2048]{2,1,0:T(8,128)(2,1)}, bf16[4,256,32]{2,1,0:T(8,128)(2,1)S(1)}, ...), condition=%wide.region_9.10_spmd, body=%wide.region_6.9_spmd.sunk | while | flops 38799616 | bytes 7603793 | solution.py:178
  32.9 1.5 fusion.93
  35.3 1.5 fusion.93
  37.7 1.4 fusion.93
  40.0 1.4 fusion.93
  43.2 66.0 %all-gather.3.cloned.1.call-done = bf16[2048,3072]{1,0:T(8,128)(2,1)} async-done(((bf16[64,3072]{1,0:T(8,128)(2,1)}), bf16[2048,3072]{1,0:T(8,128)(2,1)}) %all-gather.3.cloned.1.call-update) | async-done | bytes 12582928 | tf_op jit(solution)/shard_map/all_gather | solution.py:182
  109.2 4.6 %slice_bitcast_fusion = bf16[1024,2048]{0,1:T(8,128)(2,1)} fusion(bf16[2048,3072]{1,0:T(8,128)(2,1)} %all-gather.3.cloned.1.call-done), kind=kLoop, calls=%fused_computation.42 | loop fusion | bytes 8388608 | tf_op jit(solution)/shard_map/dot_general | solution.py:184
  113.8 6.5 %copy.109 = bf16[1024,2048]{1,0:T(8,128)(2,1)} copy(bf16[1024,2048]{0,1:T(8,128)(2,1)} %slice_bitcast_fusion) | data formatting | bytes 8388608 | tf_op jit(solution)/shard_map/dot_general | solution.py:184
  120.4 10.0 %multiply_reduce_fusion.1 = (f32[1024,8]{0,1:T(8,128)S(1)}, f32[1024,8,128]{0,2,1:T(8,128)}) fusion(bf16[1024,2048,1]{1,0,2:T(8,128)(2,1)} %bitcast.23, bf16[8,128,2048]{2,1,0:T(8,128)(2,1)} %bitcast.120), kind=kOutput, calls=%fused_computation.46 | convolution fusion | flops 4297056256 | bytes 12615680 | tf_op jit(solution)/shard_map/dot_general | solution.py:184
  130.3 3.5 %fusion.29 = f32[256,1024]{1,0:T(8,128)S(1)} fusion(bf16[2048,3072]{1,0:T(8,128)(2,1)} %all-gather.3.cloned.1.call-done, f32[256,2048]{1,0:T(8,128)S(1)} %get-tuple-element.275, f32[2048]{0:T(1024)S(1)} %bitcast.139, f32[2048]{0:T(1024)S(1)} %bitcast.138, f32[256]{0:T(256)S(1)} %add_rsqrt_fusion.4, f32[256]{0:T(256)S(1)} %broadcast_multiply_fusion.1), kind=kOutput, calls=%fused_computation.43 | convolution fusion | flops 1076363264 | bytes 7358464 | tf_op jit(solution)/shard_map/dot_general | solution.py:183
  135.1 1.7 reduce_sum.113
  137.0 4.3 %multiply_convert_fusion = bf16[1024,8,128]{0,2,1:T(8,128)(2,1)} fusion(f32[1024,8,128]{0,2,1:T(8,128)} %get-tuple-element.277, f32[128]{0:T(128)S(1)} %copy-done.8, f32[1024,8]{0,1:T(8,128)S(1)} %add_rsqrt_fusion.1), kind=kLoop, calls=%fused_computation.45 | loop fusion | flops 3145728 | bytes 6324736 | tf_op jit(solution)/shard_map/convert_element_type | solution.py:191
  142.7 9.4 %fusion.33 = bf16[1024,1024]{1,0:T(8,128)(2,1)} fusion(bf16[1024,2048]{1,0:T(8,128)(2,1)} %bitcast.22, bf16[2048,3072]{1,0:T(8,128)(2,1)} %all-gather.3.cloned.1.call-done), kind=kOutput, calls=%fused_computation.53 | convolution fusion | flops 4296015872 | bytes 10485760 | tf_op jit(solution)/shard_map/dot_general | solution.py:187
  152.1 57.2 %while.22 = (s32[]{:T(128)}, bf16[8,256,128]{1,2,0:T(8,128)(2,1)S(1)}, s32[8]{0:T(128)S(1)}, bf16[256,1024]{1,0:T(8,128)(2,1)}, bf16[1024,1024]{0,1:T(8,128)(2,1...) while((s32[]{:T(128)}, ...), condition=%wide.region_15.16_spmd.clone, body=%wide.region_12.15_spmd.clone.sunk | while | flops 170786816 | bytes 4013791 | solution.py:86
  153.3 1.7 fusion.97
  157.9 1.3 fusion.99
  160.5 1.6 fusion.97
  165.0 1.3 fusion.99
  167.7 1.6 fusion.97
  174.8 1.6 fusion.97
  182.0 1.6 fusion.97
  189.1 1.6 fusion.97
  193.6 1.3 fusion.99
  196.3 1.6 fusion.97
  203.4 1.6 fusion.97
  207.9 1.3 fusion.99
  209.4 4.5 %fusion.32 = bf16[256,2048]{1,0:T(8,128)(2,1)} fusion(f32[256,2048]{1,0:T(8,128)S(1)} %get-tuple-element.275, bf16[256,1024]{0,1:T(8,128)(2,1)S(1)} %bitcast.140, bf16[1024,2048]{0,1:T(8,128)(2,1)} %all-gather.5.cloned.1.call-done, f32[2048]{0:T(1024)S(1)} %bitcast.137), kind=kOutput, calls=%fused_computation.50 | convolution fusion | flops 1075314688 | bytes 7872512 | tf_op jit(solution)/shard_map/dot_general | solution.py:215
  (185 shorter events, 54.1 us)
Async XLA Ops:
  7.2 5.8 %copy-start = (bf16[2048,32]{0,1:T(8,128)(2,1)S(1)}, bf16[2048,32]{0,1:T(8,128)(2,1)}, u32[]{:S(2)}) copy-start(bf16[2048,32]{0,1:T(8,128)(2,1)} %param.25) | copy-start | bytes 393220
  7.2 9.9 %copy-start.3 = (f32[3,2048]{1,0:T(4,128)S(1)}, f32[3,2048]{1,0:T(4,128)}, u32[]{:S(2)}) copy-start(f32[3,2048]{1,0:T(4,128)} %param.34) | copy-start | bytes 73732
  7.2 9.9 %copy-start.10 = (f32[128]{0:T(128)S(1)}, f32[128]{0:T(128)}, u32[]{:S(2)}) copy-start(f32[128]{0:T(128)} %param.36) | copy-start | bytes 1540
  7.2 9.9 %copy-start.2 = (bf16[256,1024]{1,0:T(8,128)(2,1)S(1)}, bf16[256,1024]{1,0:T(8,128)(2,1)}, u32[]{:S(2)}) copy-start(bf16[256,1024]{1,0:T(8,128)(2,1)} %param.38) | copy-start | bytes 1572868
  7.2 102.0 %all-gather.3.cloned.1.call-start = ((), (), s32[]{:S(2)}) async-start(), calls=%async_computation | async-start | bytes 12976128 | tf_op jit(solution)/shard_map/all_gather | solution.py:182
  7.9 201.4 %all-gather.5.cloned.1.call-start = ((), (), s32[]{:S(2)}) async-start(), calls=%async_computation.1 | async-start | bytes 4325376 | tf_op jit(solution)/shard_map/all_gather | solution.py:217
  13.4 7.6 %collective-permute-start = (f32[2,2048]{1,0:T(2,128)S(1)}, f32[2,2048]{1,0:T(2,128)S(1)}, u32[]{:S(2)}, u32[]{:S(2)}) collective-permute-start(f32[2,2048]{1,0:T(2,128)S(1)} %reshape.235), channel_id=1, source_target_pairs={{0,16},{16,0},{1,17},{17,1},{2,18},{18,2},{3,19},{19,3},{4,20},{20... | collective-permute-start | bytes 49160 | tf_op jit(solution)/shard_map/ppermute | solution.py:16
  17.3 0.8 copy-start.8
  17.3 0.8 copy-start.6
  17.9 3.1 %copy-start.7 = (f32[2,2048]{1,0:T(2,128)S(1)}, f32[2,2048]{1,0:T(2,128)}, u32[]{:S(2)}) copy-start(f32[2,2048]{1,0:T(2,128)} %param.26) | copy-start | bytes 49156
  22.3 2.8 %collective-permute-start.1 = (f32[2,64,32]{2,1,0:T(8,128)S(1)}, f32[2,64,32]{2,1,0:T(8,128)S(1)}, u32[]{:S(2)}, u32[]{:S(2)}) collective-permute-start(f32[2,64,32]{2,1,0:T(8,128)S(1)} %reshape.236), channel_id=1, source_target_pairs={{0,1},{1,2},{2,3},{3,4},{4,5},{5,6},{6,7},{7,8},{8,9},{9,10},{10,1... | collective-permute-start | bytes 49160 | tf_op jit(solution)/shard_map/ppermute | solution.py:24
  23.8 4.7 %collective-permute-start.2 = (f32[2,64,32]{2,1,0:T(8,128)S(1)}, f32[2,64,32]{2,1,0:T(8,128)S(1)}, u32[]{:S(2)}, u32[]{:S(2)}) collective-permute-start(f32[2,64,32]{2,1,0:T(8,128)S(1)} %reshape.236), channel_id=1, source_target_pairs={{1,0},{2,1},{3,2},{4,3},{5,4},{6,5},{7,6},{8,7},{9,8},{10,9},{11,1... | collective-permute-start | bytes 49160 | tf_op jit(solution)/shard_map/ppermute | solution.py:27
  29.6 1.1 copy-start.5
  29.6 1.1 copy-start.9
  30.2 1.6 copy-start.1
  30.3 1.6 copy-start.4
  142.7 9.4 %copy-start.11 = (bf16[8,256,128]{1,2,0:T(8,128)(2,1)S(1)}, bf16[8,256,128]{1,2,0:T(8,128)(2,1)}, u32[]{:S(2)}) copy-start(bf16[8,256,128]{1,2,0:T(8,128)(2,1)} %custom-call.3) | copy-start | bytes 1572868
Sparse Core Ops, SparseCore 0:
  10.9 98.2 all-gather.2
  112.1 60.3 all-gather.4
where the time goes:
time: 223 us; the launch traced here: 221 us
  matrix products  72 us (32%)
  waiting for transfers between devices  70.1 us (31%)
  other arithmetic  28.7 us (13%)
  local copies, waits for them, and re-layouts  22.7 us (10%)
  between operations  16 us (7%)
  starting transfers between devices  5.86 us (3%)
  loops' own time  5.37 us (2%)
    all_gather x1, waiting for transfers between devices, per_device(): lax.all_gather(project_weight, ('cfg', 'seq'), axis=0, tiled=True)  66 us
    dot_general x8, matrix products, one_head(): lax.dot_general(query_part, key_part, dims, preferred_element_type=jnp.fl...  13.1 us
    dot_general x2, local copies, waits for them, and re-layouts, per_device(): jnp.dot(key_normed, weight_piece[:, inner:2 * inner], preferred_element_t...  11.2 us
    dot_general x8, matrix products, one_head(): jnp.dot(image_weights, value_part, preferred_element_type=jnp.float32)  10.5 us
    dot_general x1, matrix products, per_device(): jnp.dot(key_normed, weight_piece[:, inner:2 * inner], preferred_element_t...  9.97 us
    dot_general x1, matrix products, per_device(): jnp.dot(key_normed, weight_piece[:, 2 * inner:], preferred_element_type=j...  9.36 us
    dot_general x8, matrix products, one_head(): lax.dot_general(query_part, text_key_part, dims, preferred_element_type=j...  8.8 us
    dot_general x8, matrix products, one_head(): jnp.dot(text_weights, text_value_part, preferred_element_type=jnp.float32)  8.65 us
  transfers between devices with their start and end apart: 5, of which 2 were waited for; matrix products, arithmetic and copies ran while one was open for 54% of the time, Pallas kernels for 0%

commit v1 on v0

v1 whole, which is shorter than its diff:
```python
import functools

import jax
import jax.numpy as jnp
from jax import lax
from jax.experimental import pallas as pl
from jax.experimental.pallas import tpu as pltpu
from jax.sharding import PartitionSpec as P

HEADS = 8
STEPS = 50

epsilon = 1e-06
flow_shift = 5.0
highest = lax.Precision.HIGHEST
f32 = jnp.float32
bf16 = jnp.bfloat16
LOG2E = 1.4426950408889634
TERMS = 40
SLAB = 48
DEPTH = 256


def vmem(count):
    return [pl.BlockSpec(memory_space=pltpu.VMEM) for _ in range(count)]


def smem(count):
    return [pl.BlockSpec(memory_space=pltpu.SMEM) for _ in range(count)]


def cost(flops, moved):
    return pl.CostEstimate(flops=int(flops), bytes_accessed=int(moved), transcendentals=0)


def dot_rows(left, right):
    return lax.dot_general(left, right, (((0,), (0,)), ((), ())), preferred_element_type=f32)


def split(values):
    high = values.astype(bf16)
    return high, (values - high.astype(f32)).astype(bf16)


def centred_embedding(embed, bias):
    width = embed.shape[1]
    embed = embed - jnp.sum(embed, -1, keepdims=True) * (1.0 / width)
    bias = bias - jnp.sum(bias, -1, keepdims=True) * (1.0 / width)
    return embed, bias


def with_tail(body, first, second):
    row = lax.broadcasted_iota(jnp.int32, (16, body.shape[1]), 0)
    tail = jnp.where(row == 0, first, jnp.where(row == 1, second, 0.0))
    return jnp.concatenate([body, tail], 0)


def partial_kernel(seq_count, embed_ref, bias_ref, mod_ref, weight_ref, keep_ref, send_ref):
    seq_index = lax.axis_index("seq")
    core = seq_index % 2
    depth = weight_ref.shape[0]
    half = keep_ref.shape[1]
    embed = embed_ref[...].astype(f32)
    width = embed.shape[1]
    embed_mean = jnp.sum(embed, -1, keepdims=True) * (1.0 / width)
    bias_mean = jnp.sum(bias_ref[...], -1, keepdims=True) * (1.0 / width)
    start = (lax.axis_index("cfg") * seq_count + seq_index) * depth
    base = pl.multiple_of(start // 128 * 128, 128)
    offset = start - base
    window = pl.ds(base, 128)
    scale = 1.0 + mod_ref[1:2, window]
    rows = with_tail(
        (embed_ref[:, window].astype(f32) - embed_mean) * scale,
        (bias_ref[:, window] - bias_mean) * scale,
        mod_ref[0:1, window],
    )
    rows = pltpu.roll(rows, (128 - offset) % 128, 1)[:, :depth]
    high, low = split(rows)
    left = jnp.concatenate([high, low], 0)

    def part(which):
        columns = pl.ds(pl.multiple_of(which * half, 128), half)
        product = jnp.dot(left, weight_ref[:, columns], preferred_element_type=f32)
        return product[:TERMS] + product[SLAB : SLAB + TERMS]

    send_ref[...] = part(1 - core).astype(bf16)
    keep_ref[...] = part(core)


def velocity_kernel(hidden_ref, mod_ref, weight_ref, out_ref):
    values = hidden_ref[...].astype(f32)
    width = values.shape[1]
    centred = values - jnp.sum(values, -1, keepdims=True) * (1.0 / width)
    variance = jnp.sum(centred * centred, -1, keepdims=True) * (1.0 / width)
    normed = centred * lax.rsqrt(variance + epsilon)
    modulated = (normed * (1.0 + mod_ref[1:2, :]) + mod_ref[0:1, :]).astype(bf16)
    out_ref[...] = jnp.dot(modulated, weight_ref[...], preferred_element_type=f32).T


def guide_kernel(step_ref, slot_ref, table_ref, own_ref, other_ref, latent_ref, guided_ref, next_ref):
    branch = lax.axis_index("cfg")
    own = own_ref[...]
    other = other_ref[...]
    first = branch == 0
    conditional = jnp.where(first, own, other)
    unconditional = jnp.where(first, other, own)
    table = table_ref[...]
    slots = lax.broadcasted_iota(jnp.int32, table.shape, 0) * table.shape[
        1
    ] + lax.broadcasted_iota(jnp.int32, table.shape, 1)
    picked = jnp.where(slots == slot_ref[0], table, 0.0)
    guidance = jnp.sum(jnp.sum(picked, 0, keepdims=True), 1, keepdims=True)
    guided = unconditional + guidance * (conditional - unconditional)

    def sigma(step):
        fraction = 1.0 - jnp.full((1, 128), step, jnp.int32).astype(f32) / STEPS
        return flow_shift * fraction / (1.0 + (flow_shift - 1.0) * fraction)

    change = (sigma(step_ref[0] + 1) - sigma(step_ref[0]))[:, :1]
    guided_ref[...] = guided
    next_ref[...] = latent_ref[...] + change * guided


def fine_kernel(
    cells,
    up_ref,
    own_ref,
    down_ref,
    taps_ref,
    shift_ref,
    embed_ref,
    bias_ref,
    text_ref,
    gain_ref,
    fine_ref,
    keys_ref,
    keys_t_ref,
    query_ref,
    token_ref,
    text_out_ref,
):
    channels, own_lanes = own_ref.shape
    rows = own_lanes // cells
    lanes = (rows + 2) * cells
    gain = gain_ref[...]
    head = gain.shape[1]
    for h in range(text_ref.shape[1] // head):
        part = text_ref[:, h * head : (h + 1) * head].astype(f32)
        mean = jnp.sum(part * part, -1, keepdims=True) * (1.0 / head)
        text_out_ref[:, h * head : (h + 1) * head] = (
            part * lax.rsqrt(mean + epsilon) * gain
        ).astype(bf16)

    extended = jnp.concatenate([up_ref[...], own_ref[...], down_ref[...]], 1)
    total = extended.shape[1]
    origin = own_lanes - cells
    lane = lax.broadcasted_iota(jnp.int32, (channels, lanes), 1) % cells

    def shifted(down, right):
        start = origin + down * cells + right
        moved = pltpu.roll(extended, (-start) % total, 1)[:, :lanes]
        if right < 0:
            moved = jnp.where(lane == 0, 0.0, moved)
        if right > 0:
            moved = jnp.where(lane == cells - 1, 0.0, moved)
        return moved

    around = {(i, j): shifted(i, j) for i in (-1, 0, 1) for j in (-1, 0, 1)}

    def tap(r, s):
        first = (3 * r + s) * channels
        return taps_ref[first : first + channels, :]

    blocks = {}
    for a in range(2):
        for c in range(2):
            patches, weights = [], []
            for i in (a - 1, a):
                for j in (c - 1, c):
                    merged = None
                    for r in range(3):
                        for s in range(3):
                            if (a + r - 1) // 2 == i and (c + s - 1) // 2 == j:
                                merged = tap(r, s) if merged is None else merged + tap(r, s)
                    patches.append(around[i, j])
                    weights.append(merged)
            stacked = jnp.concatenate(weights, 0).T
            product = jnp.dot(
                stacked, jnp.concatenate(patches, 0), precision=highest, preferred_element_type=f32
            )
            blocks[a, c] = product + shift_ref[...] + around[0, 0]

    embed, bias = centred_embedding(embed_ref[...].astype(f32), bias_ref[...])
    high, low = split(with_tail(embed, bias, jnp.zeros_like(bias)))
    pair = jnp.concatenate([high, low], 0)
    width = embed.shape[1]
    step = min(width, 512)

    def features(tokens):
        count = tokens.shape[1]
        one = jnp.ones((1, count), f32)
        values = with_tail(tokens.astype(f32), one, jnp.zeros_like(one)).astype(bf16)
        double = jnp.concatenate([values, values], 0)
        square = jnp.zeros((1, count), f32)
        for first in range(0, width, step):
            state = dot_rows(pair[:, first : first + step], double)
            square += jnp.sum(state * state, 0, keepdims=True)
        spread = lax.rsqrt(square * (1.0 / width) + epsilon)
        top, rest = split(with_tail(tokens.astype(f32) * spread, spread, one))
        fill = jnp.zeros((DEPTH - 3 * SLAB, count), bf16)
        return jnp.concatenate([top, rest, top, fill], 0)

    for a in range(2):
        for c in range(2):
            turned = features(blocks[a, c].astype(bf16)).T
            for r in range(rows + 2):
                first = (4 * r + 2 * a + c) * cells
                keys_ref[first : first + cells, :] = turned[r * cells : (r + 1) * cells, :]
    keys_t_ref[...] = keys_ref[...].T

    parity = lax.axis_index("cfg")
    tokens = jnp.zeros((channels, 2 * own_lanes), f32)
    cell = lax.broadcasted_iota(jnp.int32, (own_lanes, 2 * own_lanes), 0)
    place = lax.broadcasted_iota(jnp.int32, (own_lanes, 2 * own_lanes), 1)
    for c in range(2):
        mine = jnp.where(parity == 0, blocks[0, c], blocks[1, c])
        mine = pltpu.roll(mine, lanes - cells, 1)[:, :own_lanes]
        fine_ref[c] = mine
        chosen = jnp.where(place == 2 * cell + c, 1.0, 0.0).astype(bf16)
        tokens += jnp.dot(mine.astype(bf16), chosen, preferred_element_type=f32)
    token_ref[...] = tokens.astype(bf16)
    query_ref[...] = features(tokens.astype(bf16)).T


def attend_kernel(
    rows,
    window,
    length_ref,
    kept_ref,
    other_ref,
    keys_ref,
    keys_t_ref,
    query_ref,
    query_gain_ref,
    key_gain_ref,
    text_ref,
    text_values_ref,
    out_ref,
    mix_ref,
    value_ref,
):
    head_index = pl.program_id(0)
    heads = pl.num_programs(0)
    seq_index = lax.axis_index("seq")
    head = query_gain_ref.shape[1]
    half = kept_ref.shape[1]
    key_count = keys_ref.shape[0]
    text_count = text_ref.shape[0]
    inner = heads * head
    low_ok = seq_index > 0
    high_ok = seq_index < lax.axis_size("seq") - 1
    key_row = lax.broadcasted_iota(jnp.int32, (key_count, head), 0)
    allowed = (low_ok | (key_row >= window)) & (high_ok | (key_row < key_count - window))
    text_row = lax.broadcasted_iota(jnp.int32, (text_count, head), 0)
    text_allowed = text_row < length_ref[0]

    @pl.when(head_index == 0)
    def _():
        core = seq_index % 2
        mix_ref[...] = jnp.zeros_like(mix_ref)
        kept = kept_ref[...]
        top, rest = split(kept)
        mine = pl.ds(pl.multiple_of(core * half, 128), half)
        mix_ref[0:TERMS, mine] = top
        mix_ref[SLAB : SLAB + TERMS, mine] = top
        mix_ref[2 * SLAB : 2 * SLAB + TERMS, mine] = rest
        theirs = pl.ds(pl.multiple_of((1 - core) * half, 128), half)
        mix_ref[0:TERMS, theirs] = other_ref[...]
        mix_ref[SLAB : SLAB + TERMS, theirs] = other_ref[...]
        value_ref[0:key_count, head : 2 * head] = jnp.where(allowed, 1.0, 0.0).astype(bf16)
        value_ref[key_count : key_count + text_count, head : 2 * head] = jnp.where(
            text_allowed, 1.0, 0.0
        ).astype(bf16)

    def columns(which):
        return pl.ds(pl.multiple_of(which * inner + head_index * head, 128), head)

    query = jnp.dot(query_ref[...], mix_ref[:, columns(0)], preferred_element_type=f32)
    mean = jnp.sum(query * query, -1, keepdims=True) * (1.0 / head)
    query = (query * lax.rsqrt(mean + epsilon) * query_gain_ref[...]).astype(bf16)
    keys = dot_rows(mix_ref[:, columns(1)], keys_t_ref[...])
    mean = jnp.sum(keys * keys, 0, keepdims=True) * (1.0 / head)
    keys = (keys * lax.rsqrt(mean + epsilon) * key_gain_ref[...]).astype(bf16)
    values = jnp.dot(keys_ref[...], mix_ref[:, columns(2)], preferred_element_type=f32)
    value_ref[0:key_count, 0:head] = jnp.where(allowed, values, 0.0).astype(bf16)
    value_ref[key_count : key_count + text_count, 0:head] = jnp.where(
        text_allowed, text_values_ref[...].astype(f32), 0.0
    ).astype(bf16)
    factor = head ** (-0.5) * LOG2E
    tokens = query.shape[0] // rows
    for r in range(rows):
        part = query[r * tokens : (r + 1) * tokens]
        near = slice(r * window, (r + 3) * window)
        scores = jnp.dot(part, keys[:, near], preferred_element_type=f32)
        text_scores = lax.dot_general(
            part, text_ref[...], (((1,), (1,)), ((), ())), preferred_element_type=f32
        )
        mixed = jnp.dot(
            jnp.exp2(scores * factor).astype(bf16), value_ref[near, :], preferred_element_type=f32
        ) + jnp.dot(
            jnp.exp2(text_scores * factor).astype(bf16),
            value_ref[key_count : key_count + text_count, :],
            preferred_element_type=f32,
        )
        out_ref[r * tokens : (r + 1) * tokens, :] = (mixed[:, :head] / mixed[:, head:]).astype(bf16)


def output_kernel(
    orders,
    attended_ref,
    token_ref,
    embed_ref,
    bias_ref,
    gate_ref,
    own_a_ref,
    own_b_ref,
    other_a_ref,
    other_b_ref,
    out_ref,
):
    chips, piece, inner = own_a_ref.shape
    seq_index = lax.axis_index("seq")
    core = seq_index % 2
    coordinate = {"cfg": lax.axis_index("cfg"), "seq": seq_index // 2}
    seq_chips = lax.axis_size("seq") // 2
    attended = attended_ref[...]
    tokens = token_ref[...]

    def place(chip, order):
        target = {"cfg": chip // seq_chips, "seq": chip % seq_chips}
        position = 0
        for level, (axis, bit) in enumerate(order):
            shift = bit - 1 if axis == "seq" else bit
            differs = ((coordinate[axis] >> shift) & 1) ^ ((target[axis] >> shift) & 1)
            position = position + (differs << level)
        return position

    for chip in range(chips):
        at_a, at_b = place(chip, orders[0]), place(chip, orders[1])
        weight = jnp.concatenate(
            [own_a_ref[at_a], own_b_ref[at_b], other_a_ref[at_a], other_b_ref[at_b]], 0
        )
        product = lax.dot_general(
            attended, weight, (((1,), (1,)), ((), ())), preferred_element_type=f32
        )
        product = pltpu.roll(product, core * 2 * piece, 1)
        lanes = slice(chip * 4 * piece, (chip + 1) * 4 * piece)
        state = dot_rows(tokens, embed_ref[:, lanes]) + bias_ref[:, lanes]
        out_ref[:, lanes] = (state + gate_ref[:, lanes] * product).astype(bf16)


def per_device(
    coarse_hidden,
    coarse_modulation,
    final_weight,
    coarse_latent,
    step_index,
    guide_index,
    guide_scales,
    upsample_weight,
    upsample_bias,
    embed_weight,
    embed_bias,
    fine_modulation,
    project_weight,
    query_gain,
    key_gain,
    text_keys,
    text_values,
    text_length,
    output_weight,
):
    rows = coarse_hidden.shape[1]
    cells = coarse_hidden.shape[2]
    width = coarse_hidden.shape[3]
    channels = final_weight.shape[1]
    head = query_gain.shape[0]
    inner = project_weight.shape[1] // 3
    cfg_count = lax.axis_size("cfg")
    seq_count = lax.axis_size("seq")
    seq_index = lax.axis_index("seq")
    seq_bits = seq_count.bit_length() - 1
    assert seq_count == 1 << seq_bits and cfg_count == 2 and rows >= 2
    own = rows * cells
    fine_tokens = 2 * own
    key_count = (rows + 2) * 4 * cells
    text_count = text_keys.shape[0]
    bias_row = embed_bias.reshape(1, width)

    def swap(value, *stages):
        size = cfg_count * seq_count
        flip = 0
        for axis, bit in stages:
            flip |= seq_count if axis == "cfg" else 1 << bit
        return lax.ppermute(value, ("cfg", "seq"), [(i, i ^ flip) for i in range(size)])

    across = ("seq", 0)
    levels = [("cfg", 0)] + [("seq", bit) for bit in range(1, seq_bits)]

    half = 3 * inner // 2
    kept, sent = pl.pallas_call(
        functools.partial(partial_kernel, seq_count),
        out_shape=(
            jax.ShapeDtypeStruct((TERMS, half), f32),
            jax.ShapeDtypeStruct((TERMS, half), bf16),
        ),
        in_specs=vmem(4),
        out_specs=tuple(vmem(2)),
        cost_estimate=cost(2 * 96 * 64 * 3 * inner, 1e6),
        name="partial_mix",
    )(embed_weight, bias_row, fine_modulation, project_weight)

    velocity = pl.pallas_call(
        velocity_kernel,
        out_shape=jax.ShapeDtypeStruct((channels, own), f32),
        in_specs=vmem(3),
        out_specs=vmem(1)[0],
        cost_estimate=cost(2 * own * width * 128, 1e6),
        name="velocity",
    )(coarse_hidden.reshape(own, width), coarse_modulation[0], final_weight)

    total = kept + swap(sent, across).astype(f32)
    partner = swap(velocity, ("cfg", 0))

    piece = output_weight.shape[1] // 2
    turned = output_weight.T
    orders = (tuple(levels), tuple(levels[2:] + levels[:2]))

    def gathered(block, order):
        held = block[None]
        for stage in order:
            held = jnp.concatenate([held, swap(held, stage)], 0)
        return held

    first, second = levels[0], levels[1]
    rounded = total.astype(bf16)
    total = (
        total
        + swap(rounded, first).astype(f32)
        + swap(rounded, second).astype(f32)
        + swap(rounded, first, second).astype(f32)
    )
    for stage in levels[2:]:
        total = total + swap(total.astype(bf16), stage).astype(f32)
    others = swap(total.astype(bf16), across)

    latent = coarse_latent.reshape(own, channels).T
    guided, stepped = pl.pallas_call(
        guide_kernel,
        out_shape=(jax.ShapeDtypeStruct((channels, own), f32),) * 2,
        in_specs=smem(2) + vmem(4),
        out_specs=tuple(vmem(2)),
        cost_estimate=cost(1e6, 1e5),
        name="guide",
    )(step_index, guide_index, guide_scales.reshape(-1, 128), velocity, partner, latent)

    forward = [(i, i + 1) for i in range(seq_count - 1)]
    backward = [(target, source) for source, target in forward]
    up = lax.ppermute(stepped, "seq", forward)
    down = lax.ppermute(stepped, "seq", backward)

    fine, keys, keys_t, query, tokens, text_normed = pl.pallas_call(
        functools.partial(fine_kernel, cells),
        out_shape=(
            jax.ShapeDtypeStruct((2, channels, own), f32),
            jax.ShapeDtypeStruct((key_count, DEPTH), bf16),
            jax.ShapeDtypeStruct((DEPTH, key_count), bf16),
            jax.ShapeDtypeStruct((fine_tokens, DEPTH), bf16),
            jax.ShapeDtypeStruct((channels, fine_tokens), bf16),
            jax.ShapeDtypeStruct(text_keys.shape, bf16),
        ),
        in_specs=vmem(9),
        out_specs=tuple(vmem(6)),
        cost_estimate=cost(4e9, 4e6),
        name="fine_features",
    )(
        up,
        stepped,
        down,
        upsample_weight,
        upsample_bias.reshape(channels, 1),
        embed_weight,
        bias_row,
        text_keys,
        key_gain.reshape(1, head),
    )

    whole = pl.BlockSpec(memory_space=pltpu.VMEM)
    per_head = pl.BlockSpec((text_count, head), lambda h: (0, h))
    attended = pl.pallas_call(
        functools.partial(attend_kernel, rows, 4 * cells),
        grid=(HEADS,),
        out_shape=jax.ShapeDtypeStruct((fine_tokens, inner), bf16),
        in_specs=smem(1) + [whole] * 7 + [per_head, per_head],
        out_specs=pl.BlockSpec((fine_tokens, head), lambda h: (0, h)),
        scratch_shapes=[
            pltpu.VMEM((DEPTH, 3 * inner), bf16),
            pltpu.VMEM((key_count + text_count, 2 * head), bf16),
        ],
        cost_estimate=cost(8e9, 4e6),
        name="attend",
    )(
        text_length,
        total,
        others,
        keys,
        keys_t,
        query,
        query_gain.reshape(1, head),
        key_gain.reshape(head, 1),
        text_normed,
        text_values,
    )

    own_a = gathered(turned[:piece], orders[0])
    own_b = gathered(turned[piece:], orders[1])
    other_a = swap(own_a, across)
    other_b = swap(own_b, across)
    gate = fine_modulation[2:3]
    if piece % 16 == 0:
        hidden = pl.pallas_call(
            functools.partial(output_kernel, orders),
            out_shape=jax.ShapeDtypeStruct((fine_tokens, width), bf16),
            in_specs=vmem(9),
            out_specs=vmem(1)[0],
            cost_estimate=cost(2e9, 6e6),
            name="output",
        )(attended, tokens, embed_weight, bias_row, gate, own_a, own_b, other_a, other_b)
    else:
        chip = jnp.arange(cfg_count * seq_count // 2, dtype=jnp.int32)
        seq_chips = seq_count // 2
        apart = {
            "cfg": chip // seq_chips ^ lax.axis_index("cfg"),
            "seq": chip % seq_chips ^ seq_index // 2,
        }

        def ordered(block, order):
            position = jnp.zeros_like(chip)
            for level, (axis, bit) in enumerate(order):
                shift = bit - 1 if axis == "seq" else bit
                position = position + ((apart[axis] >> shift & 1) << level)
            return jnp.take(block, position, axis=0)

        mine = jnp.concatenate([ordered(own_a, orders[0]), ordered(own_b, orders[1])], 1)
        theirs = jnp.concatenate([ordered(other_a, orders[0]), ordered(other_b, orders[1])], 1)
        even = seq_index % 2 == 0
        both = jnp.stack([jnp.where(even, mine, theirs), jnp.where(even, theirs, mine)], 1)
        weight = both.reshape(width, inner)
        product = lax.dot_general(
            attended, weight, (((1,), (1,)), ((), ())), preferred_element_type=f32
        )
        state = dot_rows(tokens, embed_weight) + bias_row
        hidden = (state + gate * product).astype(bf16)

    fine_latent = fine.transpose(2, 0, 1).reshape(rows, 1, 2 * cells * channels)
    return (
        guided.T.reshape(rows, cells * channels),
        fine_latent,
        hidden.reshape(rows, 1, 2 * cells, width),
    )


def solution(mesh):
    placed = (
        P("cfg", "seq", None, None),
        P("cfg", None, None),
        P(),
        P("seq", None),
        P(),
        P(),
        P(),
        P(),
        P(),
        P(),
        P(),
        P(),
        P(("cfg", "seq"), None),
        P(),
        P(),
        P(),
        P(),
        P(),
        P(None, ("cfg", "seq")),
    )
    return jax.shard_map(
        per_device,
        mesh=mesh,
        in_specs=placed,
        out_specs=(P("seq", None), P("seq", "cfg", None), P("seq", "cfg", None, None)),
        check_vma=False,
    )
```

time: 223 us -> 109 us (0.49)
  matrix products: 72 us -> 0 us
  waiting for transfers between devices: 70.1 us -> 37.1 us
  Pallas kernels: 0 us -> 27.8 us
  other arithmetic: 28.7 us -> 1.06 us
  starting transfers between devices: 5.86 us -> 27.9 us
  between operations: 16 us -> 2.84 us
  local copies, waits for them, and re-layouts: 22.7 us -> 11.5 us
  loops' own time: 5.37 us -> 0 us
    dot_general x43 -> x0, matrix products: 72 us -> none  [the longest x8 13.1 us: one_head(): lax.dot_general(query_part, key_part, dims, preferred_element_type=jnp.fl...]
    all_gather x2 -> x0, waiting for transfers between devices: 66 us -> none  [the longest x1 66 us: per_device(): lax.all_gather(project_weight, ('cfg', 'seq'), axis=0, tiled=True)]
    ppermute x3 -> x20, waiting for transfers between devices: 3.4 us -> 37.1 us  [the longest x18 37.1 us: swap(): lax.ppermute(value, ('cfg', 'seq'), [(i, i ^ flip) for i in range(size)])]
    pallas_call x0 -> x6, Pallas kernels: none -> 27.8 us  [the longest x1 11.3 us: per_device(): pl.pallas_call(functools.partial(attend_kernel, rows, 4 * cells), grid=(H...]
    ppermute x3 -> x20, starting transfers between devices: 5.78 us -> 27.9 us  [the longest x18 25.4 us: swap(): lax.ppermute(value, ('cfg', 'seq'), [(i, i ^ flip) for i in range(size)])]
    dot_general x2 -> x0, local copies, waits for them, and re-layouts: 11.2 us -> none  [per_device(): jnp.dot(key_normed, weight_piece[:, inner:2 * inner], preferred_element_t...]
    convert_element_type x5 -> x4, other arithmetic: 8.02 us -> 0.87 us  [the longest x1 0.74 us: per_device(): others = swap(total.astype(bf16), across)]
    reduce_sum x10 -> x0, other arithmetic: 6.95 us -> none  [the longest x6 3.12 us: layer_norm(): jnp.mean(centred * centred, -1, keepdims=True) + epsilon]
  transfers between devices with their start and end apart: 5 -> 20, of which waited for: 2 -> 4; matrix products, arithmetic and copies ran while one was open for 54% -> 9% of each run, Pallas kernels for 0% -> 20%
where the time goes in v1:
time: 109 us; the launch traced here: 108 us
  waiting for transfers between devices  37.1 us (34%)
  starting transfers between devices  27.9 us (26%)
  Pallas kernels  27.8 us (26%)
  local copies, waits for them, and re-layouts  11.5 us (11%)
  between operations  2.84 us (3%)
    ppermute x18, waiting for transfers between devices, swap(): lax.ppermute(value, ('cfg', 'seq'), [(i, i ^ flip) for i in range(size)])  37.1 us
    ppermute x18, starting transfers between devices, swap(): lax.ppermute(value, ('cfg', 'seq'), [(i, i ^ flip) for i in range(size)])  25.4 us
    pallas_call x1, Pallas kernels, per_device(): pl.pallas_call(functools.partial(attend_kernel, rows, 4 * cells), grid=(H...  11.3 us
    pallas_call x1, Pallas kernels, per_device(): pl.pallas_call(functools.partial(output_kernel, orders), out_shape=jax.Sh...  6.08 us
    pallas_call x1, Pallas kernels, per_device(): pl.pallas_call(functools.partial(fine_kernel, cells), out_shape=(jax.Shap...  4.24 us
    unnamed x37, local copies, waits for them, and re-layouts  3.85 us
    pallas_call x1, Pallas kernels, per_device(): pl.pallas_call(velocity_kernel, out_shape=jax.ShapeDtypeStruct((channels,...  2.49 us
    pallas_call x1, Pallas kernels, per_device(): pl.pallas_call(functools.partial(partial_kernel, seq_count), out_shape=(j...  2.28 us
  transfers between devices with their start and end apart: 20, of which 4 were waited for; matrix products, arithmetic and copies ran while one was open for 9% of the time, Pallas kernels for 20%

profile of v1, /device:TPU:0, one launch (start us, length us, event | category | flops | bytes accessed | tf_op | source)
XLA Modules:
  0.0 108.4 jit_solution(651596815946822847)
XLA Ops:
  0.6 0.9 slice_bitcast_fusion
  1.5 3.1 %collective-permute-start.14 = (bf16[1,32,1024]{2,1,0:T(8,128)(2,1)S(1)}, bf16[1,32,1024]{2,1,0:T(8,128)(2,1)S(1)}, u32[]{:S(2)}, u32[]{:S(2)}) collective-permute-start(bf16[1,32,1024]{2,1,0:T(8,128)(2,1)S(1)} %get-tuple-element.33), channel_id=1, source_target_pairs={{0,4},{1,5},{2,6},{3,7},{4,0},{5,1},{6,2},{7,3},{8,12},{9,13},{10,... | collective-permute-start | bytes 196616 | tf_op jit(solution)/shard_map/ppermute | solution.py:405
  4.6 1.5 %collective-permute-start.10 = (bf16[1,32,1024]{2,1,0:T(8,128)(2,1)S(1)}, bf16[1,32,1024]{2,1,0:T(8,128)(2,1)S(1)}, u32[]{:S(2)}, u32[]{:S(2)}) collective-permute-start(bf16[1,32,1024]{2,1,0:T(8,128)(2,1)S(1)} %get-tuple-element.34), channel_id=1, source_target_pairs={{0,16},{1,17},{2,18},{3,19},{4,20},{5,21},{6,22},{7,23},{8,24},{9,... | collective-permute-start | bytes 196616 | tf_op jit(solution)/shard_map/ppermute | solution.py:405
  6.1 2.3 %partial_mix.1 = (f32[40,1536]{1,0:T(8,128)}, bf16[40,1536]{1,0:T(8,128)(2,1)}) custom-call(bf16[32,2048]{1,0:T(8,128)(2,1)} %embed_ref.5, f32[1,2048]{1,0:T(1,128)} %bitcast.31, f32[3,2048]{1,0:T(4,128)} %mod_ref.1, bf16[64,3072]{1,0:T(8,128)(2,1)} %weight_ref.2), custom_call_target="tpu_custom_call" | custom-call | flops 37748736 | bytes 1000000 | tf_op jit(solution)/shard_map/partial_mix/pallas_call | solution.py:411
  8.4 1.0 copy.27.weight_ref
  9.4 2.5 %velocity.1.own_ref = f32[32,128]{1,0:T(8,128)} custom-call(bf16[128,2048]{1,0:T(8,128)(2,1)} %bitcast.23, f32[2,2048]{1,0:T(2,128)} %bitcast.28, bf16[2048,32]{1,0:T(8,128)(2,1)} %copy.27.weight_ref), custom_call_target="tpu_custom_call" | custom-call | flops 67108864 | bytes 1000000 | tf_op jit(solution)/shard_map/velocity/pallas_call | solution.py:423
  12.5 1.4 %slice.9.gate_ref = f32[1,2048]{1,0:T(1,128)} slice(f32[3,2048]{1,0:T(4,128)} %mod_ref.1), slice={[2:3], [0:2048]} | slice | bytes 16384 | tf_op jit(solution)/shard_map/slice | solution.py:529
  17.3 0.7 copy.33.key_gain_ref
  18.1 0.8 copy.30.taps_ref
  19.5 1.5 %guide.1 = (f32[32,128]{1,0:T(8,128)}, f32[32,128]{1,0:T(8,128)}) custom-call(s32[1]{0:T(128)S(6)} %copy.44.step_ref, s32[1]{0:T(128)S(6)} %copy.45.slot_ref, f32[32,128]{1,0:T(8,128)} %bitcast.30, f32[32,128]{1,0:T(8,128)} %velocity.1.own_ref, f32[32,128]{1,0:T(8,128)} %copy-done.5, f32[32,128]{1,0:T(8,128)} %bitcast.26), custom_call_target="tpu_custom_call" | custom-call | flops 1000000 | bytes 100000 | tf_op jit(solution)/shard_map/guide/pallas_call | solution.py:458
  20.9 1.3 %collective-permute-start.2 = (f32[32,128]{1,0:T(8,128)}, f32[32,128]{1,0:T(8,128)S(1)}, u32[]{:S(2)}, u32[]{:S(2)}) collective-permute-start(f32[32,128]{1,0:T(8,128)} %get-tuple-element.14.own_ref), channel_id=1, source_target_pairs={{1,0},{2,1},{3,2},{4,3},{5,4},{6,5},{7,6},{8,7},{9,8},{10,9},{11,1... | collective-permute-start | bytes 49160 | tf_op jit(solution)/shard_map/ppermute | solution.py:470
  22.2 0.8 copy.29
  23.8 3.4 %collective-permute-start.15 = (bf16[2,32,1024]{2,1,0:T(8,128)(2,1)S(1)}, bf16[2,32,1024]{2,1,0:T(8,128)(2,1)S(1)}, u32[]{:S(2)}, u32[]{:S(2)}) collective-permute-start(bf16[2,32,1024]{2,1,0:T(8,128)(2,1)S(1)} %pad_maximum_fusion.5), channel_id=1, source_target_pairs={{0,8},{1,9},{2,10},{3,11},{4,12},{5,13},{6,14},{7,15},{8,0},{9,1},... | collective-permute-start | bytes 393224 | tf_op jit(solution)/shard_map/ppermute | solution.py:405
  27.2 1.8 %collective-permute-start.11 = (bf16[2,32,1024]{2,1,0:T(8,128)(2,1)S(1)}, bf16[2,32,1024]{2,1,0:T(8,128)(2,1)S(1)}, u32[]{:S(2)}, u32[]{:S(2)}) collective-permute-start(bf16[2,32,1024]{2,1,0:T(8,128)(2,1)S(1)} %pad_maximum_fusion.4), channel_id=1, source_target_pairs={{0,2},{1,3},{2,0},{3,1},{4,6},{5,7},{6,4},{7,5},{8,10},{9,11},{10,... | collective-permute-start | bytes 393224 | tf_op jit(solution)/shard_map/ppermute | solution.py:405
  29.1 1.3 %collective-permute-start.6 = (bf16[40,1536]{1,0:T(8,128)(2,1)S(1)}, bf16[40,1536]{1,0:T(8,128)(2,1)S(1)}, u32[]{:S(2)}, u32[]{:S(2)}) collective-permute-start(bf16[40,1536]{1,0:T(8,128)(2,1)S(1)} %fusion), channel_id=1, source_target_pairs={{0,18},{1,19},{2,16},{3,17},{4,22},{5,23},{6,20},{7,21},{8,26},{9,... | collective-permute-start | bytes 368648 | tf_op jit(solution)/shard_map/ppermute | solution.py:405
  30.3 1.7 %collective-permute-start.5 = (bf16[40,1536]{1,0:T(8,128)(2,1)S(1)}, bf16[40,1536]{1,0:T(8,128)(2,1)S(1)}, u32[]{:S(2)}, u32[]{:S(2)}) collective-permute-start(bf16[40,1536]{1,0:T(8,128)(2,1)S(1)} %fusion), channel_id=1, source_target_pairs={{0,2},{1,3},{2,0},{3,1},{4,6},{5,7},{6,4},{7,5},{8,10},{9,11},{10,... | collective-permute-start | bytes 368648 | tf_op jit(solution)/shard_map/ppermute | solution.py:405
  32.1 3.7 %collective-permute-done.11 = bf16[2,32,1024]{2,1,0:T(8,128)(2,1)S(1)} collective-permute-done((bf16[2,32,1024]{2,1,0:T(8,128)(2,1)S(1)}, bf16[2,32,1024]{2,1,0:T(8,128)(2,1)S(1)}, u32[]{:S(2)}, u32[]{:S(2)}) %collective-permute-start.11) | collective-permute-done | bytes 131104 | tf_op jit(solution)/shard_map/ppermute | solution.py:405
  35.8 1.9 %collective-permute-start.4 = (bf16[40,1536]{1,0:T(8,128)(2,1)S(1)}, bf16[40,1536]{1,0:T(8,128)(2,1)S(1)}, u32[]{:S(2)}, u32[]{:S(2)}) collective-permute-start(bf16[40,1536]{1,0:T(8,128)(2,1)S(1)} %fusion), channel_id=1, source_target_pairs={{0,16},{1,17},{2,18},{3,19},{4,20},{5,21},{6,22},{7,23},{8,24},{9,... | collective-permute-start | bytes 368648 | tf_op jit(solution)/shard_map/ppermute | solution.py:405
  37.8 1.3 %collective-permute-start.1 = (f32[32,128]{1,0:T(8,128)S(1)}, f32[32,128]{1,0:T(8,128)S(1)}, u32[]{:S(2)}, u32[]{:S(2)}) collective-permute-start(f32[32,128]{1,0:T(8,128)S(1)} %copy-done.11), channel_id=1, source_target_pairs={{0,1},{1,2},{2,3},{3,4},{4,5},{5,6},{6,7},{7,8},{8,9},{9,10},{10,1... | collective-permute-start | bytes 49160 | tf_op jit(solution)/shard_map/ppermute | solution.py:469
  39.3 2.8 %collective-permute-start.12 = (bf16[4,32,1024]{2,1,0:T(8,128)(2,1)S(1)}, bf16[4,32,1024]{2,1,0:T(8,128)(2,1)S(1)}, u32[]{:S(2)}, u32[]{:S(2)}) collective-permute-start(bf16[4,32,1024]{2,1,0:T(8,128)(2,1)S(1)} %pad_maximum_fusion.2), channel_id=1, source_target_pairs={{0,4},{1,5},{2,6},{3,7},{4,0},{5,1},{6,2},{7,3},{8,12},{9,13},{10,... | collective-permute-start | bytes 786440 | tf_op jit(solution)/shard_map/ppermute | solution.py:405
  42.2 0.8 collective-permute-start.7
  43.1 8.0 %collective-permute-done.7 = bf16[40,1536]{1,0:T(8,128)(2,1)S(1)} collective-permute-done((bf16[40,1536]{1,0:T(8,128)(2,1)S(1)}, bf16[40,1536]{1,0:T(8,128)(2,1)S(1)}, u32[]{:S(2)}, u32[]{:S(2)}) %collective-permute-start.7) | collective-permute-done | bytes 122912 | tf_op jit(solution)/shard_map/ppermute | solution.py:405
  51.7 2.2 %collective-permute-start.17 = (bf16[8,32,1024]{2,1,0:T(8,128)(2,1)S(1)}, bf16[8,32,1024]{2,1,0:T(8,128)(2,1)S(1)}, u32[]{:S(2)}, u32[]{:S(2)}) collective-permute-start(bf16[8,32,1024]{2,1,0:T(8,128)(2,1)S(1)} %pad_maximum_fusion.1), channel_id=1, source_target_pairs={{0,2},{1,3},{2,0},{3,1},{4,6},{5,7},{6,4},{7,5},{8,10},{9,11},{10,... | collective-permute-start | bytes 1572872 | tf_op jit(solution)/shard_map/ppermute | solution.py:405
  54.0 2.8 %collective-permute-start.13 = (bf16[8,32,1024]{2,1,0:T(8,128)(2,1)S(1)}, bf16[8,32,1024]{2,1,0:T(8,128)(2,1)S(1)}, u32[]{:S(2)}, u32[]{:S(2)}) collective-permute-start(bf16[8,32,1024]{2,1,0:T(8,128)(2,1)S(1)} %pad_maximum_fusion), channel_id=1, source_target_pairs={{0,8},{1,9},{2,10},{3,11},{4,12},{5,13},{6,14},{7,15},{8,0},{9,1},... | collective-permute-start | bytes 1572872 | tf_op jit(solution)/shard_map/ppermute | solution.py:405
  56.9 14.9 %collective-permute-done.8 = bf16[40,1536]{1,0:T(8,128)(2,1)S(1)} collective-permute-done((bf16[40,1536]{1,0:T(8,128)(2,1)S(1)}, bf16[40,1536]{1,0:T(8,128)(2,1)S(1)}, u32[]{:S(2)}, u32[]{:S(2)}) %collective-permute-start.8) | collective-permute-done | bytes 122912 | tf_op jit(solution)/shard_map/ppermute | solution.py:405
  71.8 0.7 fusion.2
  72.6 10.4 %collective-permute-done.13 = bf16[8,32,1024]{2,1,0:T(8,128)(2,1)S(1)} collective-permute-done((bf16[8,32,1024]{2,1,0:T(8,128)(2,1)S(1)}, bf16[8,32,1024]{2,1,0:T(8,128)(2,1)S(1)}, u32[]{:S(2)}, u32[]{:S(2)}) %collective-permute-start.13) | collective-permute-done | bytes 524320 | tf_op jit(solution)/shard_map/ppermute | solution.py:405
  84.4 4.2 %fine_features.1 = (f32[2,32,128]{2,1,0:T(8,128)}, bf16[1024,256]{1,0:T(8,128)(2,1)}, bf16[256,1024]{1,0:T(8,128)(2,1)}, bf16[256,256]{1,0:T(8,128)(2,1)}, bf16[...) custom-call(f32[32,128]{1,0:T(8,128)} %copy-done.13, f32[32,128]{1,0:T(8,128)} %get-tuple-element.14.own_ref, ...), custom_call_target="tpu_custom_call" | custom-call | flops 4000000000 | bytes 4000000 | tf_op jit(solution)/shard_map/fine_features/pallas_call | solution.py:472
  88.7 0.9 copy.32
  89.6 0.8 reshape.50
  91.0 11.3 %attend.1.attended_ref = bf16[256,1024]{1,0:T(8,128)(2,1)} custom-call(s32[1]{0:T(128)S(6)} %copy.46.length_ref, f32[40,1536]{1,0:T(8,128)} %get-tuple-element.30.kept_ref, bf16[40,1536]{1,0:T(8,128)(2,1)} %copy-done.10, bf16[1024,256]{1,0:T(8,128)(2,1)} %get-tuple-element.18.keys_ref, bf16[256,1024]{1,0:T(8,128)(2,1)} %get-tuple-element.19.keys_t_ref, ...), custom_call_target="tpu_custom_call" | custom-call | flops 8000000000 | bytes 4000000 | tf_op jit(solution)/shard_map/attend/pallas_call | solution.py:500
  102.3 6.1 %output.1 = bf16[256,2048]{1,0:T(8,128)(2,1)} custom-call(bf16[256,1024]{1,0:T(8,128)(2,1)} %attend.1.attended_ref, bf16[32,256]{1,0:T(8,128)(2,1)} %get-tuple-element.22.token_ref, bf16[32,2048]{1,0:T(8,128)(2,1)} %embed_ref.5, f32[1,2048]{1,0:T(1,128)} %bitcast.33, f32[1,2048]{1,0:T(1,128)} %slice.9.gate_ref, bf16[16,32,1024]{2,1,0:T(8,128)(2,1)} %copy-done.6, ...), custom_call_target="tpu_custom_call" | custom-call | flops 2000000000 | bytes 6000000 | tf_op jit(solution)/shard_map/output/pallas_call | solution.py:531
  (73 shorter events, 6.6 us)
Async XLA Ops:
  1.5 22.2 %collective-permute-start.14 = (bf16[1,32,1024]{2,1,0:T(8,128)(2,1)S(1)}, bf16[1,32,1024]{2,1,0:T(8,128)(2,1)S(1)}, u32[]{:S(2)}, u32[]{:S(2)}) collective-permute-start(bf16[1,32,1024]{2,1,0:T(8,128)(2,1)S(1)} %get-tuple-element.33), channel_id=1, source_target_pairs={{0,4},{1,5},{2,6},{3,7},{4,0},{5,1},{6,2},{7,3},{8,12},{9,13},{10,... | collective-permute-start | bytes 196616 | tf_op jit(solution)/shard_map/ppermute | solution.py:405
  4.6 22.5 %collective-permute-start.10 = (bf16[1,32,1024]{2,1,0:T(8,128)(2,1)S(1)}, bf16[1,32,1024]{2,1,0:T(8,128)(2,1)S(1)}, u32[]{:S(2)}, u32[]{:S(2)}) collective-permute-start(bf16[1,32,1024]{2,1,0:T(8,128)(2,1)S(1)} %get-tuple-element.34), channel_id=1, source_target_pairs={{0,16},{1,17},{2,18},{3,19},{4,20},{5,21},{6,22},{7,23},{8,24},{9,... | collective-permute-start | bytes 196616 | tf_op jit(solution)/shard_map/ppermute | solution.py:405
  6.1 2.3 %copy-start.2 = (bf16[2048,32]{0,1:T(8,128)(2,1)S(1)}, bf16[2048,32]{0,1:T(8,128)(2,1)}, u32[]{:S(2)}) copy-start(bf16[2048,32]{0,1:T(8,128)(2,1)} %param.21) | copy-start | bytes 393220
  8.4 20.6 %collective-permute-start.3 = (bf16[40,1536]{1,0:T(8,128)(2,1)}, bf16[40,1536]{1,0:T(8,128)(2,1)S(1)}, u32[]{:S(2)}, u32[]{:S(2)}) collective-permute-start(bf16[40,1536]{1,0:T(8,128)(2,1)} %get-tuple-element.17), channel_id=1, source_target_pairs={{0,1},{1,0},{2,3},{3,2},{4,5},{5,4},{6,7},{7,6},{8,9},{9,8},{10,11... | collective-permute-start | bytes 368648 | tf_op jit(solution)/shard_map/ppermute | solution.py:405
  9.4 3.0 %copy-start.1 = (bf16[1024,64]{0,1:T(8,128)(2,1)S(1)}, bf16[1024,64]{0,1:T(8,128)(2,1)}, u32[]{:S(2)}) copy-start(bf16[1024,64]{0,1:T(8,128)(2,1)} %param.37) | copy-start | bytes 393220
  11.9 6.9 %collective-permute-start = (f32[32,128]{1,0:T(8,128)}, f32[32,128]{1,0:T(8,128)S(1)}, u32[]{:S(2)}, u32[]{:S(2)}) collective-permute-start(f32[32,128]{1,0:T(8,128)} %velocity.1.own_ref), channel_id=1, source_target_pairs={{0,16},{1,17},{2,18},{3,19},{4,20},{5,21},{6,22},{7,23},{8,24},{9,... | collective-permute-start | bytes 49160 | tf_op jit(solution)/shard_map/ppermute | solution.py:405
  12.4 3.3 %copy-start.9 = (f32[32]{0:T(128)S(1)}, f32[32]{0:T(128)}, u32[]{:S(2)}) copy-start(f32[32]{0:T(128)} %param.27) | copy-start | bytes 388
  13.8 2.7 %copy-start.4 = (f32[2,2048]{1,0:T(2,128)S(1)}, f32[2,2048]{1,0:T(2,128)}, u32[]{:S(2)}) copy-start(f32[2,2048]{1,0:T(2,128)} %param.22) | copy-start | bytes 49156
  16.6 0.7 copy-start.8
  17.3 0.8 copy-start.3
  20.9 62.8 %collective-permute-start.2 = (f32[32,128]{1,0:T(8,128)}, f32[32,128]{1,0:T(8,128)S(1)}, u32[]{:S(2)}, u32[]{:S(2)}) collective-permute-start(f32[32,128]{1,0:T(8,128)} %get-tuple-element.14.own_ref), channel_id=1, source_target_pairs={{1,0},{2,1},{3,2},{4,3},{5,4},{6,5},{7,6},{8,7},{9,8},{10,9},{11,1... | collective-permute-start | bytes 49160 | tf_op jit(solution)/shard_map/ppermute | solution.py:470
  23.8 5.3 %copy-start = (f32[40,1536]{1,0:T(8,128)S(1)}, f32[40,1536]{1,0:T(8,128)}, u32[]{:S(2)}) copy-start(f32[40,1536]{1,0:T(8,128)} %get-tuple-element.16) | copy-start | bytes 737284
  23.8 14.0 %collective-permute-start.15 = (bf16[2,32,1024]{2,1,0:T(8,128)(2,1)S(1)}, bf16[2,32,1024]{2,1,0:T(8,128)(2,1)S(1)}, u32[]{:S(2)}, u32[]{:S(2)}) collective-permute-start(bf16[2,32,1024]{2,1,0:T(8,128)(2,1)S(1)} %pad_maximum_fusion.5), channel_id=1, source_target_pairs={{0,8},{1,9},{2,10},{3,11},{4,12},{5,13},{6,14},{7,15},{8,0},{9,1},... | collective-permute-start | bytes 393224 | tf_op jit(solution)/shard_map/ppermute | solution.py:405
  27.2 8.6 %collective-permute-start.11 = (bf16[2,32,1024]{2,1,0:T(8,128)(2,1)S(1)}, bf16[2,32,1024]{2,1,0:T(8,128)(2,1)S(1)}, u32[]{:S(2)}, u32[]{:S(2)}) collective-permute-start(bf16[2,32,1024]{2,1,0:T(8,128)(2,1)S(1)} %pad_maximum_fusion.4), channel_id=1, source_target_pairs={{0,2},{1,3},{2,0},{3,1},{4,6},{5,7},{6,4},{7,5},{8,10},{9,11},{10,... | collective-permute-start | bytes 393224 | tf_op jit(solution)/shard_map/ppermute | solution.py:405
  29.0 8.7 %copy-start.11 = (f32[32,128]{1,0:T(8,128)S(1)}, f32[32,128]{1,0:T(8,128)}, u32[]{:S(2)}) copy-start(f32[32,128]{1,0:T(8,128)} %get-tuple-element.14.own_ref) | copy-start | bytes 49156
  29.1 10.1 %collective-permute-start.6 = (bf16[40,1536]{1,0:T(8,128)(2,1)S(1)}, bf16[40,1536]{1,0:T(8,128)(2,1)S(1)}, u32[]{:S(2)}, u32[]{:S(2)}) collective-permute-start(bf16[40,1536]{1,0:T(8,128)(2,1)S(1)} %fusion), channel_id=1, source_target_pairs={{0,18},{1,19},{2,16},{3,17},{4,22},{5,23},{6,20},{7,21},{8,26},{9,... | collective-permute-start | bytes 368648 | tf_op jit(solution)/shard_map/ppermute | solution.py:405
  30.3 9.0 %collective-permute-start.5 = (bf16[40,1536]{1,0:T(8,128)(2,1)S(1)}, bf16[40,1536]{1,0:T(8,128)(2,1)S(1)}, u32[]{:S(2)}, u32[]{:S(2)}) collective-permute-start(bf16[40,1536]{1,0:T(8,128)(2,1)S(1)} %fusion), channel_id=1, source_target_pairs={{0,2},{1,3},{2,0},{3,1},{4,6},{5,7},{6,4},{7,5},{8,10},{9,11},{10,... | collective-permute-start | bytes 368648 | tf_op jit(solution)/shard_map/ppermute | solution.py:405
  35.8 6.3 %collective-permute-start.4 = (bf16[40,1536]{1,0:T(8,128)(2,1)S(1)}, bf16[40,1536]{1,0:T(8,128)(2,1)S(1)}, u32[]{:S(2)}, u32[]{:S(2)}) collective-permute-start(bf16[40,1536]{1,0:T(8,128)(2,1)S(1)} %fusion), channel_id=1, source_target_pairs={{0,16},{1,17},{2,18},{3,19},{4,20},{5,21},{6,22},{7,23},{8,24},{9,... | collective-permute-start | bytes 368648 | tf_op jit(solution)/shard_map/ppermute | solution.py:405
  37.8 46.0 %collective-permute-start.1 = (f32[32,128]{1,0:T(8,128)S(1)}, f32[32,128]{1,0:T(8,128)S(1)}, u32[]{:S(2)}, u32[]{:S(2)}) collective-permute-start(f32[32,128]{1,0:T(8,128)S(1)} %copy-done.11), channel_id=1, source_target_pairs={{0,1},{1,2},{2,3},{3,4},{4,5},{5,6},{6,7},{7,8},{8,9},{9,10},{10,1... | collective-permute-start | bytes 49160 | tf_op jit(solution)/shard_map/ppermute | solution.py:469
  39.1 12.5 %collective-permute-start.16 = (bf16[4,32,1024]{2,1,0:T(8,128)(2,1)S(1)}, bf16[4,32,1024]{2,1,0:T(8,128)(2,1)S(1)}, u32[]{:S(2)}, u32[]{:S(2)}) collective-permute-start(bf16[4,32,1024]{2,1,0:T(8,128)(2,1)S(1)} %pad_maximum_fusion.3), channel_id=1, source_target_pairs={{0,16},{1,17},{2,18},{3,19},{4,20},{5,21},{6,22},{7,23},{8,24},{9,... | collective-permute-start | bytes 786440 | tf_op jit(solution)/shard_map/ppermute | solution.py:405
  39.3 14.6 %collective-permute-start.12 = (bf16[4,32,1024]{2,1,0:T(8,128)(2,1)S(1)}, bf16[4,32,1024]{2,1,0:T(8,128)(2,1)S(1)}, u32[]{:S(2)}, u32[]{:S(2)}) collective-permute-start(bf16[4,32,1024]{2,1,0:T(8,128)(2,1)S(1)} %pad_maximum_fusion.2), channel_id=1, source_target_pairs={{0,4},{1,5},{2,6},{3,7},{4,0},{5,1},{6,2},{7,3},{8,12},{9,13},{10,... | collective-permute-start | bytes 786440 | tf_op jit(solution)/shard_map/ppermute | solution.py:405
  42.2 8.9 %collective-permute-start.7 = (bf16[40,1536]{1,0:T(8,128)(2,1)S(1)}, bf16[40,1536]{1,0:T(8,128)(2,1)S(1)}, u32[]{:S(2)}, u32[]{:S(2)}) collective-permute-start(bf16[40,1536]{1,0:T(8,128)(2,1)S(1)} %get-tuple-element.31), channel_id=1, source_target_pairs={{0,4},{1,5},{2,6},{3,7},{4,0},{5,1},{6,2},{7,3},{8,12},{9,13},{10,... | collective-permute-start | bytes 368648 | tf_op jit(solution)/shard_map/ppermute | solution.py:405
  51.1 20.7 %collective-permute-start.8 = (bf16[40,1536]{1,0:T(8,128)(2,1)S(1)}, bf16[40,1536]{1,0:T(8,128)(2,1)S(1)}, u32[]{:S(2)}, u32[]{:S(2)}) collective-permute-start(bf16[40,1536]{1,0:T(8,128)(2,1)S(1)} %fusion.1), channel_id=1, source_target_pairs={{0,8},{1,9},{2,10},{3,11},{4,12},{5,13},{6,14},{7,15},{8,0},{9,1},... | collective-permute-start | bytes 368648 | tf_op jit(solution)/shard_map/ppermute | solution.py:405
  51.7 31.5 %collective-permute-start.17 = (bf16[8,32,1024]{2,1,0:T(8,128)(2,1)S(1)}, bf16[8,32,1024]{2,1,0:T(8,128)(2,1)S(1)}, u32[]{:S(2)}, u32[]{:S(2)}) collective-permute-start(bf16[8,32,1024]{2,1,0:T(8,128)(2,1)S(1)} %pad_maximum_fusion.1), channel_id=1, source_target_pairs={{0,2},{1,3},{2,0},{3,1},{4,6},{5,7},{6,4},{7,5},{8,10},{9,11},{10,... | collective-permute-start | bytes 1572872 | tf_op jit(solution)/shard_map/ppermute | solution.py:405
  54.0 29.0 %collective-permute-start.13 = (bf16[8,32,1024]{2,1,0:T(8,128)(2,1)S(1)}, bf16[8,32,1024]{2,1,0:T(8,128)(2,1)S(1)}, u32[]{:S(2)}, u32[]{:S(2)}) collective-permute-start(bf16[8,32,1024]{2,1,0:T(8,128)(2,1)S(1)} %pad_maximum_fusion), channel_id=1, source_target_pairs={{0,8},{1,9},{2,10},{3,11},{4,12},{5,13},{6,14},{7,15},{8,0},{9,1},... | collective-permute-start | bytes 1572872 | tf_op jit(solution)/shard_map/ppermute | solution.py:405
  72.5 17.8 %collective-permute-start.9 = (bf16[40,1536]{1,0:T(8,128)(2,1)S(1)}, bf16[40,1536]{1,0:T(8,128)(2,1)S(1)}, u32[]{:S(2)}, u32[]{:S(2)}) collective-permute-start(bf16[40,1536]{1,0:T(8,128)(2,1)S(1)} %get-tuple-element.29), channel_id=1, source_target_pairs={{0,1},{1,0},{2,3},{3,2},{4,5},{5,4},{6,7},{7,6},{8,9},{9,8},{10,11... | collective-permute-start | bytes 368648 | tf_op jit(solution)/shard_map/ppermute | solution.py:405
  83.1 5.6 %copy-start.6 = (bf16[16,32,1024]{2,1,0:T(8,128)(2,1)}, bf16[16,32,1024]{2,1,0:T(8,128)(2,1)S(1)}, u32[]{:S(2)}) copy-start(bf16[16,32,1024]{2,1,0:T(8,128)(2,1)S(1)} %constant_dynamic-update-slice_fusion.own_a_ref) | copy-start | bytes 3145732
  83.1 19.2 %collective-permute-start.18 = (bf16[16,32,1024]{2,1,0:T(8,128)(2,1)S(1)}, bf16[16,32,1024]{2,1,0:T(8,128)(2,1)}, u32[]{:S(2)}, u32[]{:S(2)}) collective-permute-start(bf16[16,32,1024]{2,1,0:T(8,128)(2,1)S(1)} %constant_dynamic-update-slice_fusion.own_a_ref), channel_id=1, source_target_pairs={{0,1},{1,0},{2,3},{3,2},{4,5},{5,4},{6,7},{7,6},{8,9},{9,8},{10,11... | collective-permute-start | bytes 3145736 | tf_op jit(solution)/shard_map/ppermute | solution.py:405
  83.3 5.4 %copy-start.7 = (bf16[16,32,1024]{2,1,0:T(8,128)(2,1)}, bf16[16,32,1024]{2,1,0:T(8,128)(2,1)S(1)}, u32[]{:S(2)}) copy-start(bf16[16,32,1024]{2,1,0:T(8,128)(2,1)S(1)} %constant_dynamic-update-slice_fusion.5.own_b_ref) | copy-start | bytes 3145732
  83.3 19.0 %collective-permute-start.19 = (bf16[16,32,1024]{2,1,0:T(8,128)(2,1)S(1)}, bf16[16,32,1024]{2,1,0:T(8,128)(2,1)}, u32[]{:S(2)}, u32[]{:S(2)}) collective-permute-start(bf16[16,32,1024]{2,1,0:T(8,128)(2,1)S(1)} %constant_dynamic-update-slice_fusion.5.own_b_ref), channel_id=1, source_target_pairs={{0,1},{1,0},{2,3},{3,2},{4,5},{5,4},{6,7},{7,6},{8,9},{9,8},{10,11... | collective-permute-start | bytes 3145736 | tf_op jit(solution)/shard_map/ppermute | solution.py:405
  83.8 0.6 copy-start.13
  90.3 0.6 copy-start.10
  (2 other events, 1.2 us)

commit v2 on v1

v2 whole, which is shorter than its diff:
```python
import functools

import jax
import jax.numpy as jnp
from jax import lax
from jax.experimental import pallas as pl
from jax.experimental.pallas import tpu as pltpu
from jax.sharding import PartitionSpec as P

STEPS = 50

epsilon = 1e-06
flow_shift = 5.0
highest = lax.Precision.HIGHEST
f32 = jnp.float32
bf16 = jnp.bfloat16
LOG2E = 1.4426950408889634
TERMS = 40
SLAB = 48
DEPTH = 256


def vmem(count):
    return [pl.BlockSpec(memory_space=pltpu.VMEM) for _ in range(count)]


def cost(flops, moved):
    return pl.CostEstimate(flops=int(flops), bytes_accessed=int(moved), transcendentals=0)


def dot_rows(left, right):
    return lax.dot_general(left, right, (((0,), (0,)), ((), ())), preferred_element_type=f32)


def anywhere(count):
    return [pl.BlockSpec(memory_space=pl.ANY) for _ in range(count)]


def fetch(pairs, sems):
    copies = [pltpu.make_async_copy(src, dst, sems.at[i]) for i, (src, dst) in enumerate(pairs)]
    for copy in copies:
        copy.start()
    for copy in copies:
        copy.wait()


def exact(left, right, contract):
    return lax.dot_general(
        left, right, ((contract[:1], contract[1:]), ((), ())), precision=highest,
        preferred_element_type=f32,
    )


def lane_repeat(channels):
    lane = lax.broadcasted_iota(jnp.int32, (channels, 128), 1)
    row = lax.broadcasted_iota(jnp.int32, (channels, 128), 0)
    return jnp.where(lane % channels == row, 1.0, 0.0)


def split(values):
    high = values.astype(bf16)
    return high, (values - high.astype(f32)).astype(bf16)


def centred_embedding(embed, bias):
    width = embed.shape[1]
    embed = embed - jnp.sum(embed, -1, keepdims=True) * (1.0 / width)
    bias = bias - jnp.sum(bias, -1, keepdims=True) * (1.0 / width)
    return embed, bias


def with_tail(body, first, second):
    row = lax.broadcasted_iota(jnp.int32, (16, body.shape[1]), 0)
    tail = jnp.where(row == 0, first, jnp.where(row == 1, second, 0.0))
    return jnp.concatenate([body, tail], 0)


def partial_kernel(seq_count, embed_ref, bias_ref, mod_ref, weight_ref, keep_ref, send_ref):
    seq_index = lax.axis_index("seq")
    core = seq_index % 2
    depth = weight_ref.shape[0]
    half = keep_ref.shape[1]
    embed = embed_ref[...].astype(f32)
    width = embed.shape[1]
    embed_mean = jnp.sum(embed, -1, keepdims=True) * (1.0 / width)
    bias_mean = jnp.sum(bias_ref[...], -1, keepdims=True) * (1.0 / width)
    start = (lax.axis_index("cfg") * seq_count + seq_index) * depth
    base = pl.multiple_of(start // 128 * 128, 128)
    offset = start - base
    window = pl.ds(base, 128)
    scale = 1.0 + mod_ref[1:2, window]
    rows = with_tail(
        (embed_ref[:, window].astype(f32) - embed_mean) * scale,
        (bias_ref[:, window] - bias_mean) * scale,
        mod_ref[0:1, window],
    )
    rows = pltpu.roll(rows, (128 - offset) % 128, 1)[:, :depth]
    high, low = split(rows)
    left = jnp.concatenate([high, low], 0)

    def part(which):
        columns = pl.ds(pl.multiple_of(which * half, 128), half)
        product = jnp.dot(left, weight_ref[:, columns], preferred_element_type=f32)
        return product[:TERMS] + product[SLAB : SLAB + TERMS]

    send_ref[...] = part(1 - core)
    keep_ref[...] = part(core)


def velocity_kernel(hidden_ref, mod_ref, weight_ref, out_ref):
    values = hidden_ref[...].astype(f32)
    width = values.shape[1]
    centred = values - jnp.sum(values, -1, keepdims=True) * (1.0 / width)
    variance = jnp.sum(centred * centred, -1, keepdims=True) * (1.0 / width)
    normed = centred * lax.rsqrt(variance + epsilon)
    modulated = (normed * (1.0 + mod_ref[1:2, :]) + mod_ref[0:1, :]).astype(bf16)
    out_ref[...] = lax.dot_general(
        weight_ref[...], modulated, (((1,), (1,)), ((), ())), preferred_element_type=f32
    )


def guide_kernel(
    rows, step_ref, slot_ref, table_ref, latent_ref, own_any, other_any, guided_ref, next_ref,
    own_ref, other_ref, sems,
):
    fetch([(own_any, own_ref), (other_any, other_ref)], sems)
    branch = lax.axis_index("cfg")
    own = own_ref[...]
    other = other_ref[...]
    channels, count = own.shape
    group = 128 // channels
    cells = count // rows
    line = lax.broadcasted_iota(jnp.int32, (count // group, count), 0)
    column = lax.broadcasted_iota(jnp.int32, (count // group, count), 1)
    belongs = jnp.where(line == column % cells // group * rows + column // cells, 1.0, 0.0)
    lane = lax.broadcasted_iota(jnp.int32, (count, 128), 1)
    cell = lax.broadcasted_iota(jnp.int32, (count, 128), 0)
    slot = lane // channels == cell % group
    repeat = lane_repeat(channels)
    spread = jnp.where(slot, exact(belongs, latent_ref[...], (0, 0)), 0.0)
    latent = exact(repeat, spread, (1, 1))
    first = branch == 0
    conditional = jnp.where(first, own, other)
    unconditional = jnp.where(first, other, own)
    table = table_ref[...]
    slots = lax.broadcasted_iota(jnp.int32, table.shape, 0) * table.shape[
        1
    ] + lax.broadcasted_iota(jnp.int32, table.shape, 1)
    picked = jnp.where(slots == slot_ref[...], table, 0.0)
    guidance = jnp.sum(jnp.sum(picked, 0, keepdims=True), 1, keepdims=True)
    guided = unconditional + guidance * (conditional - unconditional)

    def sigma(step):
        fraction = 1.0 - step.astype(f32) / STEPS
        return flow_shift * fraction / (1.0 + (flow_shift - 1.0) * fraction)

    change = sigma(step_ref[...] + 1) - sigma(step_ref[...])
    next_ref[...] = latent + change * guided
    guided_ref[...] = exact(belongs, jnp.where(slot, exact(guided, repeat, (0, 0)), 0.0), (1, 0))


def fine_kernel(
    cells,
    taps_ref,
    shift_ref,
    embed_ref,
    bias_ref,
    text_ref,
    gain_ref,
    near_any,
    own_any,
    far_any,
    fine_ref,
    keys_ref,
    keys_t_ref,
    query_ref,
    token_ref,
    text_out_ref,
    near_ref,
    own_ref,
    far_ref,
    sems,
):
    fetch([(near_any, near_ref), (own_any, own_ref), (far_any, far_ref)], sems)
    channels, own_lanes = own_ref.shape
    rows = own_lanes // cells
    lanes = (rows + 2) * cells
    gain = gain_ref[...]
    head = gain.shape[1]
    for h in range(text_ref.shape[1] // head):
        part = text_ref[:, h * head : (h + 1) * head].astype(f32)
        mean = jnp.sum(part * part, -1, keepdims=True) * (1.0 / head)
        text_out_ref[:, h * head : (h + 1) * head] = (
            part * lax.rsqrt(mean + epsilon) * gain
        ).astype(bf16)

    even = lax.axis_index("seq") % 2 == 0
    up = jnp.where(even, far_ref[...], near_ref[...])
    down = jnp.where(even, near_ref[...], far_ref[...])
    extended = jnp.concatenate([up, own_ref[...], down], 1)
    total = extended.shape[1]
    origin = own_lanes - cells
    lane = lax.broadcasted_iota(jnp.int32, (channels, lanes), 1) % cells

    def shifted(down, right):
        start = origin + down * cells + right
        moved = pltpu.roll(extended, (-start) % total, 1)[:, :lanes]
        if right < 0:
            moved = jnp.where(lane == 0, 0.0, moved)
        if right > 0:
            moved = jnp.where(lane == cells - 1, 0.0, moved)
        return moved

    around = {(i, j): shifted(i, j) for i in (-1, 0, 1) for j in (-1, 0, 1)}

    taps = taps_ref[...].T
    same = lax.broadcasted_iota(jnp.int32, (channels, channels), 0) == lax.broadcasted_iota(
        jnp.int32, (channels, channels), 1
    )
    shift = jnp.sum(jnp.where(same, shift_ref[...], 0.0), 1, keepdims=True)

    def tap(r, s):
        first = (3 * r + s) * channels
        return taps[first : first + channels, :]

    blocks = {}
    for a in range(2):
        for c in range(2):
            patches, weights = [], []
            for i in (a - 1, a):
                for j in (c - 1, c):
                    merged = None
                    for r in range(3):
                        for s in range(3):
                            if (a + r - 1) // 2 == i and (c + s - 1) // 2 == j:
                                merged = tap(r, s) if merged is None else merged + tap(r, s)
                    patches.append(around[i, j])
                    weights.append(merged)
            stacked = jnp.concatenate(weights, 0).T
            product = jnp.dot(
                stacked, jnp.concatenate(patches, 0), precision=highest, preferred_element_type=f32
            )
            blocks[a, c] = product + shift + around[0, 0]

    embed, bias = centred_embedding(embed_ref[...].astype(f32), bias_ref[...])
    high, low = split(with_tail(embed, bias, jnp.zeros_like(bias)))
    pair = jnp.concatenate([high, low], 0)
    width = embed.shape[1]
    step = min(width, 512)

    def features(tokens):
        count = tokens.shape[1]
        one = jnp.ones((1, count), f32)
        values = with_tail(tokens.astype(f32), one, jnp.zeros_like(one)).astype(bf16)
        double = jnp.concatenate([values, values], 0)
        square = jnp.zeros((1, count), f32)
        for first in range(0, width, step):
            state = dot_rows(pair[:, first : first + step], double)
            square += jnp.sum(state * state, 0, keepdims=True)
        spread = lax.rsqrt(square * (1.0 / width) + epsilon)
        top, rest = split(with_tail(tokens.astype(f32) * spread, spread, one))
        fill = jnp.zeros((DEPTH - 3 * SLAB, count), bf16)
        return jnp.concatenate([top, rest, top, fill], 0)

    for a in range(2):
        for c in range(2):
            turned = features(blocks[a, c].astype(bf16)).T
            for r in range(rows + 2):
                first = (4 * r + 2 * a + c) * cells
                keys_ref[first : first + cells, :] = turned[r * cells : (r + 1) * cells, :]
    keys_t_ref[...] = keys_ref[...].T

    parity = lax.axis_index("cfg")
    tokens = jnp.zeros((channels, 2 * own_lanes), f32)
    cell = lax.broadcasted_iota(jnp.int32, (own_lanes, 2 * own_lanes), 0)
    place = lax.broadcasted_iota(jnp.int32, (own_lanes, 2 * own_lanes), 1)
    group = 128 // channels
    fine_lines = 2 * own_lanes // group
    line = lax.broadcasted_iota(jnp.int32, (fine_lines, own_lanes), 0)
    column = lax.broadcasted_iota(jnp.int32, (fine_lines, own_lanes), 1)
    belongs = jnp.where(line == 2 * column // group, 1.0, 0.0)
    lane128 = lax.broadcasted_iota(jnp.int32, (own_lanes, 128), 1) // channels
    cell128 = lax.broadcasted_iota(jnp.int32, (own_lanes, 128), 0)
    repeat = lane_repeat(channels)
    fine = jnp.zeros((own_lanes, 128), f32)
    for c in range(2):
        mine = jnp.where(parity == 0, blocks[0, c], blocks[1, c])
        mine = pltpu.roll(mine, lanes - cells, 1)[:, :own_lanes]
        fine += jnp.where(lane128 == (2 * cell128 + c) % group, exact(mine, repeat, (0, 0)), 0.0)
        chosen = jnp.where(place == 2 * cell + c, 1.0, 0.0).astype(bf16)
        tokens += jnp.dot(mine.astype(bf16), chosen, preferred_element_type=f32)
    fine_ref[...] = exact(belongs, fine, (1, 0))
    token_ref[...] = tokens.astype(bf16)
    query_ref[...] = features(tokens.astype(bf16)).T


def attend_kernel(
    rows,
    window,
    length_ref,
    keys_ref,
    keys_t_ref,
    query_ref,
    query_gain_ref,
    key_gain_ref,
    text_ref,
    text_values_ref,
    kept_any,
    other_any,
    out_ref,
    mix_ref,
    value_ref,
    gain_ref,
    kept_ref,
    other_ref,
    sems,
):
    step = pl.program_id(0)
    seq_index = lax.axis_index("seq")
    head = query_gain_ref.shape[1]
    half = kept_ref.shape[1]
    key_count = keys_ref.shape[0]
    text_count, span = text_ref.shape
    per_step = span // head
    inner = pl.num_programs(0) * span
    low_ok = seq_index > 0
    high_ok = seq_index < lax.axis_size("seq") - 1
    key_row = lax.broadcasted_iota(jnp.int32, (key_count, head), 0)
    allowed = (low_ok | (key_row >= window)) & (high_ok | (key_row < key_count - window))
    text_row = lax.broadcasted_iota(jnp.int32, (text_count, head), 0)
    text_allowed = text_row < length_ref[...]
    text_rows = slice(key_count, key_count + text_count)

    @pl.when(step == 0)
    def _():
        fetch([(kept_any, kept_ref), (other_any, other_ref)], sems)
        core = seq_index % 2
        mix_ref[...] = jnp.zeros_like(mix_ref)
        for side, part_ref in ((core, kept_ref), (1 - core, other_ref)):
            top, rest = split(part_ref[...])
            where = pl.ds(pl.multiple_of(side * half, 128), half)
            mix_ref[0:TERMS, where] = top
            mix_ref[SLAB : SLAB + TERMS, where] = top
            mix_ref[2 * SLAB : 2 * SLAB + TERMS, where] = rest
        for i in range(per_step):
            value_ref[i, 0:key_count, head : 2 * head] = jnp.where(allowed, 1.0, 0.0).astype(bf16)
            value_ref[i, text_rows, head : 2 * head] = jnp.where(text_allowed, 1.0, 0.0).astype(
                bf16
            )
        same = lax.broadcasted_iota(jnp.int32, (head, head), 0) == lax.broadcasted_iota(
            jnp.int32, (head, head), 1
        )
        column = jnp.sum(jnp.where(same, key_gain_ref[...], 0.0), 1, keepdims=True)
        gain_ref[...] = jnp.broadcast_to(column, gain_ref.shape)

    def columns(which):
        return pl.ds(pl.multiple_of(which * inner + step * span, 128), span)

    queries = jnp.dot(query_ref[...], mix_ref[:, columns(0)], preferred_element_type=f32)
    all_keys = dot_rows(mix_ref[:, columns(1)], keys_t_ref[...])
    values = jnp.dot(keys_ref[...], mix_ref[:, columns(2)], preferred_element_type=f32)
    factor = head ** (-0.5) * LOG2E
    tokens = queries.shape[0] // rows
    for i in range(per_step):
        mine = slice(i * head, (i + 1) * head)
        query = queries[:, mine]
        mean = jnp.sum(query * query, -1, keepdims=True) * (1.0 / head)
        query = (query * lax.rsqrt(mean + epsilon) * query_gain_ref[...]).astype(bf16)
        keys = all_keys[mine]
        mean = jnp.sum(keys * keys, 0, keepdims=True) * (1.0 / head)
        keys = (keys * lax.rsqrt(mean + epsilon) * gain_ref[:, 0:1]).astype(bf16)
        value_ref[i, 0:key_count, 0:head] = jnp.where(allowed, values[:, mine], 0.0).astype(bf16)
        value_ref[i, text_rows, 0:head] = jnp.where(
            text_allowed, text_values_ref[:, mine].astype(f32), 0.0
        ).astype(bf16)
        for r in range(rows):
            part = query[r * tokens : (r + 1) * tokens]
            near = slice(r * window, (r + 3) * window)
            scores = jnp.dot(part, keys[:, near], preferred_element_type=f32)
            text_scores = lax.dot_general(
                part, text_ref[:, mine], (((1,), (1,)), ((), ())), preferred_element_type=f32
            )
            mixed = jnp.dot(
                jnp.exp2(scores * factor).astype(bf16),
                value_ref[i, near, :],
                preferred_element_type=f32,
            ) + jnp.dot(
                jnp.exp2(text_scores * factor).astype(bf16),
                value_ref[i, text_rows, :],
                preferred_element_type=f32,
            )
            out_ref[r * tokens : (r + 1) * tokens, mine] = (mixed[:, :head] / mixed[:, head:]).astype(
                bf16
            )


def output_kernel(
    levels,
    last,
    attended_ref,
    token_ref,
    embed_ref,
    bias_ref,
    mod_ref,
    own_first_ref,
    own_second_ref,
    other_first_ref,
    other_second_ref,
    *rest,
):
    out_any, block_ref, sems = rest[-3:]
    count, piece, _ = own_first_ref.shape
    seq_index = lax.axis_index("seq")
    core = seq_index % 2
    low = len(levels) - 3
    seq_chips = lax.axis_size("seq") // 2
    attended = attended_ref[...]
    tokens = token_ref[...]
    lanes = 2 * piece
    sides = ((own_first_ref, other_first_ref), (own_second_ref, other_second_ref))
    group = 2
    copies = []
    for top, (own_ref, other_ref) in enumerate(sides):
        for start in range(0, count, group):
            blocks = []
            for index in range(start, start + group):
                blocks += [own_ref[index], other_ref[index]]
            product = lax.dot_general(
                attended,
                jnp.concatenate(blocks, 0),
                (((1,), (1,)), ((), ())),
                preferred_element_type=f32,
            )
            for i in range(group):
                index = start + i
                near = index >> low & 1
                first, second = (near, last) if top == 0 else (last, near)
                flip = second + (top << (levels[-1][1] - 1))
                for j in range(low):
                    flip = flip + ((index >> j & 1) << (levels[2 + j][1] - 1))
                chip = (lax.axis_index("cfg") ^ first) * seq_chips + (seq_index // 2 ^ flip)
                where = pl.ds(pl.multiple_of(chip * lanes, lanes), lanes)
                block = pltpu.roll(product[:, i * lanes : (i + 1) * lanes], core * piece, 1)
                state = dot_rows(tokens, embed_ref[:, where]) + bias_ref[:, where]
                slot = top * count + index
                block_ref[slot] = (state + mod_ref[2:3, where] * block).astype(bf16)
                copy = pltpu.make_async_copy(block_ref.at[slot], out_any.at[:, where], sems.at[slot])
                copy.start()
                copies.append(copy)
    for copy in copies:
        copy.wait()


def per_device(
    coarse_hidden,
    coarse_modulation,
    final_weight,
    coarse_latent,
    step_index,
    guide_index,
    guide_scales,
    upsample_weight,
    upsample_bias,
    embed_weight,
    embed_bias,
    fine_modulation,
    project_weight,
    query_gain,
    key_gain,
    text_keys,
    text_values,
    text_length,
    output_weight,
):
    rows = coarse_hidden.shape[1]
    cells = coarse_hidden.shape[2]
    width = coarse_hidden.shape[3]
    channels = final_weight.shape[1]
    head = query_gain.shape[0]
    inner = project_weight.shape[1] // 3
    cfg_count = lax.axis_size("cfg")
    seq_count = lax.axis_size("seq")
    seq_index = lax.axis_index("seq")
    seq_bits = seq_count.bit_length() - 1
    assert seq_count == 1 << seq_bits and cfg_count == 2 and rows >= 2 and seq_bits >= 3
    own = rows * cells
    fine_tokens = 2 * own
    key_count = (rows + 2) * 4 * cells
    text_count = text_keys.shape[0]
    bias_row = embed_bias.reshape(1, width)

    def swap(value, *stages):
        size = cfg_count * seq_count
        flip = 0
        for axis, bit in stages:
            flip |= seq_count if axis == "cfg" else 1 << bit
        return lax.ppermute(value, ("cfg", "seq"), [(i, i ^ flip) for i in range(size)])

    across = ("seq", 0)
    levels = [("cfg", 0)] + [("seq", bit) for bit in range(1, seq_bits)]

    half = 3 * inner // 2
    kept, sent = pl.pallas_call(
        functools.partial(partial_kernel, seq_count),
        out_shape=(jax.ShapeDtypeStruct((TERMS, half), f32),) * 2,
        in_specs=vmem(4),
        out_specs=tuple(vmem(2)),
        cost_estimate=cost(2e9, 1e6),
        name="partial_mix",
    )(embed_weight, bias_row, fine_modulation, project_weight)
    met = swap(sent, across)

    velocity = pl.pallas_call(
        velocity_kernel,
        out_shape=jax.ShapeDtypeStruct((channels, own), f32),
        in_specs=vmem(3),
        out_specs=vmem(1)[0],
        cost_estimate=cost(2e9, 1e6),
        name="velocity",
        compiler_params=pltpu.CompilerParams(vmem_limit_bytes=6 << 20),
    )(coarse_hidden.reshape(own, width), coarse_modulation[0], final_weight.T)
    partner = swap(velocity, ("cfg", 0))

    held = output_weight.T[None]

    def doubled(block, stage):
        return jnp.concatenate([block, swap(block, stage)], 0)

    first, second = levels[0], levels[1]
    total = kept + met
    rounded = total.astype(bf16)
    for stage in levels[2:]:
        held = doubled(held, stage)
    total = (
        total
        + swap(rounded, first).astype(f32)
        + swap(rounded, second).astype(f32)
        + swap(rounded, first, second).astype(f32)
    )

    lines = own * channels // 128
    latent = coarse_latent.reshape(rows, lines // rows, 128).transpose(1, 0, 2).reshape(lines, 128)
    guided, stepped = pl.pallas_call(
        functools.partial(guide_kernel, rows),
        out_shape=(
            jax.ShapeDtypeStruct((lines, 128), f32),
            jax.ShapeDtypeStruct((channels, own), f32),
        ),
        in_specs=vmem(4) + anywhere(2),
        out_specs=tuple(vmem(2)),
        scratch_shapes=[pltpu.VMEM((channels, own), f32)] * 2 + [pltpu.SemaphoreType.DMA((2,))],
        cost_estimate=cost(1e9, 1e5),
        name="guide",
        compiler_params=pltpu.CompilerParams(vmem_limit_bytes=2 << 20),
    )(
        step_index.reshape(1, 1),
        guide_index.reshape(1, 1),
        guide_scales.reshape(-1, 128),
        latent,
        velocity,
        partner,
    )

    near_rows = swap(stepped, across)
    ahead = [(i, i + 1) for i in range(1, seq_count - 1, 2)]
    behind = [(target, source) for source, target in ahead]
    far_rows = lax.ppermute(stepped, "seq", ahead + behind)

    fine, keys, keys_t, query, tokens, text_normed = pl.pallas_call(
        functools.partial(fine_kernel, cells),
        out_shape=(
            jax.ShapeDtypeStruct((2 * lines, 128), f32),
            jax.ShapeDtypeStruct((key_count, DEPTH), bf16),
            jax.ShapeDtypeStruct((DEPTH, key_count), bf16),
            jax.ShapeDtypeStruct((fine_tokens, DEPTH), bf16),
            jax.ShapeDtypeStruct((channels, fine_tokens), bf16),
            jax.ShapeDtypeStruct(text_keys.shape, bf16),
        ),
        in_specs=vmem(6) + anywhere(3),
        out_specs=tuple(vmem(6)),
        scratch_shapes=[pltpu.VMEM((channels, own), f32)] * 3 + [pltpu.SemaphoreType.DMA((3,))],
        cost_estimate=cost(4e9, 4e6),
        name="fine_features",
        compiler_params=pltpu.CompilerParams(vmem_limit_bytes=20 << 20),
    )(
        upsample_weight.T,
        upsample_bias.reshape(1, channels),
        embed_weight,
        bias_row,
        text_keys,
        key_gain.reshape(1, head),
        near_rows,
        stepped,
        far_rows,
    )

    for stage in levels[2:]:
        moved = swap(total.astype(bf16), stage)
        total = total + moved.astype(f32)
    others = swap(total, across)

    middle = held.shape[0] // 2
    own_first, own_second = held[:middle], held[middle:]
    own_first = doubled(own_first, first)
    own_second = doubled(own_second, second)
    far_first = swap(own_first, second)
    far_second = swap(own_second, first)
    near_pieces = (own_first, own_second, swap(own_first, across), swap(own_second, across))
    far_pieces = (far_first, far_second, swap(far_first, across), swap(far_second, across))

    whole = pl.BlockSpec(memory_space=pltpu.VMEM)
    free = pl.BlockSpec(memory_space=pl.ANY)
    span = 2 * head
    per_step = pl.BlockSpec((text_count, span), lambda h: (0, h))
    attended = pl.pallas_call(
        functools.partial(attend_kernel, rows, 4 * cells),
        grid=(inner // span,),
        out_shape=jax.ShapeDtypeStruct((fine_tokens, inner), bf16),
        in_specs=[whole] * 6 + [per_step, per_step, free, free],
        out_specs=pl.BlockSpec((fine_tokens, span), lambda h: (0, h)),
        scratch_shapes=[
            pltpu.VMEM((DEPTH, 3 * inner), bf16),
            pltpu.VMEM((2, key_count + text_count, 2 * head), bf16),
            pltpu.VMEM((head, 128), f32),
            pltpu.VMEM((TERMS, half), f32),
            pltpu.VMEM((TERMS, half), f32),
            pltpu.SemaphoreType.DMA((2,)),
        ],
        cost_estimate=cost(8e9, 4e6),
        name="attend",
        compiler_params=pltpu.CompilerParams(vmem_limit_bytes=24 << 20),
    )(
        text_length.reshape(1, 1),
        keys,
        keys_t,
        query,
        query_gain.reshape(1, head),
        key_gain.reshape(1, head),
        text_normed,
        text_values,
        total,
        others,
    )

    piece = output_weight.shape[1]
    count = own_first.shape[0]
    if 2 * piece == 128:

        def output(last, pieces, *before):
            return pl.pallas_call(
                functools.partial(output_kernel, tuple(levels), last),
                out_shape=jax.ShapeDtypeStruct((fine_tokens, width), bf16),
                in_specs=[whole] * 9 + [free] * len(before),
                out_specs=free,
                input_output_aliases={9: 0} if before else {},
                scratch_shapes=[
                    pltpu.VMEM((2 * count, fine_tokens, 128), bf16),
                    pltpu.SemaphoreType.DMA((2 * count,)),
                ],
                cost_estimate=cost(1e9, 3e6),
                compiler_params=pltpu.CompilerParams(vmem_limit_bytes=16 << 20),
            )(attended, tokens, embed_weight, bias_row, fine_modulation, *pieces, *before)

        near = output(0, near_pieces)
        hidden = output(1, far_pieces, near)
    else:
        low = len(levels) - 3
        chip = jnp.arange(4 * count, dtype=jnp.int32)
        seq_chips = seq_count // 2
        apart = chip // seq_chips ^ lax.axis_index("cfg")
        flip = chip % seq_chips ^ seq_index // 2
        side = flip & 1
        top = flip >> (levels[-1][1] - 1) & 1
        position = top * count + (jnp.where(top == 0, apart, side) << low)
        position = position + jnp.where(top == 0, side, apart) * (2 * count)
        for j in range(low):
            position = position + ((flip >> (levels[2 + j][1] - 1) & 1) << j)
        mine = jnp.take(jnp.concatenate(near_pieces[:2] + far_pieces[:2], 0), position, axis=0)
        theirs = jnp.take(jnp.concatenate(near_pieces[2:] + far_pieces[2:], 0), position, axis=0)
        even = seq_index % 2 == 0
        both = jnp.stack([jnp.where(even, mine, theirs), jnp.where(even, theirs, mine)], 1)
        product = lax.dot_general(
            attended,
            both.reshape(width, inner),
            (((1,), (1,)), ((), ())),
            preferred_element_type=f32,
        )
        state = dot_rows(tokens, embed_weight) + bias_row
        hidden = (state + fine_modulation[2:3] * product).astype(bf16)

    guided = guided.reshape(lines // rows, rows, 128).transpose(1, 0, 2)
    return (
        guided.reshape(rows, cells * channels),
        fine.reshape(rows, 1, 2 * cells * channels),
        hidden.reshape(rows, 1, 2 * cells, width),
    )


def solution(mesh):
    placed = (
        P("cfg", "seq", None, None),
        P("cfg", None, None),
        P(),
        P("seq", None),
        P(),
        P(),
        P(),
        P(),
        P(),
        P(),
        P(),
        P(),
        P(("cfg", "seq"), None),
        P(),
        P(),
        P(),
        P(),
        P(),
        P(None, ("cfg", "seq")),
    )
    return jax.shard_map(
        per_device,
        mesh=mesh,
        in_specs=placed,
        out_specs=(P("seq", None), P("seq", "cfg", None), P("seq", "cfg", None, None)),
        check_vma=False,
    )
```

time: 109 us -> 73.5 us (0.67)
  Pallas kernels: 27.8 us -> 17.4 us
  local copies, waits for them, and re-layouts: 11.5 us -> 1.41 us
  starting transfers between devices: 27.9 us -> 19.7 us
  waiting for transfers between devices: 37.1 us -> 31.6 us
    pallas_call x3 -> x4, Pallas kernels: 18.8 us -> 11.6 us  [the longest x1 6.81 us: per_device(): pl.pallas_call(functools.partial(attend_kernel, rows, 4 * cells), grid=(i...]
    ppermute x18 -> x19, starting transfers between devices: 25.4 us -> 19.1 us  [swap(): lax.ppermute(value, ('cfg', 'seq'), [(i, i ^ flip) for i in range(size)])]
    ppermute x18 -> x19, waiting for transfers between devices: 37.1 us -> 31.6 us  [swap(): lax.ppermute(value, ('cfg', 'seq'), [(i, i ^ flip) for i in range(size)])]
    reshape x6 -> x0, local copies, waits for them, and re-layouts: 3.67 us -> none  [the longest x1 0.78 us: per_device(): fine_latent = fine.transpose(2, 0, 1).reshape(rows, 1, 2 * cells * channels)]
    unnamed x37 -> x33, local copies, waits for them, and re-layouts: 3.85 us -> 1.39 us
    ppermute x2 -> x1, starting transfers between devices: 2.57 us -> 0.66 us  [per_device(): far_rows = lax.ppermute(stepped, 'seq', ahead + behind)]
    pallas_call x1, Pallas kernels: 2.49 us -> 0.59 us  [per_device(): pl.pallas_call(velocity_kernel, out_shape=jax.ShapeDtypeStruct((channels,...]
    transpose x2 -> x0, local copies, waits for them, and re-layouts: 1.69 us -> none  [the longest x1 0.88 us: per_device(): fine_latent = fine.transpose(2, 0, 1).reshape(rows, 1, 2 * cells * channels)]
  transfers between devices with their start and end apart: 20 -> 20, of which waited for: 4 -> 5; matrix products, arithmetic and copies ran while one was open for 9% -> 0% of each run, Pallas kernels for 20% -> 18%
where the time goes in v2:
time: 73.5 us; the launch traced here: 73.3 us
  waiting for transfers between devices  31.6 us (43%)
  starting transfers between devices  19.7 us (27%)
  Pallas kernels  17.4 us (24%)
  between operations  2.91 us (4%)
  local copies, waits for them, and re-layouts  1.41 us (2%)
    ppermute x19, waiting for transfers between devices, swap(): lax.ppermute(value, ('cfg', 'seq'), [(i, i ^ flip) for i in range(size)])  31.6 us
    ppermute x19, starting transfers between devices, swap(): lax.ppermute(value, ('cfg', 'seq'), [(i, i ^ flip) for i in range(size)])  19.1 us
    pallas_call x1, Pallas kernels, per_device(): pl.pallas_call(functools.partial(attend_kernel, rows, 4 * cells), grid=(i...  6.81 us
    pallas_call x2, Pallas kernels, output(): pl.pallas_call(functools.partial(output_kernel, tuple(levels), last), out...  3.44 us
    pallas_call x1, Pallas kernels, per_device(): pl.pallas_call(functools.partial(fine_kernel, cells), out_shape=(jax.Shap...  2.91 us
    pallas_call x1, Pallas kernels, per_device(): pl.pallas_call(functools.partial(partial_kernel, seq_count), out_shape=(j...  2.29 us
  transfers between devices with their start and end apart: 20, of which 5 were waited for; matrix products, arithmetic and copies ran while one was open for 0% of the time, Pallas kernels for 18%

profile of v2, /device:TPU:0, one launch (start us, length us, event | category | flops | bytes accessed | tf_op | source)
XLA Modules:
  0.0 73.3 jit_solution(13980241290343269749)
XLA Ops:
  0.7 2.3 %partial_mix.1 = (f32[40,1536]{1,0:T(8,128)}, f32[40,1536]{1,0:T(8,128)}) custom-call(bf16[32,2048]{1,0:T(8,128)(2,1)} %embed_ref.7, f32[1,2048]{1,0:T(1,128)} %bitcast.32, f32[3,2048]{1,0:T(4,128)} %mod_ref.5, bf16[64,3072]{1,0:T(8,128)(2,1)} %weight_ref.1), custom_call_target="tpu_custom_call" | custom-call | flops 2000000000 | bytes 1000000 | tf_op jit(solution)/shard_map/partial_mix/pallas_call | solution.py:503
  3.0 0.5 collective-permute-start.3
  3.5 0.6 velocity.1.own_any
  4.1 2.5 %collective-permute-start = (f32[32,128]{1,0:T(8,128)S(1)}, f32[32,128]{1,0:T(8,128)S(1)}, u32[]{:S(2)}, u32[]{:S(2)}) collective-permute-start(f32[32,128]{1,0:T(8,128)S(1)} %velocity.1.own_any), channel_id=1, source_target_pairs={{0,16},{1,17},{2,18},{3,19},{4,20},{5,21},{6,22},{7,23},{8,24},{9,... | collective-permute-start | bytes 49160 | tf_op jit(solution)/shard_map/ppermute | solution.py:497
  6.6 1.6 %collective-permute-start.10 = (bf16[1,64,1024]{2,1,0:T(8,128)(2,1)S(1)}, bf16[1,64,1024]{2,1,0:T(8,128)(2,1)S(1)}, u32[]{:S(2)}, u32[]{:S(2)}) collective-permute-start(bf16[1,64,1024]{2,1,0:T(8,128)(2,1)S(1)} %bitcast.47), channel_id=1, source_target_pairs={{0,4},{1,5},{2,6},{3,7},{4,0},{5,1},{6,2},{7,3},{8,12},{9,13},{10,... | collective-permute-start | bytes 393224 | tf_op jit(solution)/shard_map/ppermute | solution.py:497
  10.2 0.6 collective-permute-start.4
  10.8 1.5 %collective-permute-start.5 = (bf16[40,1536]{1,0:T(8,128)(2,1)S(1)}, bf16[40,1536]{1,0:T(8,128)(2,1)S(1)}, u32[]{:S(2)}, u32[]{:S(2)}) collective-permute-start(bf16[40,1536]{1,0:T(8,128)(2,1)S(1)} %get-tuple-element.28), channel_id=1, source_target_pairs={{0,2},{1,3},{2,0},{3,1},{4,6},{5,7},{6,4},{7,5},{8,10},{9,11},{10,... | collective-permute-start | bytes 368648 | tf_op jit(solution)/shard_map/ppermute | solution.py:497
  12.3 1.4 %collective-permute-start.6 = (bf16[40,1536]{1,0:T(8,128)(2,1)S(1)}, bf16[40,1536]{1,0:T(8,128)(2,1)S(1)}, u32[]{:S(2)}, u32[]{:S(2)}) collective-permute-start(bf16[40,1536]{1,0:T(8,128)(2,1)S(1)} %get-tuple-element.28), channel_id=1, source_target_pairs={{0,18},{1,19},{2,16},{3,17},{4,22},{5,23},{6,20},{7,21},{8,26},{9,... | collective-permute-start | bytes 368648 | tf_op jit(solution)/shard_map/ppermute | solution.py:497
  13.8 1.3 %guide.1 = (f32[32,128]{1,0:T(8,128)}, f32[32,128]{1,0:T(8,128)S(1)}) custom-call(s32[1,1]{1,0:T(1,128)} %bitcast.29.step_ref, s32[1,1]{1,0:T(1,128)} %bitcast.30.slot_ref, f32[32,128]{1,0:T(8,128)S(1)} %bitcast.40, f32[32,128]{1,0:T(8,128)S(1)} %bitcast.41, f32[32,128]{1,0:T(8,128)S(1)} %velocity.1.own_any, f32[32,128]{1,0:T(8,128)S(1)} %collective-permute-done.other_any), custom_call_target="tpu_custom_call" | custom-call | flops 1000000000 | bytes 100000 | tf_op jit(solution)/shard_map/guide/pallas_call | solution.py:543
  15.2 0.7 collective-permute-start.2
  15.9 0.6 collective-permute-done.4
  16.5 3.7 %collective-permute-start.13 = (bf16[2,64,1024]{2,1,0:T(8,128)(2,1)S(1)}, bf16[2,64,1024]{2,1,0:T(8,128)(2,1)S(1)}, u32[]{:S(2)}, u32[]{:S(2)}) collective-permute-start(bf16[2,64,1024]{2,1,0:T(8,128)(2,1)S(1)} %pad_maximum_fusion.1), channel_id=1, source_target_pairs={{0,8},{1,9},{2,10},{3,11},{4,12},{5,13},{6,14},{7,15},{8,0},{9,1},... | collective-permute-start | bytes 786440 | tf_op jit(solution)/shard_map/ppermute | solution.py:497
  20.2 0.5 collective-permute-start.11
  20.8 2.8 %collective-permute-start.7 = (bf16[40,1536]{1,0:T(8,128)(2,1)S(1)}, bf16[40,1536]{1,0:T(8,128)(2,1)S(1)}, u32[]{:S(2)}, u32[]{:S(2)}) collective-permute-start(bf16[40,1536]{1,0:T(8,128)(2,1)S(1)} %get-tuple-element.26), channel_id=1, source_target_pairs={{0,4},{1,5},{2,6},{3,7},{4,0},{5,1},{6,2},{7,3},{8,12},{9,13},{10,... | collective-permute-start | bytes 368648 | tf_op jit(solution)/shard_map/ppermute | solution.py:497
  23.6 5.8 %collective-permute-done.11 = bf16[2,64,1024]{2,1,0:T(8,128)(2,1)S(1)} collective-permute-done((bf16[2,64,1024]{2,1,0:T(8,128)(2,1)S(1)}, bf16[2,64,1024]{2,1,0:T(8,128)(2,1)S(1)}, u32[]{:S(2)}, u32[]{:S(2)}) %collective-permute-start.11) | collective-permute-done | bytes 262176 | tf_op jit(solution)/shard_map/ppermute | solution.py:497
  29.4 0.5 collective-permute-start.12
  29.9 2.5 %collective-permute-done.13 = bf16[2,64,1024]{2,1,0:T(8,128)(2,1)S(1)} collective-permute-done((bf16[2,64,1024]{2,1,0:T(8,128)(2,1)S(1)}, bf16[2,64,1024]{2,1,0:T(8,128)(2,1)S(1)}, u32[]{:S(2)}, u32[]{:S(2)}) %collective-permute-start.13) | collective-permute-done | bytes 262176 | tf_op jit(solution)/shard_map/ppermute | solution.py:497
  32.4 1.6 %collective-permute-start.14 = (bf16[2,64,1024]{2,1,0:T(8,128)(2,1)S(1)}, bf16[2,64,1024]{2,1,0:T(8,128)(2,1)S(1)}, u32[]{:S(2)}, u32[]{:S(2)}) collective-permute-start(bf16[2,64,1024]{2,1,0:T(8,128)(2,1)S(1)} %collective-permute-done.13), channel_id=1, source_target_pairs={{0,2},{1,3},{2,0},{3,1},{4,6},{5,7},{6,4},{7,5},{8,10},{9,11},{10,... | collective-permute-start | bytes 786440 | tf_op jit(solution)/shard_map/ppermute | solution.py:497
  34.0 0.1 collective-permute-start.8
  34.1 14.9 %collective-permute-done.14 = bf16[2,64,1024]{2,1,0:T(8,128)(2,1)S(1)} collective-permute-done((bf16[2,64,1024]{2,1,0:T(8,128)(2,1)S(1)}, bf16[2,64,1024]{2,1,0:T(8,128)(2,1)S(1)}, u32[]{:S(2)}, u32[]{:S(2)}) %collective-permute-start.14) | collective-permute-done | bytes 262176 | tf_op jit(solution)/shard_map/ppermute | solution.py:497
  49.1 0.6 collective-permute-start.15
  49.9 0.1 copy-done
  50.0 0.5 copy-done.11
  50.6 2.9 %fine_features.1 = (f32[64,128]{1,0:T(8,128)}, bf16[1024,256]{1,0:T(8,128)(2,1)S(1)}, bf16[256,1024]{1,0:T(8,128)(2,1)S(1)}, bf16[256,256]{1,0:T(8,128)(2,1)S(1)...) custom-call(f32[32,288]{1,0:T(8,128)S(1)} %bitcast.38, f32[1,32]{1,0:T(1,128)S(1)} %bitcast.42, ...), custom_call_target="tpu_custom_call" | custom-call | flops 4000000000 | bytes 4000000 | tf_op jit(solution)/shard_map/fine_features/pallas_call | solution.py:569
  53.5 0.5 collective-permute-start.18
  54.0 0.1 collective-permute-start.19
  54.1 0.4 collective-permute-start.16
  54.5 7.8 %collective-permute-done.15.own_second_ref = bf16[4,64,1024]{2,1,0:T(8,128)(2,1)S(1)} collective-permute-done((bf16[4,64,1024]{2,1,0:T(8,128)(2,1)S(1)}, bf16[4,64,1024]{2,1,0:T(8,128)(2,1)S(1)}, u32[]{:S(2)}, u32[]{:S(2)}) %collective-permute-start.15) | collective-permute-done | bytes 524320 | tf_op jit(solution)/shard_map/ppermute | solution.py:497
  62.3 0.6 copy-done.13
  63.0 6.8 %attend.1.attended_ref = bf16[256,1024]{1,0:T(8,128)(2,1)S(1)} custom-call(s32[1,1]{1,0:T(1,128)} %bitcast.31.length_ref, bf16[1024,256]{1,0:T(8,128)(2,1)S(1)} %get-tuple-element.16.keys_ref, bf16[256,1024]{1,0:T(8,128)(2,1)S(1)} %get-tuple-element.17.keys_t_ref, bf16[256,256]{1,0:T(8,128)(2,1)S(1)} %get-tuple-element.18.query_ref, f32[1,128]{1,0:T(1,128)S(1)} %bitcast.45, ...), custom_call_target="tpu_custom_call" | custom-call | flops 8000000000 | bytes 4000000 | tf_op jit(solution)/shard_map/attend/pallas_call | solution.py:615
  69.8 1.7 %shard_map.202.rest_0_ = bf16[256,2048]{1,0:T(8,128)(2,1)} custom-call(bf16[256,1024]{1,0:T(8,128)(2,1)S(1)} %attend.1.attended_ref, bf16[32,256]{1,0:T(8,128)(2,1)S(1)} %get-tuple-element.22.token_ref, bf16[32,2048]{1,0:T(8,128)(2,1)S(1)} %copy-done, f32[1,2048]{1,0:T(1,128)S(1)} %bitcast.34, f32[3,2048]{1,0:T(4,128)S(1)} %copy-done.1, ...), custom_call_target="tpu_custom_call" | custom-call | flops 1000000000 | bytes 3000000 | tf_op jit(solution)/shard_map/pallas_call | solution.py:650
  71.5 1.7 %shard_map.203 = bf16[256,2048]{1,0:T(8,128)(2,1)} custom-call(bf16[256,1024]{1,0:T(8,128)(2,1)S(1)} %attend.1.attended_ref, bf16[32,256]{1,0:T(8,128)(2,1)S(1)} %get-tuple-element.22.token_ref, bf16[32,2048]{1,0:T(8,128)(2,1)S(1)} %copy-done, f32[1,2048]{1,0:T(1,128)S(1)} %bitcast.35, f32[3,2048]{1,0:T(4,128)S(1)} %copy-done.1, ...), custom_call_target="tpu_custom_call", output_to_operand_aliasing={{}: (9, {})} | custom-call | flops 1000000000 | bytes 3000000 | tf_op jit(solution)/shard_map/pallas_call | solution.py:650
  (55 shorter events, 0.6 us)
Async XLA Ops:
  0.6 2.8 %copy-start.3 = (bf16[1,2,64,2048]{3,2,1,0:T(8,128)(2,1)S(1)}, bf16[1,2,64,2048]{3,2,1,0:T(8,128)(2,1)}, u32[]{:S(2)}) copy-start(bf16[1,2,64,2048]{3,2,1,0:T(8,128)(2,1)} %param.19) | copy-start | bytes 1572868
  0.6 2.8 %copy-start.6 = (bf16[2048,32]{0,1:T(8,128)(2,1)S(1)}, bf16[2048,32]{0,1:T(8,128)(2,1)}, u32[]{:S(2)}) copy-start(bf16[2048,32]{0,1:T(8,128)(2,1)} %param.21) | copy-start | bytes 393220
  0.7 2.8 %copy-start.8 = (f32[1,2,2048]{2,1,0:T(2,128)S(1)}, f32[1,2,2048]{2,1,0:T(2,128)}, u32[]{:S(2)}) copy-start(f32[1,2,2048]{2,1,0:T(2,128)} %param.20) | copy-start | bytes 49156
  3.0 7.2 %collective-permute-start.3 = (f32[40,1536]{1,0:T(8,128)}, f32[40,1536]{1,0:T(8,128)S(1)}, u32[]{:S(2)}, u32[]{:S(2)}) collective-permute-start(f32[40,1536]{1,0:T(8,128)} %get-tuple-element.21), channel_id=1, source_target_pairs={{0,1},{1,0},{2,3},{3,2},{4,5},{5,4},{6,7},{7,6},{8,9},{9,8},{10,11... | collective-permute-start | bytes 737288 | tf_op jit(solution)/shard_map/ppermute | solution.py:497
  3.5 3.1 %copy-start.14 = (bf16[1024,64]{0,1:T(8,128)(2,1)S(1)}, bf16[1024,64]{0,1:T(8,128)(2,1)}, u32[]{:S(2)}) copy-start(bf16[1024,64]{0,1:T(8,128)(2,1)} %param.37) | copy-start | bytes 393220
  3.5 6.7 %copy-start.15 = (f32[40,1536]{1,0:T(8,128)S(1)}, f32[40,1536]{1,0:T(8,128)}, u32[]{:S(2)}) copy-start(f32[40,1536]{1,0:T(8,128)} %get-tuple-element.20) | copy-start | bytes 737284
  4.1 9.7 %collective-permute-start = (f32[32,128]{1,0:T(8,128)S(1)}, f32[32,128]{1,0:T(8,128)S(1)}, u32[]{:S(2)}, u32[]{:S(2)}) collective-permute-start(f32[32,128]{1,0:T(8,128)S(1)} %velocity.1.own_any), channel_id=1, source_target_pairs={{0,16},{1,17},{2,18},{3,19},{4,20},{5,21},{6,22},{7,23},{8,24},{9,... | collective-permute-start | bytes 49160 | tf_op jit(solution)/shard_map/ppermute | solution.py:497
  6.6 8.6 %collective-permute-start.10 = (bf16[1,64,1024]{2,1,0:T(8,128)(2,1)S(1)}, bf16[1,64,1024]{2,1,0:T(8,128)(2,1)S(1)}, u32[]{:S(2)}, u32[]{:S(2)}) collective-permute-start(bf16[1,64,1024]{2,1,0:T(8,128)(2,1)S(1)} %bitcast.47), channel_id=1, source_target_pairs={{0,4},{1,5},{2,6},{3,7},{4,0},{5,1},{6,2},{7,3},{8,12},{9,13},{10,... | collective-permute-start | bytes 393224 | tf_op jit(solution)/shard_map/ppermute | solution.py:497
  10.1 3.6 %copy-start.9 = (f32[4096]{0:T(1024)S(1)}, f32[4096]{0:T(1024)}, u32[]{:S(2)}) copy-start(f32[4096]{0:T(1024)} %param.25) | copy-start | bytes 49156
  10.1 3.6 %copy-start.10 = (f32[2,2048]{1,0:T(2,128)S(1)}, f32[2,2048]{1,0:T(2,128)}, u32[]{:S(2)}) copy-start(f32[2,2048]{1,0:T(2,128)} %param.22) | copy-start | bytes 49156
  10.2 6.3 %collective-permute-start.4 = (bf16[40,1536]{1,0:T(8,128)(2,1)S(1)}, bf16[40,1536]{1,0:T(8,128)(2,1)S(1)}, u32[]{:S(2)}, u32[]{:S(2)}) collective-permute-start(bf16[40,1536]{1,0:T(8,128)(2,1)S(1)} %get-tuple-element.28), channel_id=1, source_target_pairs={{0,16},{1,17},{2,18},{3,19},{4,20},{5,21},{6,22},{7,23},{8,24},{9,... | collective-permute-start | bytes 368648 | tf_op jit(solution)/shard_map/ppermute | solution.py:497
  10.8 9.4 %collective-permute-start.5 = (bf16[40,1536]{1,0:T(8,128)(2,1)S(1)}, bf16[40,1536]{1,0:T(8,128)(2,1)S(1)}, u32[]{:S(2)}, u32[]{:S(2)}) collective-permute-start(bf16[40,1536]{1,0:T(8,128)(2,1)S(1)} %get-tuple-element.28), channel_id=1, source_target_pairs={{0,2},{1,3},{2,0},{3,1},{4,6},{5,7},{6,4},{7,5},{8,10},{9,11},{10,... | collective-permute-start | bytes 368648 | tf_op jit(solution)/shard_map/ppermute | solution.py:497
  12.3 8.4 %collective-permute-start.6 = (bf16[40,1536]{1,0:T(8,128)(2,1)S(1)}, bf16[40,1536]{1,0:T(8,128)(2,1)S(1)}, u32[]{:S(2)}, u32[]{:S(2)}) collective-permute-start(bf16[40,1536]{1,0:T(8,128)(2,1)S(1)} %get-tuple-element.28), channel_id=1, source_target_pairs={{0,18},{1,19},{2,16},{3,17},{4,22},{5,23},{6,20},{7,21},{8,26},{9,... | collective-permute-start | bytes 368648 | tf_op jit(solution)/shard_map/ppermute | solution.py:497
  15.1 34.7 %collective-permute-start.1 = (f32[32,128]{1,0:T(8,128)S(1)}, f32[32,128]{1,0:T(8,128)S(1)}, u32[]{:S(2)}, u32[]{:S(2)}) collective-permute-start(f32[32,128]{1,0:T(8,128)S(1)} %get-tuple-element.14.own_any), channel_id=1, source_target_pairs={{0,1},{1,0},{2,3},{3,2},{4,5},{5,4},{6,7},{7,6},{8,9},{9,8},{10,11... | collective-permute-start | bytes 49160 | tf_op jit(solution)/shard_map/ppermute | solution.py:497
  15.2 34.6 %collective-permute-start.2 = (f32[32,128]{1,0:T(8,128)S(1)}, f32[32,128]{1,0:T(8,128)S(1)}, u32[]{:S(2)}, u32[]{:S(2)}) collective-permute-start(f32[32,128]{1,0:T(8,128)S(1)} %get-tuple-element.14.own_any), channel_id=1, source_target_pairs={{1,2},{3,4},{5,6},{7,8},{9,10},{11,12},{13,14},{2,1},{4,3},{6,5},{... | collective-permute-start | bytes 49160 | tf_op jit(solution)/shard_map/ppermute | solution.py:567
  16.5 16.0 %collective-permute-start.13 = (bf16[2,64,1024]{2,1,0:T(8,128)(2,1)S(1)}, bf16[2,64,1024]{2,1,0:T(8,128)(2,1)S(1)}, u32[]{:S(2)}, u32[]{:S(2)}) collective-permute-start(bf16[2,64,1024]{2,1,0:T(8,128)(2,1)S(1)} %pad_maximum_fusion.1), channel_id=1, source_target_pairs={{0,8},{1,9},{2,10},{3,11},{4,12},{5,13},{6,14},{7,15},{8,0},{9,1},... | collective-permute-start | bytes 786440 | tf_op jit(solution)/shard_map/ppermute | solution.py:497
  20.2 9.2 %collective-permute-start.11 = (bf16[2,64,1024]{2,1,0:T(8,128)(2,1)S(1)}, bf16[2,64,1024]{2,1,0:T(8,128)(2,1)S(1)}, u32[]{:S(2)}, u32[]{:S(2)}) collective-permute-start(bf16[2,64,1024]{2,1,0:T(8,128)(2,1)S(1)} %pad_maximum_fusion.1), channel_id=1, source_target_pairs={{0,16},{1,17},{2,18},{3,19},{4,20},{5,21},{6,22},{7,23},{8,24},{9,... | collective-permute-start | bytes 786440 | tf_op jit(solution)/shard_map/ppermute | solution.py:497
  20.8 13.2 %collective-permute-start.7 = (bf16[40,1536]{1,0:T(8,128)(2,1)S(1)}, bf16[40,1536]{1,0:T(8,128)(2,1)S(1)}, u32[]{:S(2)}, u32[]{:S(2)}) collective-permute-start(bf16[40,1536]{1,0:T(8,128)(2,1)S(1)} %get-tuple-element.26), channel_id=1, source_target_pairs={{0,4},{1,5},{2,6},{3,7},{4,0},{5,1},{6,2},{7,3},{8,12},{9,13},{10,... | collective-permute-start | bytes 368648 | tf_op jit(solution)/shard_map/ppermute | solution.py:497
  29.4 24.7 %collective-permute-start.12 = (bf16[4,64,1024]{2,1,0:T(8,128)(2,1)S(1)}, bf16[4,64,1024]{2,1,0:T(8,128)(2,1)S(1)}, u32[]{:S(2)}, u32[]{:S(2)}) collective-permute-start(bf16[4,64,1024]{2,1,0:T(8,128)(2,1)S(1)} %pad_maximum_fusion.own_first_ref), channel_id=1, source_target_pairs={{0,2},{1,3},{2,0},{3,1},{4,6},{5,7},{6,4},{7,5},{8,10},{9,11},{10,... | collective-permute-start | bytes 1572872 | tf_op jit(solution)/shard_map/ppermute | solution.py:497
  32.4 16.6 %collective-permute-start.14 = (bf16[2,64,1024]{2,1,0:T(8,128)(2,1)S(1)}, bf16[2,64,1024]{2,1,0:T(8,128)(2,1)S(1)}, u32[]{:S(2)}, u32[]{:S(2)}) collective-permute-start(bf16[2,64,1024]{2,1,0:T(8,128)(2,1)S(1)} %collective-permute-done.13), channel_id=1, source_target_pairs={{0,2},{1,3},{2,0},{3,1},{4,6},{5,7},{6,4},{7,5},{8,10},{9,11},{10,... | collective-permute-start | bytes 786440 | tf_op jit(solution)/shard_map/ppermute | solution.py:497
  34.0 15.7 %collective-permute-start.8 = (bf16[40,1536]{1,0:T(8,128)(2,1)S(1)}, bf16[40,1536]{1,0:T(8,128)(2,1)S(1)}, u32[]{:S(2)}, u32[]{:S(2)}) collective-permute-start(bf16[40,1536]{1,0:T(8,128)(2,1)S(1)} %fusion), channel_id=1, source_target_pairs={{0,8},{1,9},{2,10},{3,11},{4,12},{5,13},{6,14},{7,15},{8,0},{9,1},... | collective-permute-start | bytes 368648 | tf_op jit(solution)/shard_map/ppermute | solution.py:497
  34.1 15.8 %copy-start.4 = (bf16[256,1024]{1,0:T(8,128)(2,1)S(1)}, bf16[256,1024]{1,0:T(8,128)(2,1)}, u32[]{:S(2)}) copy-start(bf16[256,1024]{1,0:T(8,128)(2,1)} %text_ref.1) | copy-start | bytes 1572868
  49.1 0.9 %copy-start = (bf16[32,2048]{1,0:T(8,128)(2,1)S(1)}, bf16[32,2048]{1,0:T(8,128)(2,1)}, u32[]{:S(2)}) copy-start(bf16[32,2048]{1,0:T(8,128)(2,1)} %embed_ref.7) | copy-start | bytes 393220
  49.1 0.9 %copy-start.2 = (f32[2048]{0:T(1024)S(1)}, f32[2048]{0:T(1024)}, u32[]{:S(2)}) copy-start(f32[2048]{0:T(1024)} %param.29) | copy-start | bytes 24580
  49.1 13.2 %collective-permute-start.15 = (bf16[4,64,1024]{2,1,0:T(8,128)(2,1)S(1)}, bf16[4,64,1024]{2,1,0:T(8,128)(2,1)S(1)}, u32[]{:S(2)}, u32[]{:S(2)}) collective-permute-start(bf16[4,64,1024]{2,1,0:T(8,128)(2,1)S(1)} %constant_dynamic-update-slice_fusion.own_second_ref), channel_id=1, source_target_pairs={{0,16},{1,17},{2,18},{3,19},{4,20},{5,21},{6,22},{7,23},{8,24},{9,... | collective-permute-start | bytes 1572872 | tf_op jit(solution)/shard_map/ppermute | solution.py:497
  49.8 12.5 %collective-permute-start.9 = (f32[40,1536]{1,0:T(8,128)S(1)}, f32[40,1536]{1,0:T(8,128)S(1)}, u32[]{:S(2)}, u32[]{:S(2)}) collective-permute-start(f32[40,1536]{1,0:T(8,128)S(1)} %convert_add_fusion.kept_any), channel_id=1, source_target_pairs={{0,1},{1,0},{2,3},{3,2},{4,5},{5,4},{6,7},{7,6},{8,9},{9,8},{10,11... | collective-permute-start | bytes 737288 | tf_op jit(solution)/shard_map/ppermute | solution.py:497
  50.6 11.7 %copy-start.5 = (bf16[256,1024]{1,0:T(8,128)(2,1)S(1)}, bf16[256,1024]{1,0:T(8,128)(2,1)}, u32[]{:S(2)}) copy-start(bf16[256,1024]{1,0:T(8,128)(2,1)} %text_values_ref.1) | copy-start | bytes 1572868
  53.5 16.3 %collective-permute-start.18 = (bf16[4,64,1024]{2,1,0:T(8,128)(2,1)S(1)}, bf16[4,64,1024]{2,1,0:T(8,128)(2,1)S(1)}, u32[]{:S(2)}, u32[]{:S(2)}) collective-permute-start(bf16[4,64,1024]{2,1,0:T(8,128)(2,1)S(1)} %pad_maximum_fusion.own_first_ref), channel_id=1, source_target_pairs={{0,1},{1,0},{2,3},{3,2},{4,5},{5,4},{6,7},{7,6},{8,9},{9,8},{10,11... | collective-permute-start | bytes 1572872 | tf_op jit(solution)/shard_map/ppermute | solution.py:497
  54.0 15.8 %collective-permute-start.19 = (bf16[4,64,1024]{2,1,0:T(8,128)(2,1)S(1)}, bf16[4,64,1024]{2,1,0:T(8,128)(2,1)S(1)}, u32[]{:S(2)}, u32[]{:S(2)}) collective-permute-start(bf16[4,64,1024]{2,1,0:T(8,128)(2,1)S(1)} %constant_dynamic-update-slice_fusion.own_second_ref), channel_id=1, source_target_pairs={{0,1},{1,0},{2,3},{3,2},{4,5},{5,4},{6,7},{7,6},{8,9},{9,8},{10,11... | collective-permute-start | bytes 1572872 | tf_op jit(solution)/shard_map/ppermute | solution.py:497
  54.1 17.4 %collective-permute-start.16 = (bf16[4,64,1024]{2,1,0:T(8,128)(2,1)S(1)}, bf16[4,64,1024]{2,1,0:T(8,128)(2,1)S(1)}, u32[]{:S(2)}, u32[]{:S(2)}) collective-permute-start(bf16[4,64,1024]{2,1,0:T(8,128)(2,1)S(1)} %collective-permute-done.12.own_first_ref), channel_id=1, source_target_pairs={{0,1},{1,0},{2,3},{3,2},{4,5},{5,4},{6,7},{7,6},{8,9},{9,8},{10,11... | collective-permute-start | bytes 1572872 | tf_op jit(solution)/shard_map/ppermute | solution.py:497
  62.3 9.3 %collective-permute-start.17 = (bf16[4,64,1024]{2,1,0:T(8,128)(2,1)S(1)}, bf16[4,64,1024]{2,1,0:T(8,128)(2,1)S(1)}, u32[]{:S(2)}, u32[]{:S(2)}) collective-permute-start(bf16[4,64,1024]{2,1,0:T(8,128)(2,1)S(1)} %collective-permute-done.15.own_second_ref), channel_id=1, source_target_pairs={{0,1},{1,0},{2,3},{3,2},{4,5},{5,4},{6,7},{7,6},{8,9},{9,8},{10,11... | collective-permute-start | bytes 1572872 | tf_op jit(solution)/shard_map/ppermute | solution.py:497
  63.0 6.8 %copy-start.1 = (f32[3,2048]{1,0:T(4,128)S(1)}, f32[3,2048]{1,0:T(4,128)}, u32[]{:S(2)}) copy-start(f32[3,2048]{1,0:T(4,128)} %mod_ref.5) | copy-start | bytes 73732
  (4 other events, 2.9 us)

commit v3 on v2

--- a/solution.py
+++ b/solution.py
@@ -107,7 +107,13 @@
     keep_ref[...] = part(core)
 
 
-def velocity_kernel(hidden_ref, mod_ref, weight_ref, out_ref):
+def velocity_kernel(
+    hidden_ref, mod_ref, weight_ref, shift_ref, key_gain_ref, query_gain_ref, out_ref, small_ref
+):
+    small_ref[...] = jnp.zeros_like(small_ref)
+    small_ref[0:1, 0 : shift_ref.shape[1]] = shift_ref[...]
+    small_ref[1:2, :] = key_gain_ref[...]
+    small_ref[2:3, :] = query_gain_ref[...]
     values = hidden_ref[...].astype(f32)
     width = values.shape[1]
     centred = values - jnp.sum(values, -1, keepdims=True) * (1.0 / width)
@@ -120,10 +126,24 @@
 
 
 def guide_kernel(
-    rows, step_ref, slot_ref, table_ref, latent_ref, own_any, other_any, guided_ref, next_ref,
-    own_ref, other_ref, sems,
+    rows,
+    table_ref,
+    latent_ref,
+    step_any,
+    slot_any,
+    own_any,
+    other_any,
+    guided_ref,
+    next_ref,
+    step_ref,
+    slot_ref,
+    own_ref,
+    other_ref,
+    sems,
 ):
-    fetch([(own_any, own_ref), (other_any, other_ref)], sems)
+    fetch(
+        [(step_any, step_ref), (slot_any, slot_ref), (own_any, own_ref), (other_any, other_ref)], sems
+    )
     branch = lax.axis_index("cfg")
     own = own_ref[...]
     other = other_ref[...]
@@ -146,15 +166,15 @@
     slots = lax.broadcasted_iota(jnp.int32, table.shape, 0) * table.shape[
         1
     ] + lax.broadcasted_iota(jnp.int32, table.shape, 1)
-    picked = jnp.where(slots == slot_ref[...], table, 0.0)
+    picked = jnp.where(slots == slot_ref[0], table, 0.0)
     guidance = jnp.sum(jnp.sum(picked, 0, keepdims=True), 1, keepdims=True)
     guided = unconditional + guidance * (conditional - unconditional)
 
     def sigma(step):
-        fraction = 1.0 - step.astype(f32) / STEPS
+        fraction = 1.0 - jnp.full((1, 1), step, jnp.int32).astype(f32) / STEPS
         return flow_shift * fraction / (1.0 + (flow_shift - 1.0) * fraction)
 
-    change = sigma(step_ref[...] + 1) - sigma(step_ref[...])
+    change = sigma(step_ref[0] + 1) - sigma(step_ref[0])
     next_ref[...] = latent + change * guided
     guided_ref[...] = exact(belongs, jnp.where(slot, exact(guided, repeat, (0, 0)), 0.0), (1, 0))
 
@@ -162,11 +182,10 @@
 def fine_kernel(
     cells,
     taps_ref,
-    shift_ref,
+    small_ref,
     embed_ref,
     bias_ref,
     text_ref,
-    gain_ref,
     near_any,
     own_any,
     far_any,
@@ -185,7 +204,7 @@
     channels, own_lanes = own_ref.shape
     rows = own_lanes // cells
     lanes = (rows + 2) * cells
-    gain = gain_ref[...]
+    gain = small_ref[1:2, :]
     head = gain.shape[1]
     for h in range(text_ref.shape[1] // head):
         part = text_ref[:, h * head : (h + 1) * head].astype(f32)
@@ -217,7 +236,7 @@
     same = lax.broadcasted_iota(jnp.int32, (channels, channels), 0) == lax.broadcasted_iota(
         jnp.int32, (channels, channels), 1
     )
-    shift = jnp.sum(jnp.where(same, shift_ref[...], 0.0), 1, keepdims=True)
+    shift = jnp.sum(jnp.where(same, small_ref[0:1, :channels], 0.0), 1, keepdims=True)
 
     def tap(r, s):
         first = (3 * r + s) * channels
@@ -297,27 +316,27 @@
 def attend_kernel(
     rows,
     window,
-    length_ref,
     keys_ref,
     keys_t_ref,
     query_ref,
-    query_gain_ref,
-    key_gain_ref,
+    small_ref,
     text_ref,
     text_values_ref,
+    length_any,
     kept_any,
     other_any,
     out_ref,
     mix_ref,
     value_ref,
     gain_ref,
+    length_ref,
     kept_ref,
     other_ref,
     sems,
 ):
     step = pl.program_id(0)
     seq_index = lax.axis_index("seq")
-    head = query_gain_ref.shape[1]
+    head = small_ref.shape[1]
     half = kept_ref.shape[1]
     key_count = keys_ref.shape[0]
     text_count, span = text_ref.shape
@@ -328,12 +347,12 @@
     key_row = lax.broadcasted_iota(jnp.int32, (key_count, head), 0)
     allowed = (low_ok | (key_row >= window)) & (high_ok | (key_row < key_count - window))
     text_row = lax.broadcasted_iota(jnp.int32, (text_count, head), 0)
-    text_allowed = text_row < length_ref[...]
     text_rows = slice(key_count, key_count + text_count)
 
     @pl.when(step == 0)
     def _():
-        fetch([(kept_any, kept_ref), (other_any, other_ref)], sems)
+        fetch([(length_any, length_ref), (kept_any, kept_ref), (other_any, other_ref)], sems)
+        text_allowed = text_row < length_ref[0]
         core = seq_index % 2
         mix_ref[...] = jnp.zeros_like(mix_ref)
         for side, part_ref in ((core, kept_ref), (1 - core, other_ref)):
@@ -350,8 +369,10 @@
         same = lax.broadcasted_iota(jnp.int32, (head, head), 0) == lax.broadcasted_iota(
             jnp.int32, (head, head), 1
         )
-        column = jnp.sum(jnp.where(same, key_gain_ref[...], 0.0), 1, keepdims=True)
+        column = jnp.sum(jnp.where(same, small_ref[1:2, :], 0.0), 1, keepdims=True)
         gain_ref[...] = jnp.broadcast_to(column, gain_ref.shape)
+
+    text_allowed = text_row < length_ref[0]
 
     def columns(which):
         return pl.ds(pl.multiple_of(which * inner + step * span, 128), span)
@@ -365,7 +386,7 @@
         mine = slice(i * head, (i + 1) * head)
         query = queries[:, mine]
         mean = jnp.sum(query * query, -1, keepdims=True) * (1.0 / head)
-        query = (query * lax.rsqrt(mean + epsilon) * query_gain_ref[...]).astype(bf16)
+        query = (query * lax.rsqrt(mean + epsilon) * small_ref[2:3, :]).astype(bf16)
         keys = all_keys[mine]
         mean = jnp.sum(keys * keys, 0, keepdims=True) * (1.0 / head)
         keys = (keys * lax.rsqrt(mean + epsilon) * gain_ref[:, 0:1]).astype(bf16)
@@ -510,15 +531,25 @@
     )(embed_weight, bias_row, fine_modulation, project_weight)
     met = swap(sent, across)
 
-    velocity = pl.pallas_call(
+    velocity, small = pl.pallas_call(
         velocity_kernel,
-        out_shape=jax.ShapeDtypeStruct((channels, own), f32),
-        in_specs=vmem(3),
-        out_specs=vmem(1)[0],
+        out_shape=(
+            jax.ShapeDtypeStruct((channels, own), f32),
+            jax.ShapeDtypeStruct((8, head), f32),
+        ),
+        in_specs=vmem(6),
+        out_specs=tuple(vmem(2)),
         cost_estimate=cost(2e9, 1e6),
         name="velocity",
         compiler_params=pltpu.CompilerParams(vmem_limit_bytes=6 << 20),
-    )(coarse_hidden.reshape(own, width), coarse_modulation[0], final_weight.T)
+    )(
+        coarse_hidden.reshape(own, width),
+        coarse_modulation[0],
+        final_weight.T,
+        upsample_bias.reshape(1, channels),
+        key_gain.reshape(1, head),
+        query_gain.reshape(1, head),
+    )
     partner = swap(velocity, ("cfg", 0))
 
     held = output_weight.T[None]
@@ -546,17 +577,19 @@
             jax.ShapeDtypeStruct((lines, 128), f32),
             jax.ShapeDtypeStruct((channels, own), f32),
         ),
-        in_specs=vmem(4) + anywhere(2),
+        in_specs=vmem(2) + anywhere(4),
         out_specs=tuple(vmem(2)),
-        scratch_shapes=[pltpu.VMEM((channels, own), f32)] * 2 + [pltpu.SemaphoreType.DMA((2,))],
+        scratch_shapes=[pltpu.SMEM((1,), jnp.int32)] * 2
+        + [pltpu.VMEM((channels, own), f32)] * 2
+        + [pltpu.SemaphoreType.DMA((4,))],
         cost_estimate=cost(1e9, 1e5),
         name="guide",
         compiler_params=pltpu.CompilerParams(vmem_limit_bytes=2 << 20),
     )(
-        step_index.reshape(1, 1),
-        guide_index.reshape(1, 1),
         guide_scales.reshape(-1, 128),
         latent,
+        step_index,
+        guide_index,
         velocity,
         partner,
     )
@@ -576,7 +609,7 @@
             jax.ShapeDtypeStruct((channels, fine_tokens), bf16),
             jax.ShapeDtypeStruct(text_keys.shape, bf16),
         ),
-        in_specs=vmem(6) + anywhere(3),
+        in_specs=vmem(5) + anywhere(3),
         out_specs=tuple(vmem(6)),
         scratch_shapes=[pltpu.VMEM((channels, own), f32)] * 3 + [pltpu.SemaphoreType.DMA((3,))],
         cost_estimate=cost(4e9, 4e6),
@@ -584,11 +617,10 @@
         compiler_params=pltpu.CompilerParams(vmem_limit_bytes=20 << 20),
     )(
         upsample_weight.T,
-        upsample_bias.reshape(1, channels),
+        small,
         embed_weight,
         bias_row,
         text_keys,
-        key_gain.reshape(1, head),
         near_rows,
         stepped,
         far_rows,
@@ -616,28 +648,28 @@
         functools.partial(attend_kernel, rows, 4 * cells),
         grid=(inner // span,),
         out_shape=jax.ShapeDtypeStruct((fine_tokens, inner), bf16),
-        in_specs=[whole] * 6 + [per_step, per_step, free, free],
+        in_specs=[whole] * 4 + [per_step, per_step, free, free, free],
         out_specs=pl.BlockSpec((fine_tokens, span), lambda h: (0, h)),
         scratch_shapes=[
             pltpu.VMEM((DEPTH, 3 * inner), bf16),
             pltpu.VMEM((2, key_count + text_count, 2 * head), bf16),
             pltpu.VMEM((head, 128), f32),
+            pltpu.SMEM((1,), jnp.int32),
             pltpu.VMEM((TERMS, half), f32),
             pltpu.VMEM((TERMS, half), f32),
-            pltpu.SemaphoreType.DMA((2,)),
+            pltpu.SemaphoreType.DMA((3,)),
         ],
         cost_estimate=cost(8e9, 4e6),
         name="attend",
         compiler_params=pltpu.CompilerParams(vmem_limit_bytes=24 << 20),
     )(
-        text_length.reshape(1, 1),
         keys,
         keys_t,
         query,
-        query_gain.reshape(1, head),
-        key_gain.reshape(1, head),
+        small,
         text_normed,
         text_values,
+        text_length,
         total,
         others,
     )

time: 73.5 us -> 73.7 us (level)
  transfers between devices with their start and end apart: 20 -> 20, of which waited for: 5 -> 5; matrix products, arithmetic and copies ran while one was open for 0% -> 0% of each run, Pallas kernels for 18% -> 19%
where the time goes in v3:
time: 73.7 us; the launch traced here: 73.5 us
  waiting for transfers between devices  31.7 us (43%)
  starting transfers between devices  20.1 us (27%)
  Pallas kernels  17.6 us (24%)
  between operations  2.89 us (4%)
  local copies, waits for them, and re-layouts  0.88 us (1%)
    ppermute x19, waiting for transfers between devices, swap(): lax.ppermute(value, ('cfg', 'seq'), [(i, i ^ flip) for i in range(size)])  31.7 us
    ppermute x19, starting transfers between devices, swap(): lax.ppermute(value, ('cfg', 'seq'), [(i, i ^ flip) for i in range(size)])  19.5 us
    pallas_call x1, Pallas kernels, per_device(): pl.pallas_call(functools.partial(attend_kernel, rows, 4 * cells), grid=(i...  6.6 us
    pallas_call x2, Pallas kernels, output(): pl.pallas_call(functools.partial(output_kernel, tuple(levels), last), out...  3.43 us
    pallas_call x1, Pallas kernels, per_device(): pl.pallas_call(functools.partial(fine_kernel, cells), out_shape=(jax.Shap...  2.93 us
    pallas_call x1, Pallas kernels, per_device(): pl.pallas_call(functools.partial(partial_kernel, seq_count), out_shape=(j...  2.29 us
    pallas_call x1, Pallas kernels, per_device(): pl.pallas_call(functools.partial(guide_kernel, rows), out_shape=(jax.Shap...  1.8 us
  transfers between devices with their start and end apart: 20, of which 5 were waited for; matrix products, arithmetic and copies ran while one was open for 0% of the time, Pallas kernels for 19%

profile of v3, /device:TPU:0, one launch (start us, length us, event | category | flops | bytes accessed | tf_op | source)
XLA Modules:
  0.0 73.5 jit_solution(8355786882525714977)
XLA Ops:
  0.7 2.3 %partial_mix.1 = (f32[40,1536]{1,0:T(8,128)}, f32[40,1536]{1,0:T(8,128)}) custom-call(bf16[32,2048]{1,0:T(8,128)(2,1)} %embed_ref.7, f32[1,2048]{1,0:T(1,128)} %bitcast.26, f32[3,2048]{1,0:T(4,128)} %mod_ref.5, bf16[64,3072]{1,0:T(8,128)(2,1)} %weight_ref.1), custom_call_target="tpu_custom_call" | custom-call | flops 2000000000 | bytes 1000000 | tf_op jit(solution)/shard_map/partial_mix/pallas_call | solution.py:524
  3.0 0.5 collective-permute-start.3
  3.5 0.6 copy-done.11
  4.1 0.6 velocity.1
  4.7 2.5 %collective-permute-start = (f32[32,128]{1,0:T(8,128)S(1)}, f32[32,128]{1,0:T(8,128)S(1)}, u32[]{:S(2)}, u32[]{:S(2)}) collective-permute-start(f32[32,128]{1,0:T(8,128)S(1)} %get-tuple-element.15.own_any), channel_id=1, source_target_pairs={{0,16},{1,17},{2,18},{3,19},{4,20},{5,21},{6,22},{7,23},{8,24},{9,... | collective-permute-start | bytes 49160 | tf_op jit(solution)/shard_map/ppermute | solution.py:518
  7.2 1.6 %collective-permute-start.10 = (bf16[1,64,1024]{2,1,0:T(8,128)(2,1)S(1)}, bf16[1,64,1024]{2,1,0:T(8,128)(2,1)S(1)}, u32[]{:S(2)}, u32[]{:S(2)}) collective-permute-start(bf16[1,64,1024]{2,1,0:T(8,128)(2,1)S(1)} %bitcast.40), channel_id=1, source_target_pairs={{0,4},{1,5},{2,6},{3,7},{4,0},{5,1},{6,2},{7,3},{8,12},{9,13},{10,... | collective-permute-start | bytes 393224 | tf_op jit(solution)/shard_map/ppermute | solution.py:518
  10.8 0.6 collective-permute-start.4
  11.4 1.5 %collective-permute-start.5 = (bf16[40,1536]{1,0:T(8,128)(2,1)S(1)}, bf16[40,1536]{1,0:T(8,128)(2,1)S(1)}, u32[]{:S(2)}, u32[]{:S(2)}) collective-permute-start(bf16[40,1536]{1,0:T(8,128)(2,1)S(1)} %get-tuple-element.32), channel_id=1, source_target_pairs={{0,2},{1,3},{2,0},{3,1},{4,6},{5,7},{6,4},{7,5},{8,10},{9,11},{10,... | collective-permute-start | bytes 368648 | tf_op jit(solution)/shard_map/ppermute | solution.py:518
  13.0 1.4 %collective-permute-start.6 = (bf16[40,1536]{1,0:T(8,128)(2,1)S(1)}, bf16[40,1536]{1,0:T(8,128)(2,1)S(1)}, u32[]{:S(2)}, u32[]{:S(2)}) collective-permute-start(bf16[40,1536]{1,0:T(8,128)(2,1)S(1)} %get-tuple-element.32), channel_id=1, source_target_pairs={{0,18},{1,19},{2,16},{3,17},{4,22},{5,23},{6,20},{7,21},{8,26},{9,... | collective-permute-start | bytes 368648 | tf_op jit(solution)/shard_map/ppermute | solution.py:518
  14.4 1.8 %guide.1 = (f32[32,128]{1,0:T(8,128)}, f32[32,128]{1,0:T(8,128)S(1)}) custom-call(f32[32,128]{1,0:T(8,128)S(1)} %bitcast.34, f32[32,128]{1,0:T(8,128)S(1)} %bitcast.35, s32[1]{0:T(128)S(6)} %copy.29.step_any, s32[1]{0:T(128)S(6)} %copy.30.slot_any, f32[32,128]{1,0:T(8,128)S(1)} %get-tuple-element.15.own_any, f32[32,128]{1,0:T(8,128)S(1)} %collective-permute-done.other_any), custom_call_target="tpu_custom_call" | custom-call | flops 1000000000 | bytes 100000 | tf_op jit(solution)/shard_map/guide/pallas_call | solution.py:574
  16.2 0.1 collective-permute-start.1
  16.3 0.7 collective-permute-start.2
  17.0 0.1 collective-permute-done.4
  17.1 4.2 %collective-permute-start.13 = (bf16[2,64,1024]{2,1,0:T(8,128)(2,1)S(1)}, bf16[2,64,1024]{2,1,0:T(8,128)(2,1)S(1)}, u32[]{:S(2)}, u32[]{:S(2)}) collective-permute-start(bf16[2,64,1024]{2,1,0:T(8,128)(2,1)S(1)} %pad_maximum_fusion.1), channel_id=1, source_target_pairs={{0,8},{1,9},{2,10},{3,11},{4,12},{5,13},{6,14},{7,15},{8,0},{9,1},... | collective-permute-start | bytes 786440 | tf_op jit(solution)/shard_map/ppermute | solution.py:518
  21.3 0.5 collective-permute-start.11
  21.9 2.8 %collective-permute-start.7 = (bf16[40,1536]{1,0:T(8,128)(2,1)S(1)}, bf16[40,1536]{1,0:T(8,128)(2,1)S(1)}, u32[]{:S(2)}, u32[]{:S(2)}) collective-permute-start(bf16[40,1536]{1,0:T(8,128)(2,1)S(1)} %get-tuple-element.30), channel_id=1, source_target_pairs={{0,4},{1,5},{2,6},{3,7},{4,0},{5,1},{6,2},{7,3},{8,12},{9,13},{10,... | collective-permute-start | bytes 368648 | tf_op jit(solution)/shard_map/ppermute | solution.py:518
  24.7 5.8 %collective-permute-done.11 = bf16[2,64,1024]{2,1,0:T(8,128)(2,1)S(1)} collective-permute-done((bf16[2,64,1024]{2,1,0:T(8,128)(2,1)S(1)}, bf16[2,64,1024]{2,1,0:T(8,128)(2,1)S(1)}, u32[]{:S(2)}, u32[]{:S(2)}) %collective-permute-start.11) | collective-permute-done | bytes 262176 | tf_op jit(solution)/shard_map/ppermute | solution.py:518
  30.5 0.5 collective-permute-start.12
  31.0 2.5 %collective-permute-done.13 = bf16[2,64,1024]{2,1,0:T(8,128)(2,1)S(1)} collective-permute-done((bf16[2,64,1024]{2,1,0:T(8,128)(2,1)S(1)}, bf16[2,64,1024]{2,1,0:T(8,128)(2,1)S(1)}, u32[]{:S(2)}, u32[]{:S(2)}) %collective-permute-start.13) | collective-permute-done | bytes 262176 | tf_op jit(solution)/shard_map/ppermute | solution.py:518
  33.5 1.6 %collective-permute-start.14 = (bf16[2,64,1024]{2,1,0:T(8,128)(2,1)S(1)}, bf16[2,64,1024]{2,1,0:T(8,128)(2,1)S(1)}, u32[]{:S(2)}, u32[]{:S(2)}) collective-permute-start(bf16[2,64,1024]{2,1,0:T(8,128)(2,1)S(1)} %collective-permute-done.13), channel_id=1, source_target_pairs={{0,2},{1,3},{2,0},{3,1},{4,6},{5,7},{6,4},{7,5},{8,10},{9,11},{10,... | collective-permute-start | bytes 786440 | tf_op jit(solution)/shard_map/ppermute | solution.py:518
  35.1 0.1 collective-permute-start.8
  35.3 14.9 %collective-permute-done.14 = bf16[2,64,1024]{2,1,0:T(8,128)(2,1)S(1)} collective-permute-done((bf16[2,64,1024]{2,1,0:T(8,128)(2,1)S(1)}, bf16[2,64,1024]{2,1,0:T(8,128)(2,1)S(1)}, u32[]{:S(2)}, u32[]{:S(2)}) %collective-permute-start.14) | collective-permute-done | bytes 262176 | tf_op jit(solution)/shard_map/ppermute | solution.py:518
  50.2 0.6 collective-permute-start.15
  51.0 0.1 copy-done
  51.1 2.9 %fine_features.1 = (f32[64,128]{1,0:T(8,128)}, bf16[1024,256]{1,0:T(8,128)(2,1)S(1)}, bf16[256,1024]{1,0:T(8,128)(2,1)S(1)}, bf16[256,256]{1,0:T(8,128)(2,1)S(1)...) custom-call(f32[32,288]{1,0:T(8,128)S(1)} %bitcast.32, f32[8,128]{1,0:T(8,128)S(1)} %get-tuple-element.17.small_ref, ...), custom_call_target="tpu_custom_call" | custom-call | flops 4000000000 | bytes 4000000 | tf_op jit(solution)/shard_map/fine_features/pallas_call | solution.py:602
  54.0 0.5 collective-permute-start.18
  54.5 0.1 collective-permute-start.19
  54.6 0.4 collective-permute-start.16
  55.0 8.4 %collective-permute-done.15.own_second_ref = bf16[4,64,1024]{2,1,0:T(8,128)(2,1)S(1)} collective-permute-done((bf16[4,64,1024]{2,1,0:T(8,128)(2,1)S(1)}, bf16[4,64,1024]{2,1,0:T(8,128)(2,1)S(1)}, u32[]{:S(2)}, u32[]{:S(2)}) %collective-permute-start.15) | collective-permute-done | bytes 524320 | tf_op jit(solution)/shard_map/ppermute | solution.py:518
  63.4 6.6 %attend.1.attended_ref = bf16[256,1024]{1,0:T(8,128)(2,1)S(1)} custom-call(bf16[1024,256]{1,0:T(8,128)(2,1)S(1)} %get-tuple-element.20.keys_ref, bf16[256,1024]{1,0:T(8,128)(2,1)S(1)} %get-tuple-element.21.keys_t_ref, bf16[256,256]{1,0:T(8,128)(2,1)S(1)} %get-tuple-element.22.query_ref, f32[8,128]{1,0:T(8,128)S(1)} %get-tuple-element.17.small_ref, ...), custom_call_target="tpu_custom_call" | custom-call | flops 8000000000 | bytes 4000000 | tf_op jit(solution)/shard_map/attend/pallas_call | solution.py:647
  70.1 1.7 %shard_map.202.rest_0_ = bf16[256,2048]{1,0:T(8,128)(2,1)} custom-call(bf16[256,1024]{1,0:T(8,128)(2,1)S(1)} %attend.1.attended_ref, bf16[32,256]{1,0:T(8,128)(2,1)S(1)} %get-tuple-element.26.token_ref, bf16[32,2048]{1,0:T(8,128)(2,1)S(1)} %copy-done, f32[1,2048]{1,0:T(1,128)S(1)} %bitcast.28, f32[3,2048]{1,0:T(4,128)S(1)} %copy-done.1, ...), custom_call_target="tpu_custom_call" | custom-call | flops 1000000000 | bytes 3000000 | tf_op jit(solution)/shard_map/pallas_call | solution.py:682
  71.8 1.7 %shard_map.203 = bf16[256,2048]{1,0:T(8,128)(2,1)} custom-call(bf16[256,1024]{1,0:T(8,128)(2,1)S(1)} %attend.1.attended_ref, bf16[32,256]{1,0:T(8,128)(2,1)S(1)} %get-tuple-element.26.token_ref, bf16[32,2048]{1,0:T(8,128)(2,1)S(1)} %copy-done, f32[1,2048]{1,0:T(1,128)S(1)} %bitcast.29, f32[3,2048]{1,0:T(4,128)S(1)} %copy-done.1, ...), custom_call_target="tpu_custom_call", output_to_operand_aliasing={{}: (9, {})} | custom-call | flops 1000000000 | bytes 3000000 | tf_op jit(solution)/shard_map/pallas_call | solution.py:682
  (55 shorter events, 0.5 us)
Async XLA Ops:
  0.6 2.8 %copy-start.3 = (bf16[1,2,64,2048]{3,2,1,0:T(8,128)(2,1)S(1)}, bf16[1,2,64,2048]{3,2,1,0:T(8,128)(2,1)}, u32[]{:S(2)}) copy-start(bf16[1,2,64,2048]{3,2,1,0:T(8,128)(2,1)} %param.19) | copy-start | bytes 1572868
  0.6 2.8 %copy-start.6 = (bf16[2048,32]{0,1:T(8,128)(2,1)S(1)}, bf16[2048,32]{0,1:T(8,128)(2,1)}, u32[]{:S(2)}) copy-start(bf16[2048,32]{0,1:T(8,128)(2,1)} %param.21) | copy-start | bytes 393220
  0.7 2.8 %copy-start.8 = (f32[1,2,2048]{2,1,0:T(2,128)S(1)}, f32[1,2,2048]{2,1,0:T(2,128)}, u32[]{:S(2)}) copy-start(f32[1,2,2048]{2,1,0:T(2,128)} %param.20) | copy-start | bytes 49156
  3.0 7.8 %collective-permute-start.3 = (f32[40,1536]{1,0:T(8,128)}, f32[40,1536]{1,0:T(8,128)S(1)}, u32[]{:S(2)}, u32[]{:S(2)}) collective-permute-start(f32[40,1536]{1,0:T(8,128)} %get-tuple-element.25), channel_id=1, source_target_pairs={{0,1},{1,0},{2,3},{3,2},{4,5},{5,4},{6,7},{7,6},{8,9},{9,8},{10,11... | collective-permute-start | bytes 737288 | tf_op jit(solution)/shard_map/ppermute | solution.py:518
  4.1 3.1 %copy-start.14 = (bf16[1024,64]{0,1:T(8,128)(2,1)S(1)}, bf16[1024,64]{0,1:T(8,128)(2,1)}, u32[]{:S(2)}) copy-start(bf16[1024,64]{0,1:T(8,128)(2,1)} %param.37) | copy-start | bytes 393220
  4.1 6.6 %copy-start.15 = (f32[40,1536]{1,0:T(8,128)S(1)}, f32[40,1536]{1,0:T(8,128)}, u32[]{:S(2)}) copy-start(f32[40,1536]{1,0:T(8,128)} %get-tuple-element.24) | copy-start | bytes 737284
  4.7 9.7 %collective-permute-start = (f32[32,128]{1,0:T(8,128)S(1)}, f32[32,128]{1,0:T(8,128)S(1)}, u32[]{:S(2)}, u32[]{:S(2)}) collective-permute-start(f32[32,128]{1,0:T(8,128)S(1)} %get-tuple-element.15.own_any), channel_id=1, source_target_pairs={{0,16},{1,17},{2,18},{3,19},{4,20},{5,21},{6,22},{7,23},{8,24},{9,... | collective-permute-start | bytes 49160 | tf_op jit(solution)/shard_map/ppermute | solution.py:518
  7.2 9.1 %collective-permute-start.10 = (bf16[1,64,1024]{2,1,0:T(8,128)(2,1)S(1)}, bf16[1,64,1024]{2,1,0:T(8,128)(2,1)S(1)}, u32[]{:S(2)}, u32[]{:S(2)}) collective-permute-start(bf16[1,64,1024]{2,1,0:T(8,128)(2,1)S(1)} %bitcast.40), channel_id=1, source_target_pairs={{0,4},{1,5},{2,6},{3,7},{4,0},{5,1},{6,2},{7,3},{8,12},{9,13},{10,... | collective-permute-start | bytes 393224 | tf_op jit(solution)/shard_map/ppermute | solution.py:518
  10.8 3.6 %copy-start.9 = (f32[4096]{0:T(1024)S(1)}, f32[4096]{0:T(1024)}, u32[]{:S(2)}) copy-start(f32[4096]{0:T(1024)} %param.25) | copy-start | bytes 49156
  10.8 3.6 %copy-start.10 = (f32[2,2048]{1,0:T(2,128)S(1)}, f32[2,2048]{1,0:T(2,128)}, u32[]{:S(2)}) copy-start(f32[2,2048]{1,0:T(2,128)} %param.22) | copy-start | bytes 49156
  10.8 6.3 %collective-permute-start.4 = (bf16[40,1536]{1,0:T(8,128)(2,1)S(1)}, bf16[40,1536]{1,0:T(8,128)(2,1)S(1)}, u32[]{:S(2)}, u32[]{:S(2)}) collective-permute-start(bf16[40,1536]{1,0:T(8,128)(2,1)S(1)} %get-tuple-element.32), channel_id=1, source_target_pairs={{0,16},{1,17},{2,18},{3,19},{4,20},{5,21},{6,22},{7,23},{8,24},{9,... | collective-permute-start | bytes 368648 | tf_op jit(solution)/shard_map/ppermute | solution.py:518
  11.4 9.9 %collective-permute-start.5 = (bf16[40,1536]{1,0:T(8,128)(2,1)S(1)}, bf16[40,1536]{1,0:T(8,128)(2,1)S(1)}, u32[]{:S(2)}, u32[]{:S(2)}) collective-permute-start(bf16[40,1536]{1,0:T(8,128)(2,1)S(1)} %get-tuple-element.32), channel_id=1, source_target_pairs={{0,2},{1,3},{2,0},{3,1},{4,6},{5,7},{6,4},{7,5},{8,10},{9,11},{10,... | collective-permute-start | bytes 368648 | tf_op jit(solution)/shard_map/ppermute | solution.py:518
  13.0 8.9 %collective-permute-start.6 = (bf16[40,1536]{1,0:T(8,128)(2,1)S(1)}, bf16[40,1536]{1,0:T(8,128)(2,1)S(1)}, u32[]{:S(2)}, u32[]{:S(2)}) collective-permute-start(bf16[40,1536]{1,0:T(8,128)(2,1)S(1)} %get-tuple-element.32), channel_id=1, source_target_pairs={{0,18},{1,19},{2,16},{3,17},{4,22},{5,23},{6,20},{7,21},{8,26},{9,... | collective-permute-start | bytes 368648 | tf_op jit(solution)/shard_map/ppermute | solution.py:518
  16.2 34.7 %collective-permute-start.1 = (f32[32,128]{1,0:T(8,128)S(1)}, f32[32,128]{1,0:T(8,128)S(1)}, u32[]{:S(2)}, u32[]{:S(2)}) collective-permute-start(f32[32,128]{1,0:T(8,128)S(1)} %get-tuple-element.18.own_any), channel_id=1, source_target_pairs={{0,1},{1,0},{2,3},{3,2},{4,5},{5,4},{6,7},{7,6},{8,9},{9,8},{10,11... | collective-permute-start | bytes 49160 | tf_op jit(solution)/shard_map/ppermute | solution.py:518
  16.3 34.6 %collective-permute-start.2 = (f32[32,128]{1,0:T(8,128)S(1)}, f32[32,128]{1,0:T(8,128)S(1)}, u32[]{:S(2)}, u32[]{:S(2)}) collective-permute-start(f32[32,128]{1,0:T(8,128)S(1)} %get-tuple-element.18.own_any), channel_id=1, source_target_pairs={{1,2},{3,4},{5,6},{7,8},{9,10},{11,12},{13,14},{2,1},{4,3},{6,5},{... | collective-permute-start | bytes 49160 | tf_op jit(solution)/shard_map/ppermute | solution.py:600
  17.1 16.4 %collective-permute-start.13 = (bf16[2,64,1024]{2,1,0:T(8,128)(2,1)S(1)}, bf16[2,64,1024]{2,1,0:T(8,128)(2,1)S(1)}, u32[]{:S(2)}, u32[]{:S(2)}) collective-permute-start(bf16[2,64,1024]{2,1,0:T(8,128)(2,1)S(1)} %pad_maximum_fusion.1), channel_id=1, source_target_pairs={{0,8},{1,9},{2,10},{3,11},{4,12},{5,13},{6,14},{7,15},{8,0},{9,1},... | collective-permute-start | bytes 786440 | tf_op jit(solution)/shard_map/ppermute | solution.py:518
  21.3 9.2 %collective-permute-start.11 = (bf16[2,64,1024]{2,1,0:T(8,128)(2,1)S(1)}, bf16[2,64,1024]{2,1,0:T(8,128)(2,1)S(1)}, u32[]{:S(2)}, u32[]{:S(2)}) collective-permute-start(bf16[2,64,1024]{2,1,0:T(8,128)(2,1)S(1)} %pad_maximum_fusion.1), channel_id=1, source_target_pairs={{0,16},{1,17},{2,18},{3,19},{4,20},{5,21},{6,22},{7,23},{8,24},{9,... | collective-permute-start | bytes 786440 | tf_op jit(solution)/shard_map/ppermute | solution.py:518
  21.9 13.2 %collective-permute-start.7 = (bf16[40,1536]{1,0:T(8,128)(2,1)S(1)}, bf16[40,1536]{1,0:T(8,128)(2,1)S(1)}, u32[]{:S(2)}, u32[]{:S(2)}) collective-permute-start(bf16[40,1536]{1,0:T(8,128)(2,1)S(1)} %get-tuple-element.30), channel_id=1, source_target_pairs={{0,4},{1,5},{2,6},{3,7},{4,0},{5,1},{6,2},{7,3},{8,12},{9,13},{10,... | collective-permute-start | bytes 368648 | tf_op jit(solution)/shard_map/ppermute | solution.py:518
  30.5 24.1 %collective-permute-start.12 = (bf16[4,64,1024]{2,1,0:T(8,128)(2,1)S(1)}, bf16[4,64,1024]{2,1,0:T(8,128)(2,1)S(1)}, u32[]{:S(2)}, u32[]{:S(2)}) collective-permute-start(bf16[4,64,1024]{2,1,0:T(8,128)(2,1)S(1)} %pad_maximum_fusion.own_first_ref), channel_id=1, source_target_pairs={{0,2},{1,3},{2,0},{3,1},{4,6},{5,7},{6,4},{7,5},{8,10},{9,11},{10,... | collective-permute-start | bytes 1572872 | tf_op jit(solution)/shard_map/ppermute | solution.py:518
  33.5 16.6 %collective-permute-start.14 = (bf16[2,64,1024]{2,1,0:T(8,128)(2,1)S(1)}, bf16[2,64,1024]{2,1,0:T(8,128)(2,1)S(1)}, u32[]{:S(2)}, u32[]{:S(2)}) collective-permute-start(bf16[2,64,1024]{2,1,0:T(8,128)(2,1)S(1)} %collective-permute-done.13), channel_id=1, source_target_pairs={{0,2},{1,3},{2,0},{3,1},{4,6},{5,7},{6,4},{7,5},{8,10},{9,11},{10,... | collective-permute-start | bytes 786440 | tf_op jit(solution)/shard_map/ppermute | solution.py:518
  35.1 15.7 %collective-permute-start.8 = (bf16[40,1536]{1,0:T(8,128)(2,1)S(1)}, bf16[40,1536]{1,0:T(8,128)(2,1)S(1)}, u32[]{:S(2)}, u32[]{:S(2)}) collective-permute-start(bf16[40,1536]{1,0:T(8,128)(2,1)S(1)} %fusion), channel_id=1, source_target_pairs={{0,8},{1,9},{2,10},{3,11},{4,12},{5,13},{6,14},{7,15},{8,0},{9,1},... | collective-permute-start | bytes 368648 | tf_op jit(solution)/shard_map/ppermute | solution.py:518
  35.2 15.7 %copy-start.4 = (bf16[256,1024]{1,0:T(8,128)(2,1)S(1)}, bf16[256,1024]{1,0:T(8,128)(2,1)}, u32[]{:S(2)}) copy-start(bf16[256,1024]{1,0:T(8,128)(2,1)} %text_ref.1) | copy-start | bytes 1572868
  50.2 0.9 %copy-start = (bf16[32,2048]{1,0:T(8,128)(2,1)S(1)}, bf16[32,2048]{1,0:T(8,128)(2,1)}, u32[]{:S(2)}) copy-start(bf16[32,2048]{1,0:T(8,128)(2,1)} %embed_ref.7) | copy-start | bytes 393220
  50.2 0.9 %copy-start.2 = (f32[2048]{0:T(1024)S(1)}, f32[2048]{0:T(1024)}, u32[]{:S(2)}) copy-start(f32[2048]{0:T(1024)} %param.29) | copy-start | bytes 24580
  50.2 13.2 %collective-permute-start.15 = (bf16[4,64,1024]{2,1,0:T(8,128)(2,1)S(1)}, bf16[4,64,1024]{2,1,0:T(8,128)(2,1)S(1)}, u32[]{:S(2)}, u32[]{:S(2)}) collective-permute-start(bf16[4,64,1024]{2,1,0:T(8,128)(2,1)S(1)} %constant_dynamic-update-slice_fusion.own_second_ref), channel_id=1, source_target_pairs={{0,16},{1,17},{2,18},{3,19},{4,20},{5,21},{6,22},{7,23},{8,24},{9,... | collective-permute-start | bytes 1572872 | tf_op jit(solution)/shard_map/ppermute | solution.py:518
  50.9 12.5 %collective-permute-start.9 = (f32[40,1536]{1,0:T(8,128)S(1)}, f32[40,1536]{1,0:T(8,128)S(1)}, u32[]{:S(2)}, u32[]{:S(2)}) collective-permute-start(f32[40,1536]{1,0:T(8,128)S(1)} %convert_add_fusion.kept_any), channel_id=1, source_target_pairs={{0,1},{1,0},{2,3},{3,2},{4,5},{5,4},{6,7},{7,6},{8,9},{9,8},{10,11... | collective-permute-start | bytes 737288 | tf_op jit(solution)/shard_map/ppermute | solution.py:518
  51.1 12.3 %copy-start.5 = (bf16[256,1024]{1,0:T(8,128)(2,1)S(1)}, bf16[256,1024]{1,0:T(8,128)(2,1)}, u32[]{:S(2)}) copy-start(bf16[256,1024]{1,0:T(8,128)(2,1)} %text_values_ref.1) | copy-start | bytes 1572868
  54.0 16.0 %collective-permute-start.18 = (bf16[4,64,1024]{2,1,0:T(8,128)(2,1)S(1)}, bf16[4,64,1024]{2,1,0:T(8,128)(2,1)S(1)}, u32[]{:S(2)}, u32[]{:S(2)}) collective-permute-start(bf16[4,64,1024]{2,1,0:T(8,128)(2,1)S(1)} %pad_maximum_fusion.own_first_ref), channel_id=1, source_target_pairs={{0,1},{1,0},{2,3},{3,2},{4,5},{5,4},{6,7},{7,6},{8,9},{9,8},{10,11... | collective-permute-start | bytes 1572872 | tf_op jit(solution)/shard_map/ppermute | solution.py:518
  54.5 15.5 %collective-permute-start.19 = (bf16[4,64,1024]{2,1,0:T(8,128)(2,1)S(1)}, bf16[4,64,1024]{2,1,0:T(8,128)(2,1)S(1)}, u32[]{:S(2)}, u32[]{:S(2)}) collective-permute-start(bf16[4,64,1024]{2,1,0:T(8,128)(2,1)S(1)} %constant_dynamic-update-slice_fusion.own_second_ref), channel_id=1, source_target_pairs={{0,1},{1,0},{2,3},{3,2},{4,5},{5,4},{6,7},{7,6},{8,9},{9,8},{10,11... | collective-permute-start | bytes 1572872 | tf_op jit(solution)/shard_map/ppermute | solution.py:518
  54.6 17.2 %collective-permute-start.16 = (bf16[4,64,1024]{2,1,0:T(8,128)(2,1)S(1)}, bf16[4,64,1024]{2,1,0:T(8,128)(2,1)S(1)}, u32[]{:S(2)}, u32[]{:S(2)}) collective-permute-start(bf16[4,64,1024]{2,1,0:T(8,128)(2,1)S(1)} %collective-permute-done.12.own_first_ref), channel_id=1, source_target_pairs={{0,1},{1,0},{2,3},{3,2},{4,5},{5,4},{6,7},{7,6},{8,9},{9,8},{10,11... | collective-permute-start | bytes 1572872 | tf_op jit(solution)/shard_map/ppermute | solution.py:518
  63.4 8.4 %collective-permute-start.17 = (bf16[4,64,1024]{2,1,0:T(8,128)(2,1)S(1)}, bf16[4,64,1024]{2,1,0:T(8,128)(2,1)S(1)}, u32[]{:S(2)}, u32[]{:S(2)}) collective-permute-start(bf16[4,64,1024]{2,1,0:T(8,128)(2,1)S(1)} %collective-permute-done.15.own_second_ref), channel_id=1, source_target_pairs={{0,1},{1,0},{2,3},{3,2},{4,5},{5,4},{6,7},{7,6},{8,9},{9,8},{10,11... | collective-permute-start | bytes 1572872 | tf_op jit(solution)/shard_map/ppermute | solution.py:518
  63.4 6.6 %copy-start.1 = (f32[3,2048]{1,0:T(4,128)S(1)}, f32[3,2048]{1,0:T(4,128)}, u32[]{:S(2)}) copy-start(f32[3,2048]{1,0:T(4,128)} %mod_ref.5) | copy-start | bytes 73732
  (4 other events, 2.9 us)

commit v4 on v3

--- a/solution.py
+++ b/solution.py
@@ -429,7 +429,10 @@
     other_second_ref,
     *rest,
 ):
-    out_any, block_ref, sems = rest[-3:]
+    if last:
+        ready_ref, out_any, block_ref, sems = rest
+    else:
+        (block_ref,) = rest
     count, piece, _ = own_first_ref.shape
     seq_index = lax.axis_index("seq")
     core = seq_index % 2
@@ -441,6 +444,25 @@
     sides = ((own_first_ref, other_first_ref), (own_second_ref, other_second_ref))
     group = 2
     copies = []
+
+    def place(top, index, upper):
+        first, second = (index >> low & 1, upper) if top == 0 else (upper, index >> low & 1)
+        flip = second + (top << (levels[-1][1] - 1))
+        for j in range(low):
+            flip = flip + ((index >> j & 1) << (levels[2 + j][1] - 1))
+        chip = (lax.axis_index("cfg") ^ first) * seq_chips + (seq_index // 2 ^ flip)
+        return pl.ds(pl.multiple_of(chip * lanes, lanes), lanes)
+
+    def send(source, slot, where, sem):
+        copy = pltpu.make_async_copy(source.at[slot], out_any.at[:, where], sems.at[sem])
+        copy.start()
+        copies.append(copy)
+
+    if last:
+        for top in range(2):
+            for index in range(count):
+                slot = top * count + index
+                send(ready_ref, slot, place(top, index, 0), slot)
     for top, (own_ref, other_ref) in enumerate(sides):
         for start in range(0, count, group):
             blocks = []
@@ -454,20 +476,13 @@
             )
             for i in range(group):
                 index = start + i
-                near = index >> low & 1
-                first, second = (near, last) if top == 0 else (last, near)
-                flip = second + (top << (levels[-1][1] - 1))
-                for j in range(low):
-                    flip = flip + ((index >> j & 1) << (levels[2 + j][1] - 1))
-                chip = (lax.axis_index("cfg") ^ first) * seq_chips + (seq_index // 2 ^ flip)
-                where = pl.ds(pl.multiple_of(chip * lanes, lanes), lanes)
+                where = place(top, index, last)
                 block = pltpu.roll(product[:, i * lanes : (i + 1) * lanes], core * piece, 1)
                 state = dot_rows(tokens, embed_ref[:, where]) + bias_ref[:, where]
                 slot = top * count + index
                 block_ref[slot] = (state + mod_ref[2:3, where] * block).astype(bf16)
-                copy = pltpu.make_async_copy(block_ref.at[slot], out_any.at[:, where], sems.at[slot])
-                copy.start()
-                copies.append(copy)
+                if last:
+                    send(block_ref, slot, where, 2 * count + slot)
     for copy in copies:
         copy.wait()
 
@@ -678,17 +693,21 @@
     count = own_first.shape[0]
     if 2 * piece == 128:
 
+        block_shape = (2 * count, fine_tokens, 128)
+
         def output(last, pieces, *before):
+            if last:
+                out_shape = jax.ShapeDtypeStruct((fine_tokens, width), bf16)
+                scratch = [pltpu.VMEM(block_shape, bf16), pltpu.SemaphoreType.DMA((4 * count,))]
+            else:
+                out_shape = jax.ShapeDtypeStruct(block_shape, bf16)
+                scratch = []
             return pl.pallas_call(
                 functools.partial(output_kernel, tuple(levels), last),
-                out_shape=jax.ShapeDtypeStruct((fine_tokens, width), bf16),
-                in_specs=[whole] * 9 + [free] * len(before),
-                out_specs=free,
-                input_output_aliases={9: 0} if before else {},
-                scratch_shapes=[
-                    pltpu.VMEM((2 * count, fine_tokens, 128), bf16),
-                    pltpu.SemaphoreType.DMA((2 * count,)),
-                ],
+                out_shape=out_shape,
+                in_specs=[whole] * (9 + len(before)),
+                out_specs=free if last else whole,
+                scratch_shapes=scratch,
                 cost_estimate=cost(1e9, 3e6),
                 compiler_params=pltpu.CompilerParams(vmem_limit_bytes=16 << 20),
             )(attended, tokens, embed_weight, bias_row, fine_modulation, *pieces, *before)

time: 73.7 us -> 73.1 us (level)
  transfers between devices with their start and end apart: 20 -> 20, of which waited for: 5 -> 5; matrix products, arithmetic and copies ran while one was open for 0% -> 0% of each run, Pallas kernels for 19% -> 18%
where the time goes in v4:
time: 73.1 us; the launch traced here: 72.9 us
  waiting for transfers between devices  31.7 us (43%)
  starting transfers between devices  20.1 us (27%)
  Pallas kernels  17 us (23%)
  between operations  2.9 us (4%)
  local copies, waits for them, and re-layouts  0.88 us (1%)
    ppermute x19, waiting for transfers between devices, swap(): lax.ppermute(value, ('cfg', 'seq'), [(i, i ^ flip) for i in range(size)])  31.7 us
    ppermute x19, starting transfers between devices, swap(): lax.ppermute(value, ('cfg', 'seq'), [(i, i ^ flip) for i in range(size)])  19.5 us
    pallas_call x1, Pallas kernels, per_device(): pl.pallas_call(functools.partial(attend_kernel, rows, 4 * cells), grid=(i...  6.59 us
    pallas_call x1, Pallas kernels, per_device(): pl.pallas_call(functools.partial(fine_kernel, cells), out_shape=(jax.Shap...  2.93 us
    pallas_call x2, Pallas kernels, output(): pl.pallas_call(functools.partial(output_kernel, tuple(levels), last), out...  2.79 us
    pallas_call x1, Pallas kernels, per_device(): pl.pallas_call(functools.partial(partial_kernel, seq_count), out_shape=(j...  2.29 us
    pallas_call x1, Pallas kernels, per_device(): pl.pallas_call(functools.partial(guide_kernel, rows), out_shape=(jax.Shap...  1.81 us
  transfers between devices with their start and end apart: 20, of which 5 were waited for; matrix products, arithmetic and copies ran while one was open for 0% of the time, Pallas kernels for 18%

profile of v4, /device:TPU:0, one launch (start us, length us, event | category | flops | bytes accessed | tf_op | source)
XLA Modules:
  0.0 72.9 jit_solution(15963187584716807470)
XLA Ops:
  0.7 2.3 %partial_mix.1 = (f32[40,1536]{1,0:T(8,128)}, f32[40,1536]{1,0:T(8,128)}) custom-call(bf16[32,2048]{1,0:T(8,128)(2,1)} %embed_ref.7, f32[1,2048]{1,0:T(1,128)} %bitcast.26, f32[3,2048]{1,0:T(4,128)} %mod_ref.5, bf16[64,3072]{1,0:T(8,128)(2,1)} %weight_ref.1), custom_call_target="tpu_custom_call" | custom-call | flops 2000000000 | bytes 1000000 | tf_op jit(solution)/shard_map/partial_mix/pallas_call | solution.py:539
  3.0 0.5 collective-permute-start.3
  3.5 0.6 copy-done.11
  4.1 0.6 velocity.1
  4.7 2.5 %collective-permute-start = (f32[32,128]{1,0:T(8,128)S(1)}, f32[32,128]{1,0:T(8,128)S(1)}, u32[]{:S(2)}, u32[]{:S(2)}) collective-permute-start(f32[32,128]{1,0:T(8,128)S(1)} %get-tuple-element.15.own_any), channel_id=1, source_target_pairs={{0,16},{1,17},{2,18},{3,19},{4,20},{5,21},{6,22},{7,23},{8,24},{9,... | collective-permute-start | bytes 49160 | tf_op jit(solution)/shard_map/ppermute | solution.py:533
  7.2 1.6 %collective-permute-start.10 = (bf16[1,64,1024]{2,1,0:T(8,128)(2,1)S(1)}, bf16[1,64,1024]{2,1,0:T(8,128)(2,1)S(1)}, u32[]{:S(2)}, u32[]{:S(2)}) collective-permute-start(bf16[1,64,1024]{2,1,0:T(8,128)(2,1)S(1)} %bitcast.40), channel_id=1, source_target_pairs={{0,4},{1,5},{2,6},{3,7},{4,0},{5,1},{6,2},{7,3},{8,12},{9,13},{10,... | collective-permute-start | bytes 393224 | tf_op jit(solution)/shard_map/ppermute | solution.py:533
  10.8 0.6 collective-permute-start.4
  11.4 1.5 %collective-permute-start.5 = (bf16[40,1536]{1,0:T(8,128)(2,1)S(1)}, bf16[40,1536]{1,0:T(8,128)(2,1)S(1)}, u32[]{:S(2)}, u32[]{:S(2)}) collective-permute-start(bf16[40,1536]{1,0:T(8,128)(2,1)S(1)} %get-tuple-element.32), channel_id=1, source_target_pairs={{0,2},{1,3},{2,0},{3,1},{4,6},{5,7},{6,4},{7,5},{8,10},{9,11},{10,... | collective-permute-start | bytes 368648 | tf_op jit(solution)/shard_map/ppermute | solution.py:533
  13.0 1.4 %collective-permute-start.6 = (bf16[40,1536]{1,0:T(8,128)(2,1)S(1)}, bf16[40,1536]{1,0:T(8,128)(2,1)S(1)}, u32[]{:S(2)}, u32[]{:S(2)}) collective-permute-start(bf16[40,1536]{1,0:T(8,128)(2,1)S(1)} %get-tuple-element.32), channel_id=1, source_target_pairs={{0,18},{1,19},{2,16},{3,17},{4,22},{5,23},{6,20},{7,21},{8,26},{9,... | collective-permute-start | bytes 368648 | tf_op jit(solution)/shard_map/ppermute | solution.py:533
  14.4 1.8 %guide.1 = (f32[32,128]{1,0:T(8,128)}, f32[32,128]{1,0:T(8,128)S(1)}) custom-call(f32[32,128]{1,0:T(8,128)S(1)} %bitcast.34, f32[32,128]{1,0:T(8,128)S(1)} %bitcast.35, s32[1]{0:T(128)S(6)} %copy.27.step_any, s32[1]{0:T(128)S(6)} %copy.28.slot_any, f32[32,128]{1,0:T(8,128)S(1)} %get-tuple-element.15.own_any, f32[32,128]{1,0:T(8,128)S(1)} %collective-permute-done.other_any), custom_call_target="tpu_custom_call" | custom-call | flops 1000000000 | bytes 100000 | tf_op jit(solution)/shard_map/guide/pallas_call | solution.py:589
  16.2 0.1 collective-permute-start.1
  16.3 0.7 collective-permute-start.2
  17.0 0.1 collective-permute-done.4
  17.1 4.2 %collective-permute-start.13 = (bf16[2,64,1024]{2,1,0:T(8,128)(2,1)S(1)}, bf16[2,64,1024]{2,1,0:T(8,128)(2,1)S(1)}, u32[]{:S(2)}, u32[]{:S(2)}) collective-permute-start(bf16[2,64,1024]{2,1,0:T(8,128)(2,1)S(1)} %pad_maximum_fusion.1), channel_id=1, source_target_pairs={{0,8},{1,9},{2,10},{3,11},{4,12},{5,13},{6,14},{7,15},{8,0},{9,1},... | collective-permute-start | bytes 786440 | tf_op jit(solution)/shard_map/ppermute | solution.py:533
  21.3 0.5 collective-permute-start.11
  21.9 2.8 %collective-permute-start.7 = (bf16[40,1536]{1,0:T(8,128)(2,1)S(1)}, bf16[40,1536]{1,0:T(8,128)(2,1)S(1)}, u32[]{:S(2)}, u32[]{:S(2)}) collective-permute-start(bf16[40,1536]{1,0:T(8,128)(2,1)S(1)} %get-tuple-element.30), channel_id=1, source_target_pairs={{0,4},{1,5},{2,6},{3,7},{4,0},{5,1},{6,2},{7,3},{8,12},{9,13},{10,... | collective-permute-start | bytes 368648 | tf_op jit(solution)/shard_map/ppermute | solution.py:533
  24.7 5.8 %collective-permute-done.11 = bf16[2,64,1024]{2,1,0:T(8,128)(2,1)S(1)} collective-permute-done((bf16[2,64,1024]{2,1,0:T(8,128)(2,1)S(1)}, bf16[2,64,1024]{2,1,0:T(8,128)(2,1)S(1)}, u32[]{:S(2)}, u32[]{:S(2)}) %collective-permute-start.11) | collective-permute-done | bytes 262176 | tf_op jit(solution)/shard_map/ppermute | solution.py:533
  30.5 0.5 collective-permute-start.12
  31.0 2.5 %collective-permute-done.13 = bf16[2,64,1024]{2,1,0:T(8,128)(2,1)S(1)} collective-permute-done((bf16[2,64,1024]{2,1,0:T(8,128)(2,1)S(1)}, bf16[2,64,1024]{2,1,0:T(8,128)(2,1)S(1)}, u32[]{:S(2)}, u32[]{:S(2)}) %collective-permute-start.13) | collective-permute-done | bytes 262176 | tf_op jit(solution)/shard_map/ppermute | solution.py:533
  33.5 1.6 %collective-permute-start.14 = (bf16[2,64,1024]{2,1,0:T(8,128)(2,1)S(1)}, bf16[2,64,1024]{2,1,0:T(8,128)(2,1)S(1)}, u32[]{:S(2)}, u32[]{:S(2)}) collective-permute-start(bf16[2,64,1024]{2,1,0:T(8,128)(2,1)S(1)} %collective-permute-done.13), channel_id=1, source_target_pairs={{0,2},{1,3},{2,0},{3,1},{4,6},{5,7},{6,4},{7,5},{8,10},{9,11},{10,... | collective-permute-start | bytes 786440 | tf_op jit(solution)/shard_map/ppermute | solution.py:533
  35.1 0.1 collective-permute-start.8
  35.2 14.9 %collective-permute-done.14 = bf16[2,64,1024]{2,1,0:T(8,128)(2,1)S(1)} collective-permute-done((bf16[2,64,1024]{2,1,0:T(8,128)(2,1)S(1)}, bf16[2,64,1024]{2,1,0:T(8,128)(2,1)S(1)}, u32[]{:S(2)}, u32[]{:S(2)}) %collective-permute-start.14) | collective-permute-done | bytes 262176 | tf_op jit(solution)/shard_map/ppermute | solution.py:533
  50.2 0.6 collective-permute-start.15
  51.0 0.1 copy-done
  51.1 2.9 %fine_features.1 = (f32[64,128]{1,0:T(8,128)}, bf16[1024,256]{1,0:T(8,128)(2,1)S(1)}, bf16[256,1024]{1,0:T(8,128)(2,1)S(1)}, bf16[256,256]{1,0:T(8,128)(2,1)S(1)...) custom-call(f32[32,288]{1,0:T(8,128)S(1)} %bitcast.32, f32[8,128]{1,0:T(8,128)S(1)} %get-tuple-element.17.small_ref, ...), custom_call_target="tpu_custom_call" | custom-call | flops 4000000000 | bytes 4000000 | tf_op jit(solution)/shard_map/fine_features/pallas_call | solution.py:617
  54.0 0.5 collective-permute-start.18
  54.5 0.1 collective-permute-start.19
  54.6 0.4 collective-permute-start.16
  55.0 8.4 %collective-permute-done.15.own_second_ref = bf16[4,64,1024]{2,1,0:T(8,128)(2,1)S(1)} collective-permute-done((bf16[4,64,1024]{2,1,0:T(8,128)(2,1)S(1)}, bf16[4,64,1024]{2,1,0:T(8,128)(2,1)S(1)}, u32[]{:S(2)}, u32[]{:S(2)}) %collective-permute-start.15) | collective-permute-done | bytes 524320 | tf_op jit(solution)/shard_map/ppermute | solution.py:533
  63.4 6.6 %attend.1.attended_ref = bf16[256,1024]{1,0:T(8,128)(2,1)S(1)} custom-call(bf16[1024,256]{1,0:T(8,128)(2,1)S(1)} %get-tuple-element.20.keys_ref, bf16[256,1024]{1,0:T(8,128)(2,1)S(1)} %get-tuple-element.21.keys_t_ref, bf16[256,256]{1,0:T(8,128)(2,1)S(1)} %get-tuple-element.22.query_ref, f32[8,128]{1,0:T(8,128)S(1)} %get-tuple-element.17.small_ref, ...), custom_call_target="tpu_custom_call" | custom-call | flops 8000000000 | bytes 4000000 | tf_op jit(solution)/shard_map/attend/pallas_call | solution.py:662
  70.1 1.0 %shard_map.202.rest_0_ = bf16[8,256,128]{2,1,0:T(8,128)(2,1)S(1)} custom-call(bf16[256,1024]{1,0:T(8,128)(2,1)S(1)} %attend.1.attended_ref, bf16[32,256]{1,0:T(8,128)(2,1)S(1)} %get-tuple-element.26.token_ref, bf16[32,2048]{1,0:T(8,128)(2,1)S(1)} %copy-done, f32[1,2048]{1,0:T(1,128)S(1)} %bitcast.28, f32[3,2048]{1,0:T(4,128)S(1)} %copy-done.1, ...), custom_call_target="tpu_custom_call" | custom-call | flops 1000000000 | bytes 3000000 | tf_op jit(solution)/shard_map/pallas_call | solution.py:705
  71.1 1.8 %shard_map.203 = bf16[256,2048]{1,0:T(8,128)(2,1)} custom-call(bf16[256,1024]{1,0:T(8,128)(2,1)S(1)} %attend.1.attended_ref, bf16[32,256]{1,0:T(8,128)(2,1)S(1)} %get-tuple-element.26.token_ref, bf16[32,2048]{1,0:T(8,128)(2,1)S(1)} %copy-done, f32[1,2048]{1,0:T(1,128)S(1)} %bitcast.29, f32[3,2048]{1,0:T(4,128)S(1)} %copy-done.1, ...), custom_call_target="tpu_custom_call" | custom-call | flops 1000000000 | bytes 3000000 | tf_op jit(solution)/shard_map/pallas_call | solution.py:705
  (55 shorter events, 0.5 us)
Async XLA Ops:
  0.6 2.8 %copy-start.3 = (bf16[1,2,64,2048]{3,2,1,0:T(8,128)(2,1)S(1)}, bf16[1,2,64,2048]{3,2,1,0:T(8,128)(2,1)}, u32[]{:S(2)}) copy-start(bf16[1,2,64,2048]{3,2,1,0:T(8,128)(2,1)} %param.19) | copy-start | bytes 1572868
  0.6 2.8 %copy-start.6 = (bf16[2048,32]{0,1:T(8,128)(2,1)S(1)}, bf16[2048,32]{0,1:T(8,128)(2,1)}, u32[]{:S(2)}) copy-start(bf16[2048,32]{0,1:T(8,128)(2,1)} %param.21) | copy-start | bytes 393220
  0.7 2.8 %copy-start.8 = (f32[1,2,2048]{2,1,0:T(2,128)S(1)}, f32[1,2,2048]{2,1,0:T(2,128)}, u32[]{:S(2)}) copy-start(f32[1,2,2048]{2,1,0:T(2,128)} %param.20) | copy-start | bytes 49156
  3.0 7.8 %collective-permute-start.3 = (f32[40,1536]{1,0:T(8,128)}, f32[40,1536]{1,0:T(8,128)S(1)}, u32[]{:S(2)}, u32[]{:S(2)}) collective-permute-start(f32[40,1536]{1,0:T(8,128)} %get-tuple-element.25), channel_id=1, source_target_pairs={{0,1},{1,0},{2,3},{3,2},{4,5},{5,4},{6,7},{7,6},{8,9},{9,8},{10,11... | collective-permute-start | bytes 737288 | tf_op jit(solution)/shard_map/ppermute | solution.py:533
  4.1 3.1 %copy-start.14 = (bf16[1024,64]{0,1:T(8,128)(2,1)S(1)}, bf16[1024,64]{0,1:T(8,128)(2,1)}, u32[]{:S(2)}) copy-start(bf16[1024,64]{0,1:T(8,128)(2,1)} %param.37) | copy-start | bytes 393220
  4.1 6.6 %copy-start.15 = (f32[40,1536]{1,0:T(8,128)S(1)}, f32[40,1536]{1,0:T(8,128)}, u32[]{:S(2)}) copy-start(f32[40,1536]{1,0:T(8,128)} %get-tuple-element.24) | copy-start | bytes 737284
  4.7 9.7 %collective-permute-start = (f32[32,128]{1,0:T(8,128)S(1)}, f32[32,128]{1,0:T(8,128)S(1)}, u32[]{:S(2)}, u32[]{:S(2)}) collective-permute-start(f32[32,128]{1,0:T(8,128)S(1)} %get-tuple-element.15.own_any), channel_id=1, source_target_pairs={{0,16},{1,17},{2,18},{3,19},{4,20},{5,21},{6,22},{7,23},{8,24},{9,... | collective-permute-start | bytes 49160 | tf_op jit(solution)/shard_map/ppermute | solution.py:533
  7.2 9.1 %collective-permute-start.10 = (bf16[1,64,1024]{2,1,0:T(8,128)(2,1)S(1)}, bf16[1,64,1024]{2,1,0:T(8,128)(2,1)S(1)}, u32[]{:S(2)}, u32[]{:S(2)}) collective-permute-start(bf16[1,64,1024]{2,1,0:T(8,128)(2,1)S(1)} %bitcast.40), channel_id=1, source_target_pairs={{0,4},{1,5},{2,6},{3,7},{4,0},{5,1},{6,2},{7,3},{8,12},{9,13},{10,... | collective-permute-start | bytes 393224 | tf_op jit(solution)/shard_map/ppermute | solution.py:533
  10.8 3.6 %copy-start.9 = (f32[4096]{0:T(1024)S(1)}, f32[4096]{0:T(1024)}, u32[]{:S(2)}) copy-start(f32[4096]{0:T(1024)} %param.25) | copy-start | bytes 49156
  10.8 3.6 %copy-start.10 = (f32[2,2048]{1,0:T(2,128)S(1)}, f32[2,2048]{1,0:T(2,128)}, u32[]{:S(2)}) copy-start(f32[2,2048]{1,0:T(2,128)} %param.22) | copy-start | bytes 49156
  10.8 6.3 %collective-permute-start.4 = (bf16[40,1536]{1,0:T(8,128)(2,1)S(1)}, bf16[40,1536]{1,0:T(8,128)(2,1)S(1)}, u32[]{:S(2)}, u32[]{:S(2)}) collective-permute-start(bf16[40,1536]{1,0:T(8,128)(2,1)S(1)} %get-tuple-element.32), channel_id=1, source_target_pairs={{0,16},{1,17},{2,18},{3,19},{4,20},{5,21},{6,22},{7,23},{8,24},{9,... | collective-permute-start | bytes 368648 | tf_op jit(solution)/shard_map/ppermute | solution.py:533
  11.4 9.9 %collective-permute-start.5 = (bf16[40,1536]{1,0:T(8,128)(2,1)S(1)}, bf16[40,1536]{1,0:T(8,128)(2,1)S(1)}, u32[]{:S(2)}, u32[]{:S(2)}) collective-permute-start(bf16[40,1536]{1,0:T(8,128)(2,1)S(1)} %get-tuple-element.32), channel_id=1, source_target_pairs={{0,2},{1,3},{2,0},{3,1},{4,6},{5,7},{6,4},{7,5},{8,10},{9,11},{10,... | collective-permute-start | bytes 368648 | tf_op jit(solution)/shard_map/ppermute | solution.py:533
  13.0 8.9 %collective-permute-start.6 = (bf16[40,1536]{1,0:T(8,128)(2,1)S(1)}, bf16[40,1536]{1,0:T(8,128)(2,1)S(1)}, u32[]{:S(2)}, u32[]{:S(2)}) collective-permute-start(bf16[40,1536]{1,0:T(8,128)(2,1)S(1)} %get-tuple-element.32), channel_id=1, source_target_pairs={{0,18},{1,19},{2,16},{3,17},{4,22},{5,23},{6,20},{7,21},{8,26},{9,... | collective-permute-start | bytes 368648 | tf_op jit(solution)/shard_map/ppermute | solution.py:533
  16.2 34.7 %collective-permute-start.1 = (f32[32,128]{1,0:T(8,128)S(1)}, f32[32,128]{1,0:T(8,128)S(1)}, u32[]{:S(2)}, u32[]{:S(2)}) collective-permute-start(f32[32,128]{1,0:T(8,128)S(1)} %get-tuple-element.18.own_any), channel_id=1, source_target_pairs={{0,1},{1,0},{2,3},{3,2},{4,5},{5,4},{6,7},{7,6},{8,9},{9,8},{10,11... | collective-permute-start | bytes 49160 | tf_op jit(solution)/shard_map/ppermute | solution.py:533
  16.3 34.6 %collective-permute-start.2 = (f32[32,128]{1,0:T(8,128)S(1)}, f32[32,128]{1,0:T(8,128)S(1)}, u32[]{:S(2)}, u32[]{:S(2)}) collective-permute-start(f32[32,128]{1,0:T(8,128)S(1)} %get-tuple-element.18.own_any), channel_id=1, source_target_pairs={{1,2},{3,4},{5,6},{7,8},{9,10},{11,12},{13,14},{2,1},{4,3},{6,5},{... | collective-permute-start | bytes 49160 | tf_op jit(solution)/shard_map/ppermute | solution.py:615
  17.1 16.4 %collective-permute-start.13 = (bf16[2,64,1024]{2,1,0:T(8,128)(2,1)S(1)}, bf16[2,64,1024]{2,1,0:T(8,128)(2,1)S(1)}, u32[]{:S(2)}, u32[]{:S(2)}) collective-permute-start(bf16[2,64,1024]{2,1,0:T(8,128)(2,1)S(1)} %pad_maximum_fusion.1), channel_id=1, source_target_pairs={{0,8},{1,9},{2,10},{3,11},{4,12},{5,13},{6,14},{7,15},{8,0},{9,1},... | collective-permute-start | bytes 786440 | tf_op jit(solution)/shard_map/ppermute | solution.py:533
  21.3 9.2 %collective-permute-start.11 = (bf16[2,64,1024]{2,1,0:T(8,128)(2,1)S(1)}, bf16[2,64,1024]{2,1,0:T(8,128)(2,1)S(1)}, u32[]{:S(2)}, u32[]{:S(2)}) collective-permute-start(bf16[2,64,1024]{2,1,0:T(8,128)(2,1)S(1)} %pad_maximum_fusion.1), channel_id=1, source_target_pairs={{0,16},{1,17},{2,18},{3,19},{4,20},{5,21},{6,22},{7,23},{8,24},{9,... | collective-permute-start | bytes 786440 | tf_op jit(solution)/shard_map/ppermute | solution.py:533
  21.9 13.2 %collective-permute-start.7 = (bf16[40,1536]{1,0:T(8,128)(2,1)S(1)}, bf16[40,1536]{1,0:T(8,128)(2,1)S(1)}, u32[]{:S(2)}, u32[]{:S(2)}) collective-permute-start(bf16[40,1536]{1,0:T(8,128)(2,1)S(1)} %get-tuple-element.30), channel_id=1, source_target_pairs={{0,4},{1,5},{2,6},{3,7},{4,0},{5,1},{6,2},{7,3},{8,12},{9,13},{10,... | collective-permute-start | bytes 368648 | tf_op jit(solution)/shard_map/ppermute | solution.py:533
  30.5 24.1 %collective-permute-start.12 = (bf16[4,64,1024]{2,1,0:T(8,128)(2,1)S(1)}, bf16[4,64,1024]{2,1,0:T(8,128)(2,1)S(1)}, u32[]{:S(2)}, u32[]{:S(2)}) collective-permute-start(bf16[4,64,1024]{2,1,0:T(8,128)(2,1)S(1)} %pad_maximum_fusion.own_first_ref), channel_id=1, source_target_pairs={{0,2},{1,3},{2,0},{3,1},{4,6},{5,7},{6,4},{7,5},{8,10},{9,11},{10,... | collective-permute-start | bytes 1572872 | tf_op jit(solution)/shard_map/ppermute | solution.py:533
  33.5 16.6 %collective-permute-start.14 = (bf16[2,64,1024]{2,1,0:T(8,128)(2,1)S(1)}, bf16[2,64,1024]{2,1,0:T(8,128)(2,1)S(1)}, u32[]{:S(2)}, u32[]{:S(2)}) collective-permute-start(bf16[2,64,1024]{2,1,0:T(8,128)(2,1)S(1)} %collective-permute-done.13), channel_id=1, source_target_pairs={{0,2},{1,3},{2,0},{3,1},{4,6},{5,7},{6,4},{7,5},{8,10},{9,11},{10,... | collective-permute-start | bytes 786440 | tf_op jit(solution)/shard_map/ppermute | solution.py:533
  35.1 15.7 %collective-permute-start.8 = (bf16[40,1536]{1,0:T(8,128)(2,1)S(1)}, bf16[40,1536]{1,0:T(8,128)(2,1)S(1)}, u32[]{:S(2)}, u32[]{:S(2)}) collective-permute-start(bf16[40,1536]{1,0:T(8,128)(2,1)S(1)} %fusion), channel_id=1, source_target_pairs={{0,8},{1,9},{2,10},{3,11},{4,12},{5,13},{6,14},{7,15},{8,0},{9,1},... | collective-permute-start | bytes 368648 | tf_op jit(solution)/shard_map/ppermute | solution.py:533
  35.2 15.7 %copy-start.4 = (bf16[256,1024]{1,0:T(8,128)(2,1)S(1)}, bf16[256,1024]{1,0:T(8,128)(2,1)}, u32[]{:S(2)}) copy-start(bf16[256,1024]{1,0:T(8,128)(2,1)} %text_ref.1) | copy-start | bytes 1572868
  50.2 0.9 %copy-start = (bf16[32,2048]{1,0:T(8,128)(2,1)S(1)}, bf16[32,2048]{1,0:T(8,128)(2,1)}, u32[]{:S(2)}) copy-start(bf16[32,2048]{1,0:T(8,128)(2,1)} %embed_ref.7) | copy-start | bytes 393220
  50.2 0.9 %copy-start.2 = (f32[2048]{0:T(1024)S(1)}, f32[2048]{0:T(1024)}, u32[]{:S(2)}) copy-start(f32[2048]{0:T(1024)} %param.29) | copy-start | bytes 24580
  50.2 13.2 %collective-permute-start.15 = (bf16[4,64,1024]{2,1,0:T(8,128)(2,1)S(1)}, bf16[4,64,1024]{2,1,0:T(8,128)(2,1)S(1)}, u32[]{:S(2)}, u32[]{:S(2)}) collective-permute-start(bf16[4,64,1024]{2,1,0:T(8,128)(2,1)S(1)} %constant_dynamic-update-slice_fusion.own_second_ref), channel_id=1, source_target_pairs={{0,16},{1,17},{2,18},{3,19},{4,20},{5,21},{6,22},{7,23},{8,24},{9,... | collective-permute-start | bytes 1572872 | tf_op jit(solution)/shard_map/ppermute | solution.py:533
  50.9 12.5 %collective-permute-start.9 = (f32[40,1536]{1,0:T(8,128)S(1)}, f32[40,1536]{1,0:T(8,128)S(1)}, u32[]{:S(2)}, u32[]{:S(2)}) collective-permute-start(f32[40,1536]{1,0:T(8,128)S(1)} %convert_add_fusion.kept_any), channel_id=1, source_target_pairs={{0,1},{1,0},{2,3},{3,2},{4,5},{5,4},{6,7},{7,6},{8,9},{9,8},{10,11... | collective-permute-start | bytes 737288 | tf_op jit(solution)/shard_map/ppermute | solution.py:533
  51.1 12.3 %copy-start.5 = (bf16[256,1024]{1,0:T(8,128)(2,1)S(1)}, bf16[256,1024]{1,0:T(8,128)(2,1)}, u32[]{:S(2)}) copy-start(bf16[256,1024]{1,0:T(8,128)(2,1)} %text_values_ref.1) | copy-start | bytes 1572868
  54.0 16.0 %collective-permute-start.18 = (bf16[4,64,1024]{2,1,0:T(8,128)(2,1)S(1)}, bf16[4,64,1024]{2,1,0:T(8,128)(2,1)S(1)}, u32[]{:S(2)}, u32[]{:S(2)}) collective-permute-start(bf16[4,64,1024]{2,1,0:T(8,128)(2,1)S(1)} %pad_maximum_fusion.own_first_ref), channel_id=1, source_target_pairs={{0,1},{1,0},{2,3},{3,2},{4,5},{5,4},{6,7},{7,6},{8,9},{9,8},{10,11... | collective-permute-start | bytes 1572872 | tf_op jit(solution)/shard_map/ppermute | solution.py:533
  54.5 15.5 %collective-permute-start.19 = (bf16[4,64,1024]{2,1,0:T(8,128)(2,1)S(1)}, bf16[4,64,1024]{2,1,0:T(8,128)(2,1)S(1)}, u32[]{:S(2)}, u32[]{:S(2)}) collective-permute-start(bf16[4,64,1024]{2,1,0:T(8,128)(2,1)S(1)} %constant_dynamic-update-slice_fusion.own_second_ref), channel_id=1, source_target_pairs={{0,1},{1,0},{2,3},{3,2},{4,5},{5,4},{6,7},{7,6},{8,9},{9,8},{10,11... | collective-permute-start | bytes 1572872 | tf_op jit(solution)/shard_map/ppermute | solution.py:533
  54.6 16.4 %collective-permute-start.16 = (bf16[4,64,1024]{2,1,0:T(8,128)(2,1)S(1)}, bf16[4,64,1024]{2,1,0:T(8,128)(2,1)S(1)}, u32[]{:S(2)}, u32[]{:S(2)}) collective-permute-start(bf16[4,64,1024]{2,1,0:T(8,128)(2,1)S(1)} %collective-permute-done.12.own_first_ref), channel_id=1, source_target_pairs={{0,1},{1,0},{2,3},{3,2},{4,5},{5,4},{6,7},{7,6},{8,9},{9,8},{10,11... | collective-permute-start | bytes 1572872 | tf_op jit(solution)/shard_map/ppermute | solution.py:533
  63.4 7.7 %collective-permute-start.17 = (bf16[4,64,1024]{2,1,0:T(8,128)(2,1)S(1)}, bf16[4,64,1024]{2,1,0:T(8,128)(2,1)S(1)}, u32[]{:S(2)}, u32[]{:S(2)}) collective-permute-start(bf16[4,64,1024]{2,1,0:T(8,128)(2,1)S(1)} %collective-permute-done.15.own_second_ref), channel_id=1, source_target_pairs={{0,1},{1,0},{2,3},{3,2},{4,5},{5,4},{6,7},{7,6},{8,9},{9,8},{10,11... | collective-permute-start | bytes 1572872 | tf_op jit(solution)/shard_map/ppermute | solution.py:533
  63.4 6.6 %copy-start.1 = (f32[3,2048]{1,0:T(4,128)S(1)}, f32[3,2048]{1,0:T(4,128)}, u32[]{:S(2)}) copy-start(f32[3,2048]{1,0:T(4,128)} %mod_ref.5) | copy-start | bytes 73732
  (4 other events, 2.9 us)
